TPU v7x, 32 devices: a whole 2x2x4 slice. The times are simulated.
32 devices in a mesh: gx: 8 (over z, x), gy: 4 (over y, core).
Axes of the slice: x: 2, y: 2, z: 4, core: 2. Of those that a mesh axis runs over, the one named last changes fastest.
Arguments:
- state: float32 [12, 4, 256, 1024], P(None, None, 'gy', 'gx'), may hold values from -240 to 240, as said below
- inverse: float32 [128, 256, 256], P('gy'), may hold values from -0.6 to 1.8, as said below
Outputs:
- updated: float32 [12, 4, 256, 1024], P(None, None, 'gy', 'gx')
- wall_stress: float32 [12, 2, 2, 1024], P(None, None, None, 'gx')
Inputs may be any that keep to these rules, and one draw needn't show every extreme that they name: `state`: perturbation coefficients, of varying size over coefficients and x. Each inverse is a dense matrix with a positive diagonal.
All inputs are finite; a program needn't handle non-finite values.
Results may differ from a plain program's by a relative error of at most 0.0003.
Values sent between devices are 32-bit elements; how exact they have to be, the bound alone decides.
No kernel may reach another device: no remote copies, remote signals or barrier semaphores. Data moves between devices by JAX's collectives and lax.ppermute only.
A program may use at most 64 MiB of HBM per device.

v0:
```python
import functools

import jax
import jax.numpy as jnp
import numpy as np
from jax import lax
from jax.experimental import pallas as pl
from jax.experimental.pallas import tpu as pltpu
from jax.sharding import PartitionSpec as P

MODES = 128
HALO = 64

EPSILON = 1e-06
TIME_STEP = 0.5
MEAN_FLOW = 0.8
CORIOLIS = 0.6
STRATIFICATION = 0.9

LANES = 128
GROUP = 4
NT = (((1,), (1,)), ((), ()))


def window_tables(window, rim_width, points, mode_count):
    position = np.arange(window)
    mode_index = np.arange(mode_count)
    half_count = mode_count // 2
    is_cosine = mode_index <= half_count
    wave_index = np.where(is_cosine, mode_index, mode_index - half_count)
    product_index = position[:, None] * wave_index[None, :] % window
    phases = 2.0 * np.pi * product_index / window
    weights_norm = np.where(wave_index == 0, np.sqrt(1.0 / window), np.sqrt(2.0 / window))
    basis = np.where(is_cosine[None, :], np.cos(phases), np.sin(phases)) * weights_norm[None, :]
    wavenumber = 2.0 * np.pi * wave_index / window
    paired = wave_index[:, None] == wave_index[None, :]
    to_sine = is_cosine[:, None] & ~is_cosine[None, :] & paired
    to_cosine = ~is_cosine[:, None] & is_cosine[None, :] & paired
    derivative = np.where(to_sine, -wavenumber[:, None], 0.0) + np.where(
        to_cosine, wavenumber[:, None], 0.0
    )
    taper = 0.25 + 0.75 * np.sin(np.pi * (position + 0.5) / window) ** 2
    values = basis * taper[:, None]
    slopes = (basis @ derivative) * taper[:, None]
    back_table = (
        basis[rim_width : rim_width + points, :] / taper[rim_width : rim_width + points, None]
    ).T
    return values, slopes, back_table


def step_tables(values, slopes, rim, points):
    direct = values - TIME_STEP * MEAN_FLOW * slopes
    couplings = (
        (TIME_STEP * CORIOLIS, -TIME_STEP * CORIOLIS),
        (TIME_STEP, -TIME_STEP * STRATIFICATION),
    )
    tables = []
    for to_first, to_second in couplings:
        first = (direct, to_first * values)
        second = (to_second * values, direct)
        rows = []
        for part in (first, second):
            pieces = []
            for begin, end in ((rim, rim + points), (0, rim), (rim + points, points + 2 * rim)):
                pieces += [part[0][begin:end].T, part[1][begin:end].T]
            rows.append(np.concatenate(pieces, axis=1))
        tables.append(np.concatenate(rows, axis=0))
    return np.stack(tables)


def split_table(table):
    table = np.asarray(table, np.float32)
    high = table.astype(jnp.bfloat16)
    low = (table - high.astype(np.float32)).astype(jnp.bfloat16)
    return jnp.asarray(high), jnp.asarray(low)


def split(x):
    high = x.astype(jnp.bfloat16)
    low = (x - high.astype(jnp.float32)).astype(jnp.bfloat16)
    return high, low


def dot(a, b, dims):
    return lax.dot_general(a, b, dims, preferred_element_type=jnp.float32)


def left_lanes(shape):
    return lax.broadcasted_iota(jnp.int32, shape, len(shape) - 1) < LANES // 2


def swap(x):
    return pltpu.roll(x, LANES // 2, len(x.shape) - 1)


def pack_kernel(state_ref, last_ref, first_ref, sums_ref):
    rows = state_ref.shape[2]
    left = left_lanes((rows, LANES))
    totals = []
    for e in range(GROUP):
        acc = jnp.zeros((rows, LANES), jnp.float32)
        for p in range(2):
            a = state_ref[e, p]
            b = state_ref[e, p + 2]
            acc += a * a + b * b
            last_ref[e, p] = jnp.where(left, swap(a), b)
            first_ref[e, p] = jnp.where(left, a, swap(b))
        totals.append(jnp.sum(acc))
    half = left_lanes((4, LANES))
    for q in range(GROUP // 2):
        sums_ref[4 * q : 4 * q + 4] = jnp.where(half, totals[2 * q], totals[2 * q + 1])


def project_kernel(state_ref, before_ref, after_ref, high_ref, low_ref, mask_ref, sums_ref, out_ref):
    parts, slots, rows, _ = out_ref.shape
    coef = state_ref.shape[2]
    count = (slots - 1) * parts
    flat = out_ref.reshape(parts * slots * rows, LANES)
    mask = mask_ref[...]
    for p in range(2):
        x = jnp.concatenate(
            [
                state_ref[:, p].reshape(GROUP * coef, LANES),
                state_ref[:, p + 2].reshape(GROUP * coef, LANES),
                before_ref[:, p].reshape(GROUP * coef, LANES),
                after_ref[:, p].reshape(GROUP * coef, LANES),
            ],
            axis=1,
        )
        x_high, x_low = split(x)
        w_high = high_ref[p]
        w_low = low_ref[p]
        t = dot(w_high, x_high, NT) + (dot(w_high, x_low, NT) + dot(w_low, x_high, NT))
        t = t * mask
        for f in range(2):
            for q in range(GROUP // 2):
                row = 4 * q + p + 2 * f
                for k in range(parts):
                    first = f * count + k * (slots - 1)
                    flat[pl.ds(k * slots * rows + row, slots - 1, stride=rows), :] = t[
                        first : first + slots - 1, q * LANES : (q + 1) * LANES
                    ]
    for k in range(parts):
        out_ref[k, slots - 1] = sums_ref[...]


def solve_kernel(total, recv_ref, inverse_ref, wall_ref, out_ref, scale_ref, wall_sums):
    step = pl.program_id(0)
    parts, slots, rows, _ = recv_ref.shape
    per_step = inverse_ref.shape[0]
    left = left_lanes((rows, LANES))

    @pl.when(step == 0)
    def _():
        n = recv_ref[0, slots - 1]
        for s in range(1, parts):
            n = n + recv_ref[s, slots - 1]
        scale_ref[...] = lax.rsqrt(n / total + EPSILON)
        wall_sums[...] = jnp.zeros_like(wall_sums)

    scale = scale_ref[...]
    lane = lax.broadcasted_iota(jnp.int32, (rows, LANES), 1)
    sums = wall_sums[...]
    for i in range(per_step):
        m = step * per_step + i
        t = [recv_ref[s, m] * scale for s in range(parts)]
        even, odd = [], []
        for s in range(0, parts, 2):
            even.append(jnp.where(left, t[s], swap(t[s + 1])))
            odd.append(jnp.where(left, swap(t[s]), t[s + 1]))
        r = jnp.concatenate(
            [jnp.concatenate(even, axis=1), jnp.concatenate(odd, axis=1)], axis=0
        )
        r_high, r_low = split(r)
        v_high, v_low = split(inverse_ref[i])
        both = dot(jnp.concatenate([r_high, r_low], axis=0), v_high, NT)
        o = both[: 2 * rows] + (both[2 * rows :] + dot(r_high, v_low, NT))
        for s in range(0, parts, 2):
            a = o[:rows, s * 64 : s * 64 + LANES]
            b = o[rows:, s * 64 : s * 64 + LANES]
            out_ref[s, m] = jnp.where(left, a, swap(b))
            out_ref[s + 1, m] = jnp.where(left, swap(a), b)
        for w in range(2):
            q = jnp.sum(o * wall_ref[w : w + 1, :], axis=1, keepdims=True)
            for e in range(2):
                at = e * 2 * (slots - 1) + w * (slots - 1) + m
                sums = jnp.where(lane == at, q[e * rows : (e + 1) * rows], sums)
    wall_sums[...] = sums

    @pl.when(step == pl.num_programs(0) - 1)
    def _():
        for k in range(parts):
            out_ref[k, slots - 1] = wall_sums[...]


def back_kernel(recv_ref, high_ref, low_ref, out_ref, wall_ref):
    parts, slots, rows, _ = recv_ref.shape
    coef = out_ref.shape[2]
    width = slots - 1
    flat = recv_ref.reshape(parts * slots * rows, LANES)
    b_high = high_ref[...]
    b_low = low_ref[...]
    for r in range(rows):
        q, f = r // 4, r % 4
        s = jnp.concatenate(
            [flat[pl.ds(k * slots * rows + r, width, stride=rows), :] for k in range(parts)],
            axis=0,
        )
        s = s.T
        s_high, s_low = split(s)
        dims = (((1,), (0,)), ((), ()))
        o = dot(s_high, b_high, dims) + (dot(s_high, b_low, dims) + dot(s_low, b_high, dims))
        for e in range(2):
            out_ref[2 * q + e, f] = o[e * coef : (e + 1) * coef]
    lane = lax.broadcasted_iota(jnp.int32, (rows, LANES), 1)
    for e in range(2):
        for w in range(2):
            g = jnp.zeros((rows, LANES), jnp.float32)
            for k in range(parts):
                tile = recv_ref[k, slots - 1]
                shift = (k * width - (e * 2 + w) * width) % LANES
                tile = pltpu.roll(tile, shift, 1) if shift else tile
                g = jnp.where((lane >= k * width) & (lane < (k + 1) * width), tile, g)
            g_high, g_low = split(g)
            dims = (((1,), (0,)), ((), ()))
            o = dot(g_high, b_high, dims) + (dot(g_high, b_low, dims) + dot(g_low, b_high, dims))
            for q in range(GROUP // 2):
                for c in range(2):
                    row = 4 * q + 2 * c
                    wall_ref[2 * q + e, w, c : c + 1] = o[row : row + 1]


def shifted(x, axis, by):
    n = lax.axis_size(axis)
    return lax.ppermute(x, axis, [(i, (i + by) % n) for i in range(n)])


def ring_sum(x, axis):
    n = lax.axis_size(axis)
    if n & (n - 1):
        return lax.psum(x, axis)
    hop = 1
    while hop < n:
        x = x + shifted(x, axis, hop)
        hop *= 2
    return x


def whole(shape):
    return pl.BlockSpec(shape, lambda *_: (0,) * len(shape))


def per_device(state, inverse):
    members, fields, coef, points = state.shape
    parts = lax.axis_size("gy")
    coef_count = coef * parts
    grid_x = points * lax.axis_size("gx")
    window = points + 2 * HALO
    mine = MODES // parts
    rows = members * fields * coef // LANES
    group_rows = GROUP * fields * coef // LANES
    groups = members // GROUP
    slots = mine + 1

    values, slopes, back_table = window_tables(window, HALO, points, MODES)
    step_high, step_low = split_table(step_tables(values, slopes, HALO, points))
    back_high, back_low = split_table(back_table)
    k = np.arange(coef_count)
    curvature = k * k / (coef_count * coef_count)
    wall = np.zeros((8, coef_count), np.float32)
    wall[0] = curvature
    wall[1] = np.where(k % 2 == 0, -1.0, 1.0) * curvature
    wall = jnp.asarray(wall)

    last, first, sums = pl.pallas_call(
        pack_kernel,
        grid=(groups,),
        in_specs=[pl.BlockSpec((GROUP, fields, coef, points), lambda g: (g, 0, 0, 0))],
        out_specs=[
            pl.BlockSpec((GROUP, 2, coef, LANES), lambda g: (g, 0, 0, 0)),
            pl.BlockSpec((GROUP, 2, coef, LANES), lambda g: (g, 0, 0, 0)),
            pl.BlockSpec((group_rows, LANES), lambda g: (g, 0)),
        ],
        out_shape=[
            jax.ShapeDtypeStruct((members, 2, coef, LANES), jnp.float32),
            jax.ShapeDtypeStruct((members, 2, coef, LANES), jnp.float32),
            jax.ShapeDtypeStruct((rows, LANES), jnp.float32),
        ],
        name="pack",
    )(state)
    before = shifted(last, "gx", 1)
    after = shifted(first, "gx", -1)
    sums = ring_sum(sums, "gx")

    coef_global = lax.axis_index("gy") * coef + jnp.arange(coef, dtype=jnp.int32)
    keep = (coef_global < coef_count - 2).astype(jnp.float32)
    mask = jnp.tile(keep, GROUP)[None, :]

    sent = pl.pallas_call(
        project_kernel,
        grid=(groups,),
        in_specs=[
            pl.BlockSpec((GROUP, fields, coef, points), lambda g: (g, 0, 0, 0)),
            pl.BlockSpec((GROUP, 2, coef, LANES), lambda g: (g, 0, 0, 0)),
            pl.BlockSpec((GROUP, 2, coef, LANES), lambda g: (g, 0, 0, 0)),
            whole(step_high.shape),
            whole(step_low.shape),
            whole(mask.shape),
            pl.BlockSpec((group_rows, LANES), lambda g: (g, 0)),
        ],
        out_specs=pl.BlockSpec((parts, slots, group_rows, LANES), lambda g: (0, 0, g, 0)),
        out_shape=jax.ShapeDtypeStruct((parts, slots, rows, LANES), jnp.float32),
        name="project",
    )(state, before, after, step_high, step_low, mask, sums)
    got = lax.all_to_all(sent, "gy", split_axis=0, concat_axis=0, tiled=True)

    per_step = 4
    solved = pl.pallas_call(
        functools.partial(solve_kernel, float(fields * coef_count * grid_x)),
        grid=(mine // per_step,),
        in_specs=[
            whole(got.shape),
            pl.BlockSpec((per_step, coef_count, coef_count), lambda i: (i, 0, 0)),
            whole(wall.shape),
        ],
        out_specs=whole(got.shape),
        out_shape=jax.ShapeDtypeStruct(got.shape, jnp.float32),
        scratch_shapes=[
            pltpu.VMEM((rows, LANES), jnp.float32),
            pltpu.VMEM((rows, LANES), jnp.float32),
        ],
        name="solve",
    )(got, inverse, wall)
    returned = lax.all_to_all(solved, "gy", split_axis=0, concat_axis=0, tiled=True)

    return pl.pallas_call(
        back_kernel,
        grid=(groups,),
        in_specs=[
            pl.BlockSpec((parts, slots, group_rows, LANES), lambda g: (0, 0, g, 0)),
            whole(back_high.shape),
            whole(back_low.shape),
        ],
        out_specs=[
            pl.BlockSpec((GROUP, fields, coef, points), lambda g: (g, 0, 0, 0)),
            pl.BlockSpec((GROUP, 2, 2, points), lambda g: (g, 0, 0, 0)),
        ],
        out_shape=[
            jax.ShapeDtypeStruct((members, fields, coef, points), jnp.float32),
            jax.ShapeDtypeStruct((members, 2, 2, points), jnp.float32),
        ],
        name="back",
    )(returned, back_high, back_low)


def solution(mesh):
    placed = (P(None, None, "gy", "gx"), P("gy", None, None))
    return jax.shard_map(
        per_device,
        mesh=mesh,
        in_specs=placed,
        out_specs=(P(None, None, "gy", "gx"), P(None, None, None, "gx")),
        check_vma=False,
    )
```

profile of v0, /device:TPU:0, one launch (start us, length us, event | category | flops | bytes accessed | tf_op | source)
XLA Modules:
  0.0 123.8 jit_solution(3148788815921744590)
XLA Ops:
  0.6 3.8 %pack.1 = (f32[12,2,64,128]{3,2,1,0:T(8,128)}, f32[12,2,64,128]{3,2,1,0:T(8,128)}, f32[24,128]{1,0:T(8,128)}) custom-call(f32[12,4,64,128]{3,2,1,0:T(8,128)} %state_ref.3), custom_call_target="tpu_custom_call" | custom-call | tf_op jit(solution)/shard_map/pack/pallas_call | solution.py:275
  4.4 3.0 %collective-permute-start = (f32[12,2,64,128]{3,2,1,0:T(8,128)}, f32[12,2,64,128]{3,2,1,0:T(8,128)S(1)}, u32[]{:S(2)}, u32[]{:S(2)}) collective-permute-start(f32[12,2,64,128]{3,2,1,0:T(8,128)} %get-tuple-element.5), channel_id=1, source_target_pairs={{0,4},{4,8},{8,12},{12,16},{16,20},{20,24},{24,28},{28,0},{1,5},{5... | collective-permute-start | bytes 2359304 | tf_op jit(solution)/shard_map/ppermute | solution.py:235
  7.4 3.1 %collective-permute-start.1 = (f32[12,2,64,128]{3,2,1,0:T(8,128)}, f32[12,2,64,128]{3,2,1,0:T(8,128)S(1)}, u32[]{:S(2)}, u32[]{:S(2)}) collective-permute-start(f32[12,2,64,128]{3,2,1,0:T(8,128)} %get-tuple-element.6), channel_id=1, source_target_pairs={{0,28},{4,0},{8,4},{12,8},{16,12},{20,16},{24,20},{28,24},{1,29},{... | collective-permute-start | bytes 2359304 | tf_op jit(solution)/shard_map/ppermute | solution.py:235
  10.5 0.0 collective-permute-start.2
  10.5 31.0 %collective-permute-done.2 = f32[24,128]{1,0:T(8,128)S(1)} collective-permute-done((f32[24,128]{1,0:T(8,128)}, f32[24,128]{1,0:T(8,128)S(1)}, u32[]{:S(2)}, u32[]{:S(2)}) %collective-permute-start.2) | collective-permute-done | bytes 12320 | tf_op jit(solution)/shard_map/ppermute | solution.py:235
  41.5 0.7 add.21
  42.2 1.6 %collective-permute-start.3 = (f32[24,128]{1,0:T(8,128)S(1)}, f32[24,128]{1,0:T(8,128)S(1)}, u32[]{:S(2)}, u32[]{:S(2)}) collective-permute-start(f32[24,128]{1,0:T(8,128)S(1)} %add.21), channel_id=1, source_target_pairs={{0,8},{4,12},{8,16},{12,20},{16,24},{20,28},{24,0},{28,4},{1,9},{5... | collective-permute-start | bytes 36872 | tf_op jit(solution)/shard_map/ppermute | solution.py:235
  43.8 3.9 %collective-permute-done.3 = f32[24,128]{1,0:T(8,128)S(1)} collective-permute-done((f32[24,128]{1,0:T(8,128)S(1)}, f32[24,128]{1,0:T(8,128)S(1)}, u32[]{:S(2)}, u32[]{:S(2)}) %collective-permute-start.3) | collective-permute-done | bytes 12320 | tf_op jit(solution)/shard_map/ppermute | solution.py:235
  47.7 0.8 collective-permute-start.4
  48.5 0.6 broadcast_in_dim_tile.3.mask_ref
  49.1 3.2 %collective-permute-done.4 = f32[24,128]{1,0:T(8,128)S(1)} collective-permute-done((f32[24,128]{1,0:T(8,128)S(1)}, f32[24,128]{1,0:T(8,128)S(1)}, u32[]{:S(2)}, u32[]{:S(2)}) %collective-permute-start.4) | collective-permute-done | bytes 12320 | tf_op jit(solution)/shard_map/ppermute | solution.py:235
  52.3 0.6 add.23.sums_ref
  52.9 0.0 collective-permute-done.before_ref
  52.9 0.0 copy-start
  52.9 0.0 collective-permute-done.1.after_ref
  52.9 0.9 copy-done
  53.8 0.0 copy-start.1
  53.8 0.9 copy-done.1
  54.7 5.1 %project.1 = f32[4,33,24,128]{3,2,1,0:T(8,128)} custom-call(f32[12,4,64,128]{3,2,1,0:T(8,128)} %state_ref.3, f32[12,2,64,128]{3,2,1,0:T(8,128)} %copy-done, f32[12,2,64,128]{3,2,1,0:T(8,128)} %copy-done.1, bf16[2,256,512]{2,1,0:T(8,128)(2,1)} %constant.18.clone.high_ref, bf16[2,256,512]{2,1,0:T(8,128)(2,1)} %constant.19.clone.low_ref, ...), custom_call_target="tpu_custom_call" | custom-call | tf_op jit(solution)/shard_map/project/pallas_call | solution.py:299
  59.8 25.0 %all_to_all.10.recv_ref = f32[4,33,24,128]{3,2,1,0:T(8,128)} all-to-all(f32[4,33,24,128]{3,2,1,0:T(8,128)} %project.1), channel_id=1, replica_groups=mesh['gx'=8,'gy'=4] {'gy'}, dimensions={0} | all-to-all | bytes 3244032 | tf_op jit(solution)/shard_map/all_to_all | solution.py:315
  84.8 10.1 %solve.1 = f32[4,33,24,128]{3,2,1,0:T(8,128)} custom-call(f32[4,33,24,128]{3,2,1,0:T(8,128)} %all_to_all.10.recv_ref, f32[32,256,256]{2,1,0:T(8,128)} %inverse_ref.1, f32[8,256]{1,0:T(8,128)} %constant.22.clone.wall_ref), custom_call_target="tpu_custom_call" | custom-call | tf_op jit(solution)/shard_map/solve/pallas_call | solution.py:318
  94.8 25.0 %all_to_all.11.recv_ref = f32[4,33,24,128]{3,2,1,0:T(8,128)} all-to-all(f32[4,33,24,128]{3,2,1,0:T(8,128)} %solve.1), channel_id=1, replica_groups=mesh['gx'=8,'gy'=4] {'gy'}, dimensions={0} | all-to-all | bytes 3244032 | tf_op jit(solution)/shard_map/all_to_all | solution.py:334
  119.8 4.0 %back.1 = (f32[12,4,64,128]{3,2,1,0:T(8,128)}, f32[12,2,2,128]{3,2,1,0:T(2,128)}) custom-call(f32[4,33,24,128]{3,2,1,0:T(8,128)} %all_to_all.11.recv_ref, bf16[128,128]{1,0:T(8,128)(2,1)} %constant.20.clone.high_ref, bf16[128,128]{1,0:T(8,128)(2,1)} %constant.21.clone.low_ref), custom_call_target="tpu_custom_call" | custom-call | tf_op jit(solution)/shard_map/back/pallas_call | solution.py:336
  (3 shorter events, 0.0 us)
Async XLA Ops:
  4.4 48.5 %collective-permute-start = (f32[12,2,64,128]{3,2,1,0:T(8,128)}, f32[12,2,64,128]{3,2,1,0:T(8,128)S(1)}, u32[]{:S(2)}, u32[]{:S(2)}) collective-permute-start(f32[12,2,64,128]{3,2,1,0:T(8,128)} %get-tuple-element.5), channel_id=1, source_target_pairs={{0,4},{4,8},{8,12},{12,16},{16,20},{20,24},{24,28},{28,0},{1,5},{5... | collective-permute-start | bytes 2359304 | tf_op jit(solution)/shard_map/ppermute | solution.py:235
  7.4 45.5 %collective-permute-start.1 = (f32[12,2,64,128]{3,2,1,0:T(8,128)}, f32[12,2,64,128]{3,2,1,0:T(8,128)S(1)}, u32[]{:S(2)}, u32[]{:S(2)}) collective-permute-start(f32[12,2,64,128]{3,2,1,0:T(8,128)} %get-tuple-element.6), channel_id=1, source_target_pairs={{0,28},{4,0},{8,4},{12,8},{16,12},{20,16},{24,20},{28,24},{1,29},{... | collective-permute-start | bytes 2359304 | tf_op jit(solution)/shard_map/ppermute | solution.py:235
  10.5 31.0 %collective-permute-start.2 = (f32[24,128]{1,0:T(8,128)}, f32[24,128]{1,0:T(8,128)S(1)}, u32[]{:S(2)}, u32[]{:S(2)}) collective-permute-start(f32[24,128]{1,0:T(8,128)} %get-tuple-element.7), channel_id=1, source_target_pairs={{0,4},{4,8},{8,12},{12,16},{16,20},{20,24},{24,28},{28,0},{1,5},{5... | collective-permute-start | bytes 36872 | tf_op jit(solution)/shard_map/ppermute | solution.py:235
  42.2 5.5 %collective-permute-start.3 = (f32[24,128]{1,0:T(8,128)S(1)}, f32[24,128]{1,0:T(8,128)S(1)}, u32[]{:S(2)}, u32[]{:S(2)}) collective-permute-start(f32[24,128]{1,0:T(8,128)S(1)} %add.21), channel_id=1, source_target_pairs={{0,8},{4,12},{8,16},{12,20},{16,24},{20,28},{24,0},{28,4},{1,9},{5... | collective-permute-start | bytes 36872 | tf_op jit(solution)/shard_map/ppermute | solution.py:235
  47.7 4.6 %collective-permute-start.4 = (f32[24,128]{1,0:T(8,128)S(1)}, f32[24,128]{1,0:T(8,128)S(1)}, u32[]{:S(2)}, u32[]{:S(2)}) collective-permute-start(f32[24,128]{1,0:T(8,128)S(1)} %add.22), channel_id=1, source_target_pairs={{0,16},{4,20},{8,24},{12,28},{16,0},{20,4},{24,8},{28,12},{1,17},{... | collective-permute-start | bytes 36872 | tf_op jit(solution)/shard_map/ppermute | solution.py:235
  52.9 0.9 copy-start
  53.8 0.9 copy-start.1
where the time goes:
time: 124 us
  blocking collectives  50 us (40%)
  waiting for transfers between devices  38.1 us (31%)
  Pallas kernels  22.9 us (18%)
  starting transfers between devices  8.43 us (7%)
  local copies, waits for them, and re-layouts  2.37 us (2%)
  other arithmetic  1.32 us (1%)
    ppermute x5, waiting for transfers between devices, shifted(): return lax.ppermute(x, axis, [(i, (i + by) % n) for i in range(n)])  38.1 us
    all_to_all x1, blocking collectives, per_device(): got = lax.all_to_all(sent, 'gy', split_axis=0, concat_axis=0, tiled=True)  25 us
    all_to_all x1, blocking collectives, per_device(): lax.all_to_all(solved, 'gy', split_axis=0, concat_axis=0, tiled=True)  25 us
    pallas_call x1, Pallas kernels, per_device(): pl.pallas_call(functools.partial(solve_kernel, float(fields * coef_count...  10.1 us
    ppermute x5, starting transfers between devices, shifted(): return lax.ppermute(x, axis, [(i, (i + by) % n) for i in range(n)])  8.43 us
    pallas_call x1, Pallas kernels, per_device(): pl.pallas_call(project_kernel, grid=(groups,), in_specs=[pl.BlockSpec((GR...  5.12 us
    pallas_call x1, Pallas kernels, per_device(): pl.pallas_call(back_kernel, grid=(groups,), in_specs=[pl.BlockSpec((parts...  3.99 us
    pallas_call x1, Pallas kernels, per_device(): pl.pallas_call(pack_kernel, grid=(groups,), in_specs=[pl.BlockSpec((GROUP...  3.77 us
  transfers between devices with their start and end apart: 5, of which 3 were waited for; matrix products, arithmetic and copies ran while one was open for 2% of the time, Pallas kernels for 0%

commit v1 on v0

v1 whole, which is shorter than its diff:
```python
import functools

import jax
import jax.numpy as jnp
import numpy as np
from jax import lax
from jax.experimental import pallas as pl
from jax.experimental.pallas import tpu as pltpu
from jax.sharding import PartitionSpec as P

MODES = 128
HALO = 64

EPSILON = 1e-06
TIME_STEP = 0.5
MEAN_FLOW = 0.8
CORIOLIS = 0.6
STRATIFICATION = 0.9

LANES = 128
MIB = 1 << 20
GROUP = 4
NT = (((1,), (1,)), ((), ()))
NN = (((1,), (0,)), ((), ()))


def window_tables(window, rim_width, points, mode_count):
    position = np.arange(window)
    mode_index = np.arange(mode_count)
    half_count = mode_count // 2
    is_cosine = mode_index <= half_count
    wave_index = np.where(is_cosine, mode_index, mode_index - half_count)
    product_index = position[:, None] * wave_index[None, :] % window
    phases = 2.0 * np.pi * product_index / window
    weights_norm = np.where(wave_index == 0, np.sqrt(1.0 / window), np.sqrt(2.0 / window))
    basis = np.where(is_cosine[None, :], np.cos(phases), np.sin(phases)) * weights_norm[None, :]
    wavenumber = 2.0 * np.pi * wave_index / window
    paired = wave_index[:, None] == wave_index[None, :]
    to_sine = is_cosine[:, None] & ~is_cosine[None, :] & paired
    to_cosine = ~is_cosine[:, None] & is_cosine[None, :] & paired
    derivative = np.where(to_sine, -wavenumber[:, None], 0.0) + np.where(
        to_cosine, wavenumber[:, None], 0.0
    )
    taper = 0.25 + 0.75 * np.sin(np.pi * (position + 0.5) / window) ** 2
    values = basis * taper[:, None]
    slopes = (basis @ derivative) * taper[:, None]
    back_table = (
        basis[rim_width : rim_width + points, :] / taper[rim_width : rim_width + points, None]
    ).T
    return values, slopes, back_table


def step_tables(values, slopes, rim, points):
    direct = values - TIME_STEP * MEAN_FLOW * slopes
    couplings = (
        (TIME_STEP * CORIOLIS, -TIME_STEP * CORIOLIS),
        (TIME_STEP, -TIME_STEP * STRATIFICATION),
    )
    tables = []
    for to_first, to_second in couplings:
        first = (direct, to_first * values)
        second = (to_second * values, direct)
        rows = []
        for part in (first, second):
            pieces = []
            for begin, end in ((rim, rim + points), (0, rim), (rim + points, points + 2 * rim)):
                pieces += [part[0][begin:end].T, part[1][begin:end].T]
            rows.append(np.concatenate(pieces, axis=1))
        tables.append(np.concatenate(rows, axis=0))
    return np.stack(tables)


def split_table(table):
    table = np.asarray(table, np.float32)
    high = table.astype(jnp.bfloat16)
    low = (table - high.astype(np.float32)).astype(jnp.bfloat16)
    return jnp.asarray(high), jnp.asarray(low)


def split(x):
    high = x.astype(jnp.bfloat16)
    low = (x - high.astype(jnp.float32)).astype(jnp.bfloat16)
    return high, low


def dot(a, b, dims):
    return lax.dot_general(a, b, dims, preferred_element_type=jnp.float32)


def left_lanes(shape):
    return lax.broadcasted_iota(jnp.int32, shape, len(shape) - 1) < LANES // 2


def swap(x):
    return pltpu.roll(x, LANES // 2, len(x.shape) - 1)


def pack_kernel(state_ref, last_ref, first_ref, sums_ref):
    rows = state_ref.shape[2]
    left = left_lanes((rows, LANES))
    totals = []
    for e in range(GROUP):
        acc = jnp.zeros((rows, LANES), jnp.float32)
        for p in range(2):
            a = state_ref[e, p]
            b = state_ref[e, p + 2]
            acc += a * a + b * b
            last_ref[e, p] = jnp.where(left, swap(a), b)
            first_ref[e, p] = jnp.where(left, a, swap(b))
        totals.append(jnp.sum(acc))
    half = left_lanes((4, LANES))
    for q in range(GROUP // 2):
        sums_ref[4 * q : 4 * q + 4] = jnp.where(half, totals[2 * q], totals[2 * q + 1])


def split_kernel(inverse_ref, high_ref, low_ref):
    high_ref[...], low_ref[...] = split(inverse_ref[...])


def project_kernel(state_ref, before_ref, after_ref, high_ref, low_ref, mask_ref, out_ref):
    parts, slots, rows, _ = out_ref.shape
    coef = state_ref.shape[2]
    count = slots * parts
    flat = out_ref.reshape(parts * slots * rows, LANES)
    mask = mask_ref[...]
    for p in range(2):
        x = jnp.concatenate(
            [
                state_ref[:, p].reshape(GROUP * coef, LANES),
                state_ref[:, p + 2].reshape(GROUP * coef, LANES),
                before_ref[:, p].reshape(GROUP * coef, LANES),
                after_ref[:, p].reshape(GROUP * coef, LANES),
            ],
            axis=1,
        )
        x_high, x_low = split(x)
        w_high = high_ref[p]
        w_low = low_ref[p]
        t = dot(w_high, x_high, NT) + (dot(w_high, x_low, NT) + dot(w_low, x_high, NT))
        t = t * mask
        for f in range(2):
            for q in range(GROUP // 2):
                row = 4 * q + p + 2 * f
                flat[pl.ds(row, count, stride=rows), :] = t[
                    f * count : (f + 1) * count, q * LANES : (q + 1) * LANES
                ]


def solve_kernel(recv_ref, high_ref, low_ref, wall_ref, sums_ref, out_ref):
    parts, slots, rows, _ = recv_ref.shape
    left = left_lanes((rows, LANES))
    lane = lax.broadcasted_iota(jnp.int32, (rows, LANES), 1)
    sums = jnp.zeros((rows, LANES), jnp.float32)
    for m in range(slots):
        t = [recv_ref[s, m] for s in range(parts)]
        even, odd = [], []
        for s in range(0, parts, 2):
            even.append(jnp.where(left, t[s], swap(t[s + 1])))
            odd.append(jnp.where(left, swap(t[s]), t[s + 1]))
        r = jnp.concatenate(
            [jnp.concatenate(even, axis=1), jnp.concatenate(odd, axis=1)], axis=0
        )
        r_high, r_low = split(r)
        v_high = high_ref[m]
        v_low = low_ref[m]
        both = dot(jnp.concatenate([r_high, r_low], axis=0), v_high, NT)
        o = both[: 2 * rows] + (both[2 * rows :] + dot(r_high, v_low, NT))
        for s in range(0, parts, 2):
            a = o[:rows, s * 64 : s * 64 + LANES]
            b = o[rows:, s * 64 : s * 64 + LANES]
            out_ref[s, m] = jnp.where(left, a, swap(b))
            out_ref[s + 1, m] = jnp.where(left, swap(a), b)
        for w in range(2):
            q = jnp.sum(o * wall_ref[w : w + 1, :], axis=1, keepdims=True)
            for e in range(2):
                at = e * 2 * slots + w * slots + m
                sums = jnp.where(lane == at, q[e * rows : (e + 1) * rows], sums)
    for k in range(parts):
        out_ref[k, slots] = sums
        out_ref[k, slots + 1] = sums_ref[...]


def back_kernel(total, recv_ref, high_ref, low_ref, *refs):
    out_ref, wall_ref = refs[-2:]
    parts, slots, rows, _ = recv_ref.shape
    coef = out_ref.shape[2]
    width = slots - 2
    flat = recv_ref.reshape(parts * slots * rows, LANES)
    b_high = high_ref[...]
    b_low = low_ref[...]
    n = recv_ref[0, slots - 1]
    for k in range(1, parts):
        n = n + recv_ref[k, slots - 1]
    scale = lax.rsqrt(n / total + EPSILON)
    for r in range(rows):
        q, f = r // 4, r % 4
        s = jnp.concatenate(
            [flat[pl.ds(k * slots * rows + r, width, stride=rows), :] for k in range(parts)],
            axis=0,
        )
        s = (s * scale[r : r + 1]).T
        s_high, s_low = split(s)
        o = dot(s_high, b_high, NN) + (dot(s_high, b_low, NN) + dot(s_low, b_high, NN))
        for e in range(2):
            out_ref[2 * q + e, f] = o[e * coef : (e + 1) * coef]
    lane = lax.broadcasted_iota(jnp.int32, (rows, LANES), 1)
    tiles = [recv_ref[k, slots - 2] * scale for k in range(parts)]
    for e in range(2):
        for w in range(2):
            g = jnp.zeros((rows, LANES), jnp.float32)
            for k in range(parts):
                shift = (k * width - (e * 2 + w) * width) % LANES
                tile = pltpu.roll(tiles[k], shift, 1) if shift else tiles[k]
                g = jnp.where((lane >= k * width) & (lane < (k + 1) * width), tile, g)
            g_high, g_low = split(g)
            o = dot(g_high, b_high, NN) + (dot(g_high, b_low, NN) + dot(g_low, b_high, NN))
            for q in range(GROUP // 2):
                for c in range(2):
                    row = 4 * q + 2 * c
                    wall_ref[2 * q + e, w, c : c + 1] = o[row : row + 1]


def shifted(x, axis, by):
    n = lax.axis_size(axis)
    return lax.ppermute(x, axis, [(i, (i + by) % n) for i in range(n)])


def ring_sum(x, axis):
    n = lax.axis_size(axis)
    if n & (n - 1):
        return lax.psum(x, axis)
    hop = 1
    while hop < n:
        x = x + shifted(x, axis, hop)
        hop *= 2
    return x


def whole(shape):
    return pl.BlockSpec(shape, lambda *_: (0,) * len(shape))


def per_device(state, inverse):
    members, fields, coef, points = state.shape
    parts = lax.axis_size("gy")
    coef_count = coef * parts
    grid_x = points * lax.axis_size("gx")
    window = points + 2 * HALO
    mine = MODES // parts
    group_rows = GROUP * fields * coef // LANES
    groups = members // GROUP

    values, slopes, back_table = window_tables(window, HALO, points, MODES)
    step_high, step_low = split_table(step_tables(values, slopes, HALO, points))
    back_high, back_low = split_table(back_table)
    k = np.arange(coef_count)
    curvature = k * k / (coef_count * coef_count)
    wall = np.zeros((8, coef_count), np.float32)
    wall[0] = curvature
    wall[1] = np.where(k % 2 == 0, -1.0, 1.0) * curvature
    wall = jnp.asarray(wall)

    coef_global = lax.axis_index("gy") * coef + jnp.arange(coef, dtype=jnp.int32)
    keep = (coef_global < coef_count - 2).astype(jnp.float32)
    mask = jnp.tile(keep, GROUP)[None, :]

    def grouped(g, shape):
        return pl.BlockSpec((GROUP,) + shape, lambda i: (g,) + (0,) * len(shape))

    def call(kernel, name, vmem, flops, moved, **kwargs):
        return pl.pallas_call(
            kernel,
            grid=(1,),
            name=name,
            compiler_params=pltpu.CompilerParams(vmem_limit_bytes=vmem * MIB),
            cost_estimate=pl.CostEstimate(flops=flops, bytes_accessed=moved, transcendentals=0),
            **kwargs,
        )

    block = (fields, coef, points)
    halo = (GROUP, 2, coef, LANES)
    halo_bytes = 4 * int(np.prod(halo))
    small = (group_rows, LANES)
    sent_shape = (parts, mine, group_rows, LANES)
    back_shape = (parts, mine + 2, group_rows, LANES)

    packed = []
    for g in range(groups):
        packed.append(
            call(
                pack_kernel,
                f"pack{g}",
                6,
                10**6,
                4 * halo_bytes,
                in_specs=[grouped(g, block)],
                out_specs=[whole(halo), whole(halo), whole(small)],
                out_shape=[
                    jax.ShapeDtypeStruct(halo, jnp.float32),
                    jax.ShapeDtypeStruct(halo, jnp.float32),
                    jax.ShapeDtypeStruct(small, jnp.float32),
                ],
            )(state)
        )
    halos = [(shifted(p[0], "gx", 1), shifted(p[1], "gx", -1)) for p in packed]
    sums = ring_sum(jnp.concatenate([p[2] for p in packed], axis=0), "gx")

    per_step = 4
    split_shape = (per_step, coef_count, coef_count)
    inverse_high, inverse_low = pl.pallas_call(
        split_kernel,
        grid=(mine // per_step,),
        in_specs=[pl.BlockSpec(split_shape, lambda i: (i, 0, 0))],
        out_specs=[pl.BlockSpec(split_shape, lambda i: (i, 0, 0))] * 2,
        out_shape=[jax.ShapeDtypeStruct(inverse.shape, jnp.bfloat16)] * 2,
        name="split",
        compiler_params=pltpu.CompilerParams(vmem_limit_bytes=8 * MIB),
        cost_estimate=pl.CostEstimate(
            flops=10**7, bytes_accessed=8 * mine * coef_count**2, transcendentals=0
        ),
    )(inverse)

    outputs = []
    for g in range(groups):
        sent = call(
            project_kernel,
            f"project{g}",
            8,
            2 * 3 * 2 * 256 * 512 * GROUP * coef,
            6 * halo_bytes,
            in_specs=[
                grouped(g, block),
                whole(halo),
                whole(halo),
                whole(step_high.shape),
                whole(step_low.shape),
                whole(mask.shape),
            ],
            out_specs=whole(sent_shape),
            out_shape=jax.ShapeDtypeStruct(sent_shape, jnp.float32),
        )(state, *halos[g], step_high, step_low, mask)
        got = lax.all_to_all(sent, "gy", split_axis=0, concat_axis=0, tiled=True)
        solved = call(
            solve_kernel,
            f"solve{g}",
            24,
            2 * 3 * mine * coef_count**2 * 256,
            4 * mine * coef_count**2,
            in_specs=[
                whole(sent_shape),
                whole(inverse.shape),
                whole(inverse.shape),
                whole(wall.shape),
                pl.BlockSpec(small, lambda i: (g, 0)),
            ],
            out_specs=whole(back_shape),
            out_shape=jax.ShapeDtypeStruct(back_shape, jnp.float32),
        )(got, inverse_high, inverse_low, wall, sums)
        returned = lax.all_to_all(solved, "gy", split_axis=0, concat_axis=0, tiled=True)
        outputs = call(
            functools.partial(back_kernel, float(fields * coef_count * grid_x)),
            f"back{g}",
            8,
            2 * 3 * 128 * 128 * GROUP * fields * coef,
            4 * halo_bytes,
            in_specs=[whole(back_shape), whole(back_high.shape), whole(back_low.shape)]
            + [pl.BlockSpec(memory_space=pl.ANY)] * len(outputs),
            out_specs=[grouped(g, block), grouped(g, (2, 2, points))],
            out_shape=[
                jax.ShapeDtypeStruct(state.shape, jnp.float32),
                jax.ShapeDtypeStruct((members, 2, 2, points), jnp.float32),
            ],
            input_output_aliases={3 + i: i for i in range(len(outputs))},
        )(returned, back_high, back_low, *outputs)
    return tuple(outputs)


def solution(mesh):
    placed = (P(None, None, "gy", "gx"), P("gy", None, None))
    return jax.shard_map(
        per_device,
        mesh=mesh,
        in_specs=placed,
        out_specs=(P(None, None, "gy", "gx"), P(None, None, None, "gx")),
        check_vma=False,
    )
```

time: 124 us -> 132 us (1.065)
  blocking collectives: 50 us -> 0 us
  starting transfers between devices: 8.43 us -> 37.4 us
  local copies, waits for them, and re-layouts: 2.37 us -> 19.7 us
  waiting for transfers between devices: 38.1 us -> 52.4 us
  Pallas kernels: 22.9 us -> 21.1 us
    all_to_all x2 -> x0, blocking collectives: 50 us -> none  [the longest x1 25 us: per_device(): got = lax.all_to_all(sent, 'gy', split_axis=0, concat_axis=0, tiled=True)]
    all_to_all x0 -> x6, starting transfers between devices: none -> 21.6 us  [the longest x3 11.2 us: per_device(): got = lax.all_to_all(sent, 'gy', split_axis=0, concat_axis=0, tiled=True)]
    unnamed x4 -> x34, local copies, waits for them, and re-layouts: 1.75 us -> 19.6 us
    all_to_all x0 -> x6, waiting for transfers between devices: none -> 9.54 us  [the longest x3 9.53 us: per_device(): lax.all_to_all(solved, 'gy', split_axis=0, concat_axis=0, tiled=True)]
    ppermute x5 -> x9, starting transfers between devices: 8.43 us -> 15.7 us  [shifted(): return lax.ppermute(x, axis, [(i, (i + by) % n) for i in range(n)])]
    ppermute x5 -> x9, waiting for transfers between devices: 38.1 us -> 42.9 us  [shifted(): return lax.ppermute(x, axis, [(i, (i + by) % n) for i in range(n)])]
    pallas_call x4 -> x13, Pallas kernels: 22.9 us -> 21.1 us  [the longest x3 10.9 us: per_device(): call(solve_kernel, f'solve{g}', 24, 2 * 3 * mine * coef_count ** 2 * 256,...]
  transfers between devices with their start and end apart: 5 -> 15, of which waited for: 3 -> 11; matrix products, arithmetic and copies ran while one was open for 2% -> 0% of each run, Pallas kernels for 0% -> 14%
where the time goes in v1:
time: 132 us; the launch traced here: 131 us
  waiting for transfers between devices  52.4 us (40%)
  starting transfers between devices  37.4 us (28%)
  Pallas kernels  21.1 us (16%)
  local copies, waits for them, and re-layouts  19.7 us (15%)
    ppermute x9, waiting for transfers between devices, shifted(): return lax.ppermute(x, axis, [(i, (i + by) % n) for i in range(n)])  42.9 us
    unnamed x34, local copies, waits for them, and re-layouts  19.6 us
    ppermute x9, starting transfers between devices, shifted(): return lax.ppermute(x, axis, [(i, (i + by) % n) for i in range(n)])  15.7 us
    all_to_all x3, starting transfers between devices, per_device(): got = lax.all_to_all(sent, 'gy', split_axis=0, concat_axis=0, tiled=True)  11.2 us
    pallas_call x3, Pallas kernels, per_device(): call(solve_kernel, f'solve{g}', 24, 2 * 3 * mine * coef_count ** 2 * 256,...  10.9 us
    all_to_all x3, starting transfers between devices, per_device(): lax.all_to_all(solved, 'gy', split_axis=0, concat_axis=0, tiled=True)  10.4 us
    all_to_all x3, waiting for transfers between devices, per_device(): lax.all_to_all(solved, 'gy', split_axis=0, concat_axis=0, tiled=True)  9.53 us
    pallas_call x3, Pallas kernels, per_device(): call(project_kernel, f'project{g}', 8, 2 * 3 * 2 * 256 * 512 * GROUP * co...  4.36 us
  transfers between devices with their start and end apart: 15, of which 11 were waited for; matrix products, arithmetic and copies ran while one was open for 0% of the time, Pallas kernels for 14%

profile of v1, /device:TPU:0, one launch (start us, length us, event | category | flops | bytes accessed | tf_op | source)
XLA Modules:
  0.0 131.4 jit_solution(17425917305337049695)
XLA Ops:
  0.6 0.0 copy-start
  0.6 1.4 %copy-done = f32[12,4,64,128]{3,2,1,0:T(8,128)S(1)} copy-done((f32[12,4,64,128]{3,2,1,0:T(8,128)S(1)}, f32[12,4,64,128]{3,2,1,0:T(8,128)}, u32[]{:S(2)}) %copy-start) | copy-done | bytes 1572888
  2.0 0.0 copy-start.1
  2.0 0.3 pack1.1
  2.3 3.0 %collective-permute-start.5 = (f32[4,2,64,128]{3,2,1,0:T(8,128)S(1)}, f32[4,2,64,128]{3,2,1,0:T(8,128)S(1)}, u32[]{:S(2)}, u32[]{:S(2)}) collective-permute-start(f32[4,2,64,128]{3,2,1,0:T(8,128)S(1)} %get-tuple-element.24), channel_id=1, source_target_pairs={{0,4},{4,8},{8,12},{12,16},{16,20},{20,24},{24,28},{28,0},{1,5},{5... | collective-permute-start | bytes 786440 | tf_op jit(solution)/shard_map/ppermute | solution.py:225
  5.3 3.1 %collective-permute-start.6 = (f32[4,2,64,128]{3,2,1,0:T(8,128)S(1)}, f32[4,2,64,128]{3,2,1,0:T(8,128)S(1)}, u32[]{:S(2)}, u32[]{:S(2)}) collective-permute-start(f32[4,2,64,128]{3,2,1,0:T(8,128)S(1)} %get-tuple-element.25), channel_id=1, source_target_pairs={{0,28},{4,0},{8,4},{12,8},{16,12},{20,16},{24,20},{28,24},{1,29},{... | collective-permute-start | bytes 786440 | tf_op jit(solution)/shard_map/ppermute | solution.py:225
  8.5 0.1 broadcast_in_dim_tile.3.mask_ref
  8.5 8.0 %collective-permute-done.5.before_ref = f32[4,2,64,128]{3,2,1,0:T(8,128)S(1)} collective-permute-done((f32[4,2,64,128]{3,2,1,0:T(8,128)S(1)}, f32[4,2,64,128]{3,2,1,0:T(8,128)S(1)}, u32[]{:S(2)}, u32[]{:S(2)}) %collective-permute-start.5) | collective-permute-done | bytes 262176 | tf_op jit(solution)/shard_map/ppermute | solution.py:225
  16.5 2.2 %collective-permute-done.6.after_ref = f32[4,2,64,128]{3,2,1,0:T(8,128)S(1)} collective-permute-done((f32[4,2,64,128]{3,2,1,0:T(8,128)S(1)}, f32[4,2,64,128]{3,2,1,0:T(8,128)S(1)}, u32[]{:S(2)}, u32[]{:S(2)}) %collective-permute-start.6) | collective-permute-done | bytes 262176 | tf_op jit(solution)/shard_map/ppermute | solution.py:225
  18.7 0.0 copy-done.1
  18.7 1.0 copy-done.3
  19.8 1.0 copy-done.5
  20.8 1.4 %project1.1 = f32[4,32,8,128]{3,2,1,0:T(8,128)} custom-call(f32[12,4,64,128]{3,2,1,0:T(8,128)S(1)} %copy-done.1, f32[4,2,64,128]{3,2,1,0:T(8,128)S(1)} %collective-permute-done.5.before_ref, f32[4,2,64,128]{3,2,1,0:T(8,128)S(1)} %collective-permute-done.6.after_ref, bf16[2,256,512]{2,1,0:T(8,128)(2,1)S(1)} %copy-done.5, bf16[2,256,512]{2,1,0:T(8,128)(2,1)S(1)} %copy-done.3, ...), custom_call_target="tpu_custom_call" | custom-call | flops 402653184 | bytes 1572864 | tf_op jit(solution)/shard_map/project1/pallas_call | solution.py:325
  22.2 3.6 %all-to-all-start.2 = ((f32[4,32,8,128]{3,2,1,0:T(8,128)}), f32[4,32,8,128]{3,2,1,0:T(8,128)S(1)}, u32[]{:S(2)}, u32[]{:S(2)}) async-start(f32[4,32,8,128]{3,2,1,0:T(8,128)} %project1.1), calls=%async_computation.2 | async-start | bytes 1048576 | tf_op jit(solution)/shard_map/all_to_all | solution.py:342
  25.9 0.3 pack0.1
  26.1 0.3 collective-permute-start.7
  26.5 4.4 %collective-permute-start.8 = (f32[4,2,64,128]{3,2,1,0:T(8,128)S(1)}, f32[4,2,64,128]{3,2,1,0:T(8,128)S(1)}, u32[]{:S(2)}, u32[]{:S(2)}) collective-permute-start(f32[4,2,64,128]{3,2,1,0:T(8,128)S(1)} %get-tuple-element.27), channel_id=1, source_target_pairs={{0,28},{4,0},{8,4},{12,8},{16,12},{20,16},{24,20},{28,24},{1,29},{... | collective-permute-start | bytes 786440 | tf_op jit(solution)/shard_map/ppermute | solution.py:225
  30.9 7.4 %collective-permute-done.7.before_ref = f32[4,2,64,128]{3,2,1,0:T(8,128)S(1)} collective-permute-done((f32[4,2,64,128]{3,2,1,0:T(8,128)S(1)}, f32[4,2,64,128]{3,2,1,0:T(8,128)S(1)}, u32[]{:S(2)}, u32[]{:S(2)}) %collective-permute-start.7) | collective-permute-done | bytes 262176 | tf_op jit(solution)/shard_map/ppermute | solution.py:225
  38.3 2.9 %collective-permute-done.8.after_ref = f32[4,2,64,128]{3,2,1,0:T(8,128)S(1)} collective-permute-done((f32[4,2,64,128]{3,2,1,0:T(8,128)S(1)}, f32[4,2,64,128]{3,2,1,0:T(8,128)S(1)}, u32[]{:S(2)}, u32[]{:S(2)}) %collective-permute-start.8) | collective-permute-done | bytes 262176 | tf_op jit(solution)/shard_map/ppermute | solution.py:225
  41.2 0.0 copy-done.4
  41.2 0.0 copy-done.6
  41.2 1.5 %project0.1 = f32[4,32,8,128]{3,2,1,0:T(8,128)} custom-call(f32[12,4,64,128]{3,2,1,0:T(8,128)S(1)} %copy-done.1, f32[4,2,64,128]{3,2,1,0:T(8,128)S(1)} %collective-permute-done.7.before_ref, f32[4,2,64,128]{3,2,1,0:T(8,128)S(1)} %collective-permute-done.8.after_ref, bf16[2,256,512]{2,1,0:T(8,128)(2,1)S(1)} %copy-done.6, bf16[2,256,512]{2,1,0:T(8,128)(2,1)S(1)} %copy-done.4, ...), custom_call_target="tpu_custom_call" | custom-call | flops 402653184 | bytes 1572864 | tf_op jit(solution)/shard_map/project0/pallas_call | solution.py:325
  42.7 0.0 all-to-all-done.2.recv_ref
  42.7 4.1 %all-to-all-start.4 = ((f32[4,32,8,128]{3,2,1,0:T(8,128)}), f32[4,32,8,128]{3,2,1,0:T(8,128)}, u32[]{:S(2)}, u32[]{:S(2)}) async-start(f32[4,32,8,128]{3,2,1,0:T(8,128)} %project0.1), calls=%async_computation.4 | async-start | bytes 1048576 | tf_op jit(solution)/shard_map/all_to_all | solution.py:342
  46.8 0.3 pack2.1
  47.1 0.1 collective-permute-start
  47.2 4.7 %collective-permute-start.1 = (f32[4,2,64,128]{3,2,1,0:T(8,128)S(1)}, f32[4,2,64,128]{3,2,1,0:T(8,128)S(1)}, u32[]{:S(2)}, u32[]{:S(2)}) collective-permute-start(f32[4,2,64,128]{3,2,1,0:T(8,128)S(1)} %get-tuple-element.18), channel_id=1, source_target_pairs={{0,28},{4,0},{8,4},{12,8},{16,12},{20,16},{24,20},{28,24},{1,29},{... | collective-permute-start | bytes 786440 | tf_op jit(solution)/shard_map/ppermute | solution.py:225
  51.9 7.4 %collective-permute-done.before_ref = f32[4,2,64,128]{3,2,1,0:T(8,128)S(1)} collective-permute-done((f32[4,2,64,128]{3,2,1,0:T(8,128)S(1)}, f32[4,2,64,128]{3,2,1,0:T(8,128)S(1)}, u32[]{:S(2)}, u32[]{:S(2)}) %collective-permute-start) | collective-permute-done | bytes 262176 | tf_op jit(solution)/shard_map/ppermute | solution.py:225
  59.3 3.1 %collective-permute-done.1.after_ref = f32[4,2,64,128]{3,2,1,0:T(8,128)S(1)} collective-permute-done((f32[4,2,64,128]{3,2,1,0:T(8,128)S(1)}, f32[4,2,64,128]{3,2,1,0:T(8,128)S(1)}, u32[]{:S(2)}, u32[]{:S(2)}) %collective-permute-start.1) | collective-permute-done | bytes 262176 | tf_op jit(solution)/shard_map/ppermute | solution.py:225
  62.4 1.4 %project2.1 = f32[4,32,8,128]{3,2,1,0:T(8,128)} custom-call(f32[12,4,64,128]{3,2,1,0:T(8,128)S(1)} %copy-done.1, f32[4,2,64,128]{3,2,1,0:T(8,128)S(1)} %collective-permute-done.before_ref, f32[4,2,64,128]{3,2,1,0:T(8,128)S(1)} %collective-permute-done.1.after_ref, bf16[2,256,512]{2,1,0:T(8,128)(2,1)S(1)} %copy-done.6, bf16[2,256,512]{2,1,0:T(8,128)(2,1)S(1)} %copy-done.4, ...), custom_call_target="tpu_custom_call" | custom-call | flops 402653184 | bytes 1572864 | tf_op jit(solution)/shard_map/project2/pallas_call | solution.py:325
  63.8 0.0 all-to-all-done.4.recv_ref
  63.8 3.5 %all-to-all-start = ((f32[4,32,8,128]{3,2,1,0:T(8,128)}), f32[4,32,8,128]{3,2,1,0:T(8,128)S(1)}, u32[]{:S(2)}, u32[]{:S(2)}) async-start(f32[4,32,8,128]{3,2,1,0:T(8,128)} %project2.1), calls=%async_computation | async-start | bytes 1048576 | tf_op jit(solution)/shard_map/all_to_all | solution.py:342
  67.3 0.1 collective-permute-start.2
  67.4 6.4 %collective-permute-done.2 = f32[24,128]{1,0:T(8,128)S(1)} collective-permute-done((f32[24,128]{1,0:T(8,128)S(1)}, f32[24,128]{1,0:T(8,128)S(1)}, u32[]{:S(2)}, u32[]{:S(2)}) %collective-permute-start.2) | collective-permute-done | bytes 12320 | tf_op jit(solution)/shard_map/ppermute | solution.py:225
  73.7 0.0 collective-permute-start.3
  73.7 5.6 %collective-permute-done.3 = f32[24,128]{1,0:T(8,128)S(1)} collective-permute-done((f32[24,128]{1,0:T(8,128)S(1)}, f32[24,128]{1,0:T(8,128)S(1)}, u32[]{:S(2)}, u32[]{:S(2)}) %collective-permute-start.3) | collective-permute-done | bytes 12320 | tf_op jit(solution)/shard_map/ppermute | solution.py:225
  79.3 0.0 collective-permute-start.4
  79.3 3.4 %copy-done.2 = f32[32,256,256]{2,1,0:T(8,128)S(1)} copy-done((f32[32,256,256]{2,1,0:T(8,128)S(1)}, f32[32,256,256]{2,1,0:T(8,128)}, u32[]{:S(2)}) %copy-start.2) | copy-done | bytes 8388632
  82.7 1.2 split.1
  83.9 0.0 collective-permute-done.4
  83.9 0.0 copy-done.15
  84.0 4.4 %solve0.1 = f32[4,34,8,128]{3,2,1,0:T(8,128)} custom-call(f32[4,32,8,128]{3,2,1,0:T(8,128)} %all-to-all-done.4.recv_ref, bf16[32,256,256]{2,1,0:T(8,128)(2,1)S(1)} %get-tuple-element.19.high_ref, bf16[32,256,256]{2,1,0:T(8,128)(2,1)S(1)} %get-tuple-element.20.low_ref, f32[8,256]{1,0:T(8,128)S(1)} %copy-done.15, f32[24,128]{1,0:T(8,128)S(1)} %add.23.sums_ref), custom_call_target="tpu_custom_call" | custom-call | flops 3221225472 | bytes 8388608 | tf_op jit(solution)/shard_map/solve0/pallas_call | solution.py:343
  88.3 2.0 %copy-done.9 = bf16[32,256,256]{2,1,0:T(8,128)(2,1)} copy-done((bf16[32,256,256]{2,1,0:T(8,128)(2,1)}, bf16[32,256,256]{2,1,0:T(8,128)(2,1)S(1)}, u32[]{:S(2)}) %copy-start.9) | copy-done | bytes 4194328
  90.3 2.0 %copy-done.12 = bf16[32,256,256]{2,1,0:T(8,128)(2,1)} copy-done((bf16[32,256,256]{2,1,0:T(8,128)(2,1)}, bf16[32,256,256]{2,1,0:T(8,128)(2,1)S(1)}, u32[]{:S(2)}) %copy-start.12) | copy-done | bytes 4194328
  92.3 0.0 all-to-all-done.recv_ref
  92.4 3.5 %all-to-all-start.5 = ((f32[4,34,8,128]{3,2,1,0:T(8,128)}), f32[4,34,8,128]{3,2,1,0:T(8,128)S(1)}, u32[]{:S(2)}, u32[]{:S(2)}) async-start(f32[4,34,8,128]{3,2,1,0:T(8,128)} %solve0.1), calls=%async_computation.5 | async-start | bytes 1114112 | tf_op jit(solution)/shard_map/all_to_all | solution.py:359
  95.8 0.0 copy-start.10
  95.8 2.2 %copy-done.10 = bf16[32,256,256]{2,1,0:T(8,128)(2,1)S(1)} copy-done((bf16[32,256,256]{2,1,0:T(8,128)(2,1)S(1)}, bf16[32,256,256]{2,1,0:T(8,128)(2,1)}, u32[]{:S(2)}) %copy-start.10) | copy-done | bytes 4194328
  98.0 2.2 %copy-done.13 = bf16[32,256,256]{2,1,0:T(8,128)(2,1)S(1)} copy-done((bf16[32,256,256]{2,1,0:T(8,128)(2,1)S(1)}, bf16[32,256,256]{2,1,0:T(8,128)(2,1)}, u32[]{:S(2)}) %copy-start.13) | copy-done | bytes 4194328
  100.2 3.3 %solve1.1 = f32[4,34,8,128]{3,2,1,0:T(8,128)} custom-call(f32[4,32,8,128]{3,2,1,0:T(8,128)S(1)} %all-to-all-done.2.recv_ref, bf16[32,256,256]{2,1,0:T(8,128)(2,1)S(1)} %copy-done.10, bf16[32,256,256]{2,1,0:T(8,128)(2,1)S(1)} %copy-done.13, f32[8,256]{1,0:T(8,128)S(1)} %copy-done.15, f32[24,128]{1,0:T(8,128)S(1)} %add.23.sums_ref), custom_call_target="tpu_custom_call" | custom-call | flops 3221225472 | bytes 8388608 | tf_op jit(solution)/shard_map/solve1/pallas_call | solution.py:343
  103.5 1.5 %all-to-all-done.5.recv_ref = f32[4,34,8,128]{3,2,1,0:T(8,128)S(1)} async-done(((f32[4,34,8,128]{3,2,1,0:T(8,128)}), f32[4,34,8,128]{3,2,1,0:T(8,128)S(1)}, u32[]{:S(2)}, u32[]{:S(2)}) %all-to-all-start.5) | async-done | bytes 557088 | tf_op jit(solution)/shard_map/all_to_all | solution.py:359
  105.0 3.5 %all-to-all-start.3 = ((f32[4,34,8,128]{3,2,1,0:T(8,128)}), f32[4,34,8,128]{3,2,1,0:T(8,128)S(1)}, u32[]{:S(2)}, u32[]{:S(2)}) async-start(f32[4,34,8,128]{3,2,1,0:T(8,128)} %solve1.1), calls=%async_computation.3 | async-start | bytes 1114112 | tf_op jit(solution)/shard_map/all_to_all | solution.py:359
  108.4 0.0 copy-start.11
  108.5 2.2 %copy-done.11 = bf16[32,256,256]{2,1,0:T(8,128)(2,1)S(1)} copy-done((bf16[32,256,256]{2,1,0:T(8,128)(2,1)S(1)}, bf16[32,256,256]{2,1,0:T(8,128)(2,1)}, u32[]{:S(2)}) %copy-start.11) | copy-done | bytes 4194328
  110.6 2.2 %copy-done.14 = bf16[32,256,256]{2,1,0:T(8,128)(2,1)S(1)} copy-done((bf16[32,256,256]{2,1,0:T(8,128)(2,1)S(1)}, bf16[32,256,256]{2,1,0:T(8,128)(2,1)}, u32[]{:S(2)}) %copy-start.14) | copy-done | bytes 4194328
  112.8 3.3 %solve2.1 = f32[4,34,8,128]{3,2,1,0:T(8,128)} custom-call(f32[4,32,8,128]{3,2,1,0:T(8,128)S(1)} %all-to-all-done.recv_ref, bf16[32,256,256]{2,1,0:T(8,128)(2,1)S(1)} %copy-done.11, bf16[32,256,256]{2,1,0:T(8,128)(2,1)S(1)} %copy-done.14, f32[8,256]{1,0:T(8,128)S(1)} %copy-done.15, f32[24,128]{1,0:T(8,128)S(1)} %add.23.sums_ref), custom_call_target="tpu_custom_call" | custom-call | flops 3221225472 | bytes 8388608 | tf_op jit(solution)/shard_map/solve2/pallas_call | solution.py:343
  116.1 1.5 %all-to-all-done.3.recv_ref = f32[4,34,8,128]{3,2,1,0:T(8,128)S(1)} async-done(((f32[4,34,8,128]{3,2,1,0:T(8,128)}), f32[4,34,8,128]{3,2,1,0:T(8,128)S(1)}, u32[]{:S(2)}, u32[]{:S(2)}) %all-to-all-start.3) | async-done | bytes 557088 | tf_op jit(solution)/shard_map/all_to_all | solution.py:359
  117.6 3.5 %all-to-all-start.1 = ((f32[4,34,8,128]{3,2,1,0:T(8,128)}), f32[4,34,8,128]{3,2,1,0:T(8,128)S(1)}, u32[]{:S(2)}, u32[]{:S(2)}) async-start(f32[4,34,8,128]{3,2,1,0:T(8,128)} %solve2.1), calls=%async_computation.1 | async-start | bytes 1114112 | tf_op jit(solution)/shard_map/all_to_all | solution.py:359
  121.1 0.0 copy-done.7
  121.1 0.0 copy-done.8
  121.1 1.3 back0.1
  122.3 1.3 back1.1
  123.6 6.6 %all-to-all-done.1.recv_ref = f32[4,34,8,128]{3,2,1,0:T(8,128)S(1)} async-done(((f32[4,34,8,128]{3,2,1,0:T(8,128)}), f32[4,34,8,128]{3,2,1,0:T(8,128)S(1)}, u32[]{:S(2)}, u32[]{:S(2)}) %all-to-all-start.1) | async-done | bytes 557088 | tf_op jit(solution)/shard_map/all_to_all | solution.py:359
  130.2 1.3 back2.1
  (20 shorter events, 0.0 us)
Async XLA Ops:
  0.6 1.4 %copy-start = (f32[12,4,64,128]{3,2,1,0:T(8,128)S(1)}, f32[12,4,64,128]{3,2,1,0:T(8,128)}, u32[]{:S(2)}) copy-start(f32[12,4,64,128]{3,2,1,0:T(8,128)} %state_ref.11) | copy-start | bytes 4718596
  2.0 16.7 %copy-start.1 = (f32[12,4,64,128]{3,2,1,0:T(8,128)S(1)}, f32[12,4,64,128]{3,2,1,0:T(8,128)}, u32[]{:S(2)}) copy-start(f32[12,4,64,128]{3,2,1,0:T(8,128)} %state_ref.11) | copy-start | bytes 4718596
  2.3 14.2 %collective-permute-start.5 = (f32[4,2,64,128]{3,2,1,0:T(8,128)S(1)}, f32[4,2,64,128]{3,2,1,0:T(8,128)S(1)}, u32[]{:S(2)}, u32[]{:S(2)}) collective-permute-start(f32[4,2,64,128]{3,2,1,0:T(8,128)S(1)} %get-tuple-element.24), channel_id=1, source_target_pairs={{0,4},{4,8},{8,12},{12,16},{16,20},{20,24},{24,28},{28,0},{1,5},{5... | collective-permute-start | bytes 786440 | tf_op jit(solution)/shard_map/ppermute | solution.py:225
  5.3 13.4 %collective-permute-start.6 = (f32[4,2,64,128]{3,2,1,0:T(8,128)S(1)}, f32[4,2,64,128]{3,2,1,0:T(8,128)S(1)}, u32[]{:S(2)}, u32[]{:S(2)}) collective-permute-start(f32[4,2,64,128]{3,2,1,0:T(8,128)S(1)} %get-tuple-element.25), channel_id=1, source_target_pairs={{0,28},{4,0},{8,4},{12,8},{16,12},{20,16},{24,20},{28,24},{1,29},{... | collective-permute-start | bytes 786440 | tf_op jit(solution)/shard_map/ppermute | solution.py:225
  18.7 1.0 copy-start.3
  19.8 1.0 copy-start.5
  22.2 19.0 %copy-start.4 = (bf16[2,256,512]{2,1,0:T(8,128)(2,1)S(1)}, bf16[2,256,512]{2,1,0:T(8,128)(2,1)}, u32[]{:S(2)}) copy-start(bf16[2,256,512]{2,1,0:T(8,128)(2,1)} %constant.19.clone.low_ref) | copy-start | bytes 1572868
  22.2 19.0 %copy-start.6 = (bf16[2,256,512]{2,1,0:T(8,128)(2,1)S(1)}, bf16[2,256,512]{2,1,0:T(8,128)(2,1)}, u32[]{:S(2)}) copy-start(bf16[2,256,512]{2,1,0:T(8,128)(2,1)} %constant.18.clone.high_ref) | copy-start | bytes 1572868
  22.2 20.4 %all-to-all-start.2 = ((f32[4,32,8,128]{3,2,1,0:T(8,128)}), f32[4,32,8,128]{3,2,1,0:T(8,128)S(1)}, u32[]{:S(2)}, u32[]{:S(2)}) async-start(f32[4,32,8,128]{3,2,1,0:T(8,128)} %project1.1), calls=%async_computation.2 | async-start | bytes 1048576 | tf_op jit(solution)/shard_map/all_to_all | solution.py:342
  26.1 12.2 %collective-permute-start.7 = (f32[4,2,64,128]{3,2,1,0:T(8,128)S(1)}, f32[4,2,64,128]{3,2,1,0:T(8,128)S(1)}, u32[]{:S(2)}, u32[]{:S(2)}) collective-permute-start(f32[4,2,64,128]{3,2,1,0:T(8,128)S(1)} %get-tuple-element.26), channel_id=1, source_target_pairs={{0,4},{4,8},{8,12},{12,16},{16,20},{20,24},{24,28},{28,0},{1,5},{5... | collective-permute-start | bytes 786440 | tf_op jit(solution)/shard_map/ppermute | solution.py:225
  26.5 14.7 %collective-permute-start.8 = (f32[4,2,64,128]{3,2,1,0:T(8,128)S(1)}, f32[4,2,64,128]{3,2,1,0:T(8,128)S(1)}, u32[]{:S(2)}, u32[]{:S(2)}) collective-permute-start(f32[4,2,64,128]{3,2,1,0:T(8,128)S(1)} %get-tuple-element.27), channel_id=1, source_target_pairs={{0,28},{4,0},{8,4},{12,8},{16,12},{20,16},{24,20},{28,24},{1,29},{... | collective-permute-start | bytes 786440 | tf_op jit(solution)/shard_map/ppermute | solution.py:225
  42.7 21.1 %all-to-all-start.4 = ((f32[4,32,8,128]{3,2,1,0:T(8,128)}), f32[4,32,8,128]{3,2,1,0:T(8,128)}, u32[]{:S(2)}, u32[]{:S(2)}) async-start(f32[4,32,8,128]{3,2,1,0:T(8,128)} %project0.1), calls=%async_computation.4 | async-start | bytes 1048576 | tf_op jit(solution)/shard_map/all_to_all | solution.py:342
  47.1 12.1 %collective-permute-start = (f32[4,2,64,128]{3,2,1,0:T(8,128)S(1)}, f32[4,2,64,128]{3,2,1,0:T(8,128)S(1)}, u32[]{:S(2)}, u32[]{:S(2)}) collective-permute-start(f32[4,2,64,128]{3,2,1,0:T(8,128)S(1)} %get-tuple-element.17), channel_id=1, source_target_pairs={{0,4},{4,8},{8,12},{12,16},{16,20},{20,24},{24,28},{28,0},{1,5},{5... | collective-permute-start | bytes 786440 | tf_op jit(solution)/shard_map/ppermute | solution.py:225
  47.2 15.2 %collective-permute-start.1 = (f32[4,2,64,128]{3,2,1,0:T(8,128)S(1)}, f32[4,2,64,128]{3,2,1,0:T(8,128)S(1)}, u32[]{:S(2)}, u32[]{:S(2)}) collective-permute-start(f32[4,2,64,128]{3,2,1,0:T(8,128)S(1)} %get-tuple-element.18), channel_id=1, source_target_pairs={{0,28},{4,0},{8,4},{12,8},{16,12},{20,16},{24,20},{28,24},{1,29},{... | collective-permute-start | bytes 786440 | tf_op jit(solution)/shard_map/ppermute | solution.py:225
  63.8 28.5 %all-to-all-start = ((f32[4,32,8,128]{3,2,1,0:T(8,128)}), f32[4,32,8,128]{3,2,1,0:T(8,128)S(1)}, u32[]{:S(2)}, u32[]{:S(2)}) async-start(f32[4,32,8,128]{3,2,1,0:T(8,128)} %project2.1), calls=%async_computation | async-start | bytes 1048576 | tf_op jit(solution)/shard_map/all_to_all | solution.py:342
  67.3 6.4 %collective-permute-start.2 = (f32[24,128]{1,0:T(8,128)S(1)}, f32[24,128]{1,0:T(8,128)S(1)}, u32[]{:S(2)}, u32[]{:S(2)}) collective-permute-start(f32[24,128]{1,0:T(8,128)S(1)} %constant_dynamic-update-slice_fusion), channel_id=1, source_target_pairs={{0,4},{4,8},{8,12},{12,16},{16,20},{20,24},{24,28},{28,0},{1,5},{5... | collective-permute-start | bytes 36872 | tf_op jit(solution)/shard_map/ppermute | solution.py:225
  73.7 5.6 %collective-permute-start.3 = (f32[24,128]{1,0:T(8,128)S(1)}, f32[24,128]{1,0:T(8,128)S(1)}, u32[]{:S(2)}, u32[]{:S(2)}) collective-permute-start(f32[24,128]{1,0:T(8,128)S(1)} %add.21), channel_id=1, source_target_pairs={{0,8},{4,12},{8,16},{12,20},{16,24},{20,28},{24,0},{28,4},{1,9},{5... | collective-permute-start | bytes 36872 | tf_op jit(solution)/shard_map/ppermute | solution.py:225
  79.3 4.6 %collective-permute-start.4 = (f32[24,128]{1,0:T(8,128)S(1)}, f32[24,128]{1,0:T(8,128)S(1)}, u32[]{:S(2)}, u32[]{:S(2)}) collective-permute-start(f32[24,128]{1,0:T(8,128)S(1)} %add.22), channel_id=1, source_target_pairs={{0,16},{4,20},{8,24},{12,28},{16,0},{20,4},{24,8},{28,12},{1,17},{... | collective-permute-start | bytes 36872 | tf_op jit(solution)/shard_map/ppermute | solution.py:225
  79.3 3.4 %copy-start.2 = (f32[32,256,256]{2,1,0:T(8,128)S(1)}, f32[32,256,256]{2,1,0:T(8,128)}, u32[]{:S(2)}) copy-start(f32[32,256,256]{2,1,0:T(8,128)} %inverse_ref.1) | copy-start | bytes 25165828
  82.7 1.2 copy-start.15
  88.3 2.0 %copy-start.9 = (bf16[32,256,256]{2,1,0:T(8,128)(2,1)}, bf16[32,256,256]{2,1,0:T(8,128)(2,1)S(1)}, u32[]{:S(2)}) copy-start(bf16[32,256,256]{2,1,0:T(8,128)(2,1)S(1)} %get-tuple-element.19.high_ref) | copy-start | bytes 12582916
  90.3 2.0 %copy-start.12 = (bf16[32,256,256]{2,1,0:T(8,128)(2,1)}, bf16[32,256,256]{2,1,0:T(8,128)(2,1)S(1)}, u32[]{:S(2)}) copy-start(bf16[32,256,256]{2,1,0:T(8,128)(2,1)S(1)} %get-tuple-element.20.low_ref) | copy-start | bytes 12582916
  92.4 12.6 %all-to-all-start.5 = ((f32[4,34,8,128]{3,2,1,0:T(8,128)}), f32[4,34,8,128]{3,2,1,0:T(8,128)S(1)}, u32[]{:S(2)}, u32[]{:S(2)}) async-start(f32[4,34,8,128]{3,2,1,0:T(8,128)} %solve0.1), calls=%async_computation.5 | async-start | bytes 1114112 | tf_op jit(solution)/shard_map/all_to_all | solution.py:359
  95.8 2.2 %copy-start.10 = (bf16[32,256,256]{2,1,0:T(8,128)(2,1)S(1)}, bf16[32,256,256]{2,1,0:T(8,128)(2,1)}, u32[]{:S(2)}) copy-start(bf16[32,256,256]{2,1,0:T(8,128)(2,1)} %copy-done.9) | copy-start | bytes 12582916
  98.0 2.2 %copy-start.13 = (bf16[32,256,256]{2,1,0:T(8,128)(2,1)S(1)}, bf16[32,256,256]{2,1,0:T(8,128)(2,1)}, u32[]{:S(2)}) copy-start(bf16[32,256,256]{2,1,0:T(8,128)(2,1)} %copy-done.12) | copy-start | bytes 12582916
  105.0 12.6 %all-to-all-start.3 = ((f32[4,34,8,128]{3,2,1,0:T(8,128)}), f32[4,34,8,128]{3,2,1,0:T(8,128)S(1)}, u32[]{:S(2)}, u32[]{:S(2)}) async-start(f32[4,34,8,128]{3,2,1,0:T(8,128)} %solve1.1), calls=%async_computation.3 | async-start | bytes 1114112 | tf_op jit(solution)/shard_map/all_to_all | solution.py:359
  108.4 2.2 %copy-start.11 = (bf16[32,256,256]{2,1,0:T(8,128)(2,1)S(1)}, bf16[32,256,256]{2,1,0:T(8,128)(2,1)}, u32[]{:S(2)}) copy-start(bf16[32,256,256]{2,1,0:T(8,128)(2,1)} %copy-done.9) | copy-start | bytes 12582916
  110.6 2.2 %copy-start.14 = (bf16[32,256,256]{2,1,0:T(8,128)(2,1)S(1)}, bf16[32,256,256]{2,1,0:T(8,128)(2,1)}, u32[]{:S(2)}) copy-start(bf16[32,256,256]{2,1,0:T(8,128)(2,1)} %copy-done.12) | copy-start | bytes 12582916
  112.8 8.2 %copy-start.7 = (bf16[128,128]{1,0:T(8,128)(2,1)S(1)}, bf16[128,128]{1,0:T(8,128)(2,1)}, u32[]{:S(2)}) copy-start(bf16[128,128]{1,0:T(8,128)(2,1)} %constant.21.clone.low_ref) | copy-start | bytes 98308
  112.8 8.2 %copy-start.8 = (bf16[128,128]{1,0:T(8,128)(2,1)S(1)}, bf16[128,128]{1,0:T(8,128)(2,1)}, u32[]{:S(2)}) copy-start(bf16[128,128]{1,0:T(8,128)(2,1)} %constant.20.clone.high_ref) | copy-start | bytes 98308
  117.6 12.6 %all-to-all-start.1 = ((f32[4,34,8,128]{3,2,1,0:T(8,128)}), f32[4,34,8,128]{3,2,1,0:T(8,128)S(1)}, u32[]{:S(2)}, u32[]{:S(2)}) async-start(f32[4,34,8,128]{3,2,1,0:T(8,128)} %solve2.1), calls=%async_computation.1 | async-start | bytes 1114112 | tf_op jit(solution)/shard_map/all_to_all | solution.py:359

commit v2 on v1

--- a/solution.py
+++ b/solution.py
@@ -8,6 +8,7 @@
 from jax.experimental.pallas import tpu as pltpu
 from jax.sharding import PartitionSpec as P
 
+
 MODES = 128
 HALO = 64
 
@@ -20,6 +21,7 @@
 LANES = 128
 MIB = 1 << 20
 GROUP = 4
+VMEM = pl.BlockSpec(memory_space=pltpu.VMEM)
 NT = (((1,), (1,)), ((), ()))
 NN = (((1,), (0,)), ((), ()))
 
@@ -95,15 +97,15 @@
     return pltpu.roll(x, LANES // 2, len(x.shape) - 1)
 
 
-def pack_kernel(state_ref, last_ref, first_ref, sums_ref):
+def pack_kernel(base, state_ref, last_ref, first_ref, sums_ref):
     rows = state_ref.shape[2]
     left = left_lanes((rows, LANES))
     totals = []
     for e in range(GROUP):
         acc = jnp.zeros((rows, LANES), jnp.float32)
         for p in range(2):
-            a = state_ref[e, p]
-            b = state_ref[e, p + 2]
+            a = state_ref[base + e, p]
+            b = state_ref[base + e, p + 2]
             acc += a * a + b * b
             last_ref[e, p] = jnp.where(left, swap(a), b)
             first_ref[e, p] = jnp.where(left, a, swap(b))
@@ -113,50 +115,81 @@
         sums_ref[4 * q : 4 * q + 4] = jnp.where(half, totals[2 * q], totals[2 * q + 1])
 
 
+def peers(parts):
+    me = lax.axis_index("gy")
+    return [jnp.bitwise_xor(me, d) for d in range(parts)]
+
+
+def reorder_lanes(x):
+    me = lax.axis_index("gy")
+    far = jnp.bitwise_and(me, 2) != 0
+    near = jnp.bitwise_and(me, 1) != 0
+    a, b = x[..., :LANES], x[..., LANES:]
+    a, b = jnp.where(far, b, a), jnp.where(far, a, b)
+    return jnp.where(near, swap(a), a), jnp.where(near, swap(b), b)
+
+
 def split_kernel(inverse_ref, high_ref, low_ref):
-    high_ref[...], low_ref[...] = split(inverse_ref[...])
-
-
-def project_kernel(state_ref, before_ref, after_ref, high_ref, low_ref, mask_ref, out_ref):
-    parts, slots, rows, _ = out_ref.shape
+    coef_count = inverse_ref.shape[1]
+    coef = LANES // 2
+    for d, peer in enumerate(peers(coef_count // coef)):
+        rows = pl.ds(pl.multiple_of(peer * coef, coef), coef)
+        for h, x in enumerate(reorder_lanes(inverse_ref[:, rows, :])):
+            at = (slice(None), slice(d * coef, (d + 1) * coef), slice(h * LANES, (h + 1) * LANES))
+            high_ref[at], low_ref[at] = split(x)
+
+
+def project_kernel(base, state_ref, before_ref, after_ref, high_ref, low_ref, mask_ref, *out_refs):
+    parts = len(out_refs)
+    slots, rows, _ = out_refs[0].shape
     coef = state_ref.shape[2]
     count = slots * parts
-    flat = out_ref.reshape(parts * slots * rows, LANES)
     mask = mask_ref[...]
+    where = [pl.multiple_of(peer * slots, slots) for peer in peers(parts)]
     for p in range(2):
         x = jnp.concatenate(
             [
-                state_ref[:, p].reshape(GROUP * coef, LANES),
-                state_ref[:, p + 2].reshape(GROUP * coef, LANES),
+                state_ref[base : base + GROUP, p].reshape(GROUP * coef, LANES),
+                state_ref[base : base + GROUP, p + 2].reshape(GROUP * coef, LANES),
                 before_ref[:, p].reshape(GROUP * coef, LANES),
                 after_ref[:, p].reshape(GROUP * coef, LANES),
             ],
             axis=1,
         )
         x_high, x_low = split(x)
-        w_high = high_ref[p]
-        w_low = low_ref[p]
+        w_high, w_low = [
+            jnp.concatenate(
+                [ref[p, pl.ds(f * count + at, slots), :] for f in range(2) for at in where], axis=0
+            )
+            for ref in (high_ref, low_ref)
+        ]
         t = dot(w_high, x_high, NT) + (dot(w_high, x_low, NT) + dot(w_low, x_high, NT))
         t = t * mask
-        for f in range(2):
-            for q in range(GROUP // 2):
-                row = 4 * q + p + 2 * f
-                flat[pl.ds(row, count, stride=rows), :] = t[
-                    f * count : (f + 1) * count, q * LANES : (q + 1) * LANES
-                ]
-
-
-def solve_kernel(recv_ref, high_ref, low_ref, wall_ref, sums_ref, out_ref):
-    parts, slots, rows, _ = recv_ref.shape
+        for d in range(parts):
+            flat = out_refs[d].reshape(slots * rows, LANES)
+            for f in range(2):
+                first = f * count + d * slots
+                for q in range(GROUP // 2):
+                    flat[pl.ds(4 * q + p + 2 * f, slots, stride=rows), :] = t[
+                        first : first + slots, q * LANES : (q + 1) * LANES
+                    ]
+
+
+def solve_kernel(base, parts, *refs):
+    recv_refs = refs[:parts]
+    high_ref, low_ref, wall_ref, sums_ref = refs[parts : parts + 4]
+    out_refs = refs[parts + 4 :]
+    slots, rows, _ = recv_refs[0].shape
     left = left_lanes((rows, LANES))
     lane = lax.broadcasted_iota(jnp.int32, (rows, LANES), 1)
+    wall = jnp.concatenate(reorder_lanes(wall_ref[...]), axis=1)
     sums = jnp.zeros((rows, LANES), jnp.float32)
     for m in range(slots):
-        t = [recv_ref[s, m] for s in range(parts)]
+        t = [ref[m] for ref in recv_refs]
         even, odd = [], []
-        for s in range(0, parts, 2):
-            even.append(jnp.where(left, t[s], swap(t[s + 1])))
-            odd.append(jnp.where(left, swap(t[s]), t[s + 1]))
+        for d in range(0, parts, 2):
+            even.append(jnp.where(left, t[d], swap(t[d + 1])))
+            odd.append(jnp.where(left, swap(t[d]), t[d + 1]))
         r = jnp.concatenate(
             [jnp.concatenate(even, axis=1), jnp.concatenate(odd, axis=1)], axis=0
         )
@@ -165,37 +198,47 @@
         v_low = low_ref[m]
         both = dot(jnp.concatenate([r_high, r_low], axis=0), v_high, NT)
         o = both[: 2 * rows] + (both[2 * rows :] + dot(r_high, v_low, NT))
-        for s in range(0, parts, 2):
-            a = o[:rows, s * 64 : s * 64 + LANES]
-            b = o[rows:, s * 64 : s * 64 + LANES]
-            out_ref[s, m] = jnp.where(left, a, swap(b))
-            out_ref[s + 1, m] = jnp.where(left, swap(a), b)
+        for d in range(0, parts, 2):
+            a = o[:rows, d * 64 : d * 64 + LANES]
+            b = o[rows:, d * 64 : d * 64 + LANES]
+            out_refs[d][m] = jnp.where(left, a, swap(b))
+            out_refs[d + 1][m] = jnp.where(left, swap(a), b)
         for w in range(2):
-            q = jnp.sum(o * wall_ref[w : w + 1, :], axis=1, keepdims=True)
+            q = jnp.sum(o * wall[w : w + 1], axis=1, keepdims=True)
             for e in range(2):
                 at = e * 2 * slots + w * slots + m
                 sums = jnp.where(lane == at, q[e * rows : (e + 1) * rows], sums)
-    for k in range(parts):
-        out_ref[k, slots] = sums
-        out_ref[k, slots + 1] = sums_ref[...]
-
-
-def back_kernel(total, recv_ref, high_ref, low_ref, *refs):
+    for ref in out_refs:
+        ref[slots] = sums
+        ref[slots + 1] = sums_ref[base : base + rows]
+
+
+def back_kernel(total, parts, *refs):
+    recv_refs = refs[:parts]
+    high_ref, low_ref = refs[parts : parts + 2]
     out_ref, wall_ref = refs[-2:]
-    parts, slots, rows, _ = recv_ref.shape
+    slots, rows, _ = recv_refs[0].shape
     coef = out_ref.shape[2]
     width = slots - 2
-    flat = recv_ref.reshape(parts * slots * rows, LANES)
-    b_high = high_ref[...]
-    b_low = low_ref[...]
-    n = recv_ref[0, slots - 1]
-    for k in range(1, parts):
-        n = n + recv_ref[k, slots - 1]
-    scale = lax.rsqrt(n / total + EPSILON)
+    where = [pl.multiple_of(peer * width, width) for peer in peers(parts)]
+    b_high, b_low = [
+        jnp.concatenate([ref[pl.ds(at, width), :] for at in where], axis=0)
+        for ref in (high_ref, low_ref)
+    ]
+    n = [ref[slots - 1] for ref in recv_refs]
+    me = lax.axis_index("gy")
+    near = jnp.bitwise_and(me, 1) != 0
+    far = jnp.bitwise_and(me, 2) != 0
+    n = [jnp.where(near, n[d ^ 1], n[d]) for d in range(parts)]
+    n = [jnp.where(far, n[d ^ 2], n[d]) for d in range(parts)]
+    scale = lax.rsqrt(sum(n[1:], n[0]) / total + EPSILON)
     for r in range(rows):
         q, f = r // 4, r % 4
         s = jnp.concatenate(
-            [flat[pl.ds(k * slots * rows + r, width, stride=rows), :] for k in range(parts)],
+            [
+                ref.reshape(slots * rows, LANES)[pl.ds(r, width, stride=rows), :]
+                for ref in recv_refs
+            ],
             axis=0,
         )
         s = (s * scale[r : r + 1]).T
@@ -204,7 +247,11 @@
         for e in range(2):
             out_ref[2 * q + e, f] = o[e * coef : (e + 1) * coef]
     lane = lax.broadcasted_iota(jnp.int32, (rows, LANES), 1)
-    tiles = [recv_ref[k, slots - 2] * scale for k in range(parts)]
+    tiles = [ref[slots - 2] for ref in recv_refs]
+    tiles = [jnp.where(near, tiles[d ^ 1], tiles[d]) for d in range(parts)]
+    tiles = [jnp.where(far, tiles[d ^ 2], tiles[d]) * scale for d in range(parts)]
+    b_high = high_ref[...]
+    b_low = low_ref[...]
     for e in range(2):
         for w in range(2):
             g = jnp.zeros((rows, LANES), jnp.float32)
@@ -225,19 +272,24 @@
     return lax.ppermute(x, axis, [(i, (i + by) % n) for i in range(n)])
 
 
+def exchanged(pieces, axis):
+    n = lax.axis_size(axis)
+    got = list(pieces)
+    for d in range(n - 1, 0, -1):
+        got[d] = lax.ppermute(pieces[d], axis, [(i, i ^ d) for i in range(n)])
+    return got
+
+
 def ring_sum(x, axis):
     n = lax.axis_size(axis)
     if n & (n - 1):
         return lax.psum(x, axis)
     hop = 1
     while hop < n:
-        x = x + shifted(x, axis, hop)
+        other = shifted(x, axis, hop)
+        x = x + other
         hop *= 2
     return x
-
-
-def whole(shape):
-    return pl.BlockSpec(shape, lambda *_: (0,) * len(shape))
 
 
 def per_device(state, inverse):
@@ -267,11 +319,9 @@
     def grouped(g, shape):
         return pl.BlockSpec((GROUP,) + shape, lambda i: (g,) + (0,) * len(shape))
 
-    def call(kernel, name, vmem, flops, moved, **kwargs):
+    def call(kernel, vmem, flops, moved, **kwargs):
         return pl.pallas_call(
             kernel,
-            grid=(1,),
-            name=name,
             compiler_params=pltpu.CompilerParams(vmem_limit_bytes=vmem * MIB),
             cost_estimate=pl.CostEstimate(flops=flops, bytes_accessed=moved, transcendentals=0),
             **kwargs,
@@ -281,20 +331,19 @@
     halo = (GROUP, 2, coef, LANES)
     halo_bytes = 4 * int(np.prod(halo))
     small = (group_rows, LANES)
-    sent_shape = (parts, mine, group_rows, LANES)
-    back_shape = (parts, mine + 2, group_rows, LANES)
+    sent_shape = (mine, group_rows, LANES)
+    back_shape = (mine + 2, group_rows, LANES)
 
     packed = []
     for g in range(groups):
         packed.append(
             call(
-                pack_kernel,
-                f"pack{g}",
+                functools.partial(pack_kernel, g * GROUP),
                 6,
                 10**6,
                 4 * halo_bytes,
-                in_specs=[grouped(g, block)],
-                out_specs=[whole(halo), whole(halo), whole(small)],
+                in_specs=[VMEM],
+                out_specs=[VMEM] * 3,
                 out_shape=[
                     jax.ShapeDtypeStruct(halo, jnp.float32),
                     jax.ShapeDtypeStruct(halo, jnp.float32),
@@ -302,7 +351,11 @@
                 ],
             )(state)
         )
-    halos = [(shifted(p[0], "gx", 1), shifted(p[1], "gx", -1)) for p in packed]
+    halos = []
+    for last, first, _ in packed:
+        before = shifted(last, "gx", 1)
+        after = shifted(first, "gx", -1)
+        halos.append((before, after))
     sums = ring_sum(jnp.concatenate([p[2] for p in packed], axis=0), "gx")
 
     per_step = 4
@@ -323,60 +376,46 @@
     outputs = []
     for g in range(groups):
         sent = call(
-            project_kernel,
-            f"project{g}",
+            functools.partial(project_kernel, g * GROUP),
             8,
             2 * 3 * 2 * 256 * 512 * GROUP * coef,
             6 * halo_bytes,
-            in_specs=[
-                grouped(g, block),
-                whole(halo),
-                whole(halo),
-                whole(step_high.shape),
-                whole(step_low.shape),
-                whole(mask.shape),
-            ],
-            out_specs=whole(sent_shape),
-            out_shape=jax.ShapeDtypeStruct(sent_shape, jnp.float32),
+            in_specs=[VMEM] * 6,
+            out_specs=[VMEM] * parts,
+            out_shape=[jax.ShapeDtypeStruct(sent_shape, jnp.float32)] * parts,
         )(state, *halos[g], step_high, step_low, mask)
-        got = lax.all_to_all(sent, "gy", split_axis=0, concat_axis=0, tiled=True)
+        got = exchanged(sent, "gy")
         solved = call(
-            solve_kernel,
-            f"solve{g}",
+            functools.partial(solve_kernel, g * group_rows, parts),
             24,
             2 * 3 * mine * coef_count**2 * 256,
             4 * mine * coef_count**2,
-            in_specs=[
-                whole(sent_shape),
-                whole(inverse.shape),
-                whole(inverse.shape),
-                whole(wall.shape),
-                pl.BlockSpec(small, lambda i: (g, 0)),
-            ],
-            out_specs=whole(back_shape),
-            out_shape=jax.ShapeDtypeStruct(back_shape, jnp.float32),
-        )(got, inverse_high, inverse_low, wall, sums)
-        returned = lax.all_to_all(solved, "gy", split_axis=0, concat_axis=0, tiled=True)
+            in_specs=[VMEM] * (parts + 4),
+            out_specs=[VMEM] * parts,
+            out_shape=[jax.ShapeDtypeStruct(back_shape, jnp.float32)] * parts,
+        )(*got, inverse_high, inverse_low, wall, sums)
+        returned = exchanged(solved, "gy")
         outputs = call(
-            functools.partial(back_kernel, float(fields * coef_count * grid_x)),
-            f"back{g}",
+            functools.partial(back_kernel, float(fields * coef_count * grid_x), parts),
             8,
             2 * 3 * 128 * 128 * GROUP * fields * coef,
             4 * halo_bytes,
-            in_specs=[whole(back_shape), whole(back_high.shape), whole(back_low.shape)]
+            grid=(1,),
+            in_specs=[VMEM] * (parts + 2)
             + [pl.BlockSpec(memory_space=pl.ANY)] * len(outputs),
             out_specs=[grouped(g, block), grouped(g, (2, 2, points))],
             out_shape=[
                 jax.ShapeDtypeStruct(state.shape, jnp.float32),
                 jax.ShapeDtypeStruct((members, 2, 2, points), jnp.float32),
             ],
-            input_output_aliases={3 + i: i for i in range(len(outputs))},
-        )(returned, back_high, back_low, *outputs)
+            input_output_aliases={parts + 2 + i: i for i in range(len(outputs))},
+        )(*returned, back_high, back_low, *outputs)
     return tuple(outputs)
 
 
 def solution(mesh):
     placed = (P(None, None, "gy", "gx"), P("gy", None, None))
+
     return jax.shard_map(
         per_device,
         mesh=mesh,

time: 132 us -> 87.7 us (0.66)
  waiting for transfers between devices: 52.4 us -> 27.3 us
  local copies, waits for them, and re-layouts: 19.7 us -> 6.56 us
  starting transfers between devices: 37.4 us -> 31.5 us
    ppermute x9, waiting for transfers between devices: 42.9 us -> 19 us  [shifted(): return lax.ppermute(x, axis, [(i, (i + by) % n) for i in range(n)])]
    all_to_all x6 -> x0, starting transfers between devices: 21.6 us -> none  [the longest x3 11.2 us: per_device(): got = lax.all_to_all(sent, 'gy', split_axis=0, concat_axis=0, tiled=True)]
    ppermute x0 -> x18, starting transfers between devices: none -> 14.4 us  [exchanged(): got[d] = lax.ppermute(pieces[d], axis, [(i, i ^ d) for i in range(n)])]
    unnamed x34 -> x22, local copies, waits for them, and re-layouts: 19.6 us -> 6.47 us
    all_to_all x6 -> x0, waiting for transfers between devices: 9.54 us -> none  [the longest x3 9.53 us: per_device(): lax.all_to_all(solved, 'gy', split_axis=0, concat_axis=0, tiled=True)]
    ppermute x0 -> x18, waiting for transfers between devices: none -> 8.37 us  [exchanged(): got[d] = lax.ppermute(pieces[d], axis, [(i, i ^ d) for i in range(n)])]
    pallas_call x1, Pallas kernels: 1.19 us -> 2.91 us  [per_device(): pl.pallas_call(split_kernel, grid=(mine // per_step,), in_specs=[pl.Block...]
    pallas_call x12, Pallas kernels: 19.9 us -> 18.2 us  [the longest x3 7.45 us: per_device(): call(functools.partial(solve_kernel, g * group_rows, parts), 24, 2 * 3 *...]
  transfers between devices with their start and end apart: 15 -> 27, of which waited for: 11 -> 8; matrix products, arithmetic and copies ran while one was open for 0% -> 0% of each run, Pallas kernels for 14% -> 22%
where the time goes in v2:
time: 87.7 us; the launch traced here: 87.4 us
  starting transfers between devices  31.5 us (36%)
  waiting for transfers between devices  27.3 us (31%)
  Pallas kernels  21.1 us (24%)
  local copies, waits for them, and re-layouts  6.56 us (7%)
    ppermute x9, waiting for transfers between devices, shifted(): return lax.ppermute(x, axis, [(i, (i + by) % n) for i in range(n)])  19 us
    ppermute x9, starting transfers between devices, shifted(): return lax.ppermute(x, axis, [(i, (i + by) % n) for i in range(n)])  17.1 us
    ppermute x18, starting transfers between devices, exchanged(): got[d] = lax.ppermute(pieces[d], axis, [(i, i ^ d) for i in range(n)])  14.4 us
    ppermute x18, waiting for transfers between devices, exchanged(): got[d] = lax.ppermute(pieces[d], axis, [(i, i ^ d) for i in range(n)])  8.37 us
    pallas_call x3, Pallas kernels, per_device(): call(functools.partial(solve_kernel, g * group_rows, parts), 24, 2 * 3 *...  7.45 us
    unnamed x22, local copies, waits for them, and re-layouts  6.47 us
    pallas_call x3, Pallas kernels, per_device(): call(functools.partial(project_kernel, g * GROUP), 8, 2 * 3 * 2 * 256 * 5...  3.82 us
    pallas_call x3, Pallas kernels, per_device(): call(functools.partial(back_kernel, float(fields * coef_count * grid_x),...  3.79 us
  transfers between devices with their start and end apart: 27, of which 8 were waited for; matrix products, arithmetic and copies ran while one was open for 0% of the time, Pallas kernels for 22%

profile of v2, /device:TPU:0, one launch (start us, length us, event | category | flops | bytes accessed | tf_op | source)
XLA Modules:
  0.0 87.4 jit_solution(6776534623647171788)
XLA Ops:
  0.6 0.0 copy-start
  0.6 1.4 %copy-done = f32[12,4,64,128]{3,2,1,0:T(8,128)S(1)} copy-done((f32[12,4,64,128]{3,2,1,0:T(8,128)S(1)}, f32[12,4,64,128]{3,2,1,0:T(8,128)}, u32[]{:S(2)}) %copy-start) | copy-done | bytes 1572888
  2.0 1.1 %shard_map.86 = (f32[4,2,64,128]{3,2,1,0:T(8,128)}, f32[4,2,64,128]{3,2,1,0:T(8,128)}, f32[8,128]{1,0:T(8,128)S(1)}) custom-call(f32[12,4,64,128]{3,2,1,0:T(8,128)S(1)} %copy-done), custom_call_target="tpu_custom_call" | custom-call | flops 1000000 | bytes 1048576 | tf_op jit(solution)/shard_map/pallas_call | solution.py:340
  3.1 3.0 %collective-permute-start = (f32[4,2,64,128]{3,2,1,0:T(8,128)}, f32[4,2,64,128]{3,2,1,0:T(8,128)S(1)}, u32[]{:S(2)}, u32[]{:S(2)}) collective-permute-start(f32[4,2,64,128]{3,2,1,0:T(8,128)} %get-tuple-element.41), channel_id=1, source_target_pairs={{0,4},{4,8},{8,12},{12,16},{16,20},{20,24},{24,28},{28,0},{1,5},{5... | collective-permute-start | bytes 786440 | tf_op jit(solution)/shard_map/ppermute | solution.py:272
  6.1 3.1 %collective-permute-start.1 = (f32[4,2,64,128]{3,2,1,0:T(8,128)}, f32[4,2,64,128]{3,2,1,0:T(8,128)S(1)}, u32[]{:S(2)}, u32[]{:S(2)}) collective-permute-start(f32[4,2,64,128]{3,2,1,0:T(8,128)} %get-tuple-element.42), channel_id=1, source_target_pairs={{0,28},{4,0},{8,4},{12,8},{16,12},{20,16},{24,20},{28,24},{1,29},{... | collective-permute-start | bytes 786440 | tf_op jit(solution)/shard_map/ppermute | solution.py:272
  9.2 1.0 %shard_map.89 = (f32[4,2,64,128]{3,2,1,0:T(8,128)S(1)}, f32[4,2,64,128]{3,2,1,0:T(8,128)}, f32[8,128]{1,0:T(8,128)S(1)}) custom-call(f32[12,4,64,128]{3,2,1,0:T(8,128)S(1)} %copy-done), custom_call_target="tpu_custom_call" | custom-call | flops 1000000 | bytes 1048576 | tf_op jit(solution)/shard_map/pallas_call | solution.py:340
  10.2 0.0 collective-permute-start.11
  10.2 4.7 %collective-permute-start.12 = (f32[4,2,64,128]{3,2,1,0:T(8,128)}, f32[4,2,64,128]{3,2,1,0:T(8,128)}, u32[]{:S(2)}, u32[]{:S(2)}) collective-permute-start(f32[4,2,64,128]{3,2,1,0:T(8,128)} %get-tuple-element.57), channel_id=1, source_target_pairs={{0,28},{4,0},{8,4},{12,8},{16,12},{20,16},{24,20},{28,24},{1,29},{... | collective-permute-start | bytes 786440 | tf_op jit(solution)/shard_map/ppermute | solution.py:272
  14.9 1.1 %shard_map.88 = (f32[4,2,64,128]{3,2,1,0:T(8,128)}, f32[4,2,64,128]{3,2,1,0:T(8,128)}, f32[8,128]{1,0:T(8,128)S(1)}) custom-call(f32[12,4,64,128]{3,2,1,0:T(8,128)S(1)} %copy-done), custom_call_target="tpu_custom_call" | custom-call | flops 1000000 | bytes 1048576 | tf_op jit(solution)/shard_map/pallas_call | solution.py:340
  16.0 0.0 collective-permute-start.5
  16.0 13.0 %collective-permute-done.5 = f32[24,128]{1,0:T(8,128)S(1)} collective-permute-done((f32[24,128]{1,0:T(8,128)S(1)}, f32[24,128]{1,0:T(8,128)S(1)}, u32[]{:S(2)}, u32[]{:S(2)}) %collective-permute-start.5) | collective-permute-done | bytes 12320 | tf_op jit(solution)/shard_map/ppermute | solution.py:272
  29.0 1.6 %collective-permute-start.6 = (f32[24,128]{1,0:T(8,128)S(1)}, f32[24,128]{1,0:T(8,128)S(1)}, u32[]{:S(2)}, u32[]{:S(2)}) collective-permute-start(f32[24,128]{1,0:T(8,128)S(1)} %add.21), channel_id=1, source_target_pairs={{0,8},{4,12},{8,16},{12,20},{16,24},{20,28},{24,0},{28,4},{1,9},{5... | collective-permute-start | bytes 36872 | tf_op jit(solution)/shard_map/ppermute | solution.py:272
  30.5 3.9 %collective-permute-done.6 = f32[24,128]{1,0:T(8,128)S(1)} collective-permute-done((f32[24,128]{1,0:T(8,128)S(1)}, f32[24,128]{1,0:T(8,128)S(1)}, u32[]{:S(2)}, u32[]{:S(2)}) %collective-permute-start.6) | collective-permute-done | bytes 12320 | tf_op jit(solution)/shard_map/ppermute | solution.py:272
  34.5 2.5 %collective-permute-start.19 = (f32[4,2,64,128]{3,2,1,0:T(8,128)}, f32[4,2,64,128]{3,2,1,0:T(8,128)S(1)}, u32[]{:S(2)}, u32[]{:S(2)}) collective-permute-start(f32[4,2,64,128]{3,2,1,0:T(8,128)} %get-tuple-element.66), channel_id=1, source_target_pairs={{0,4},{4,8},{8,12},{12,16},{16,20},{20,24},{24,28},{28,0},{1,5},{5... | collective-permute-start | bytes 786440 | tf_op jit(solution)/shard_map/ppermute | solution.py:272
  36.9 0.7 copy-done.7
  37.7 2.2 %collective-permute-start.20 = (f32[4,2,64,128]{3,2,1,0:T(8,128)}, f32[4,2,64,128]{3,2,1,0:T(8,128)}, u32[]{:S(2)}, u32[]{:S(2)}) collective-permute-start(f32[4,2,64,128]{3,2,1,0:T(8,128)} %get-tuple-element.67), channel_id=1, source_target_pairs={{0,28},{4,0},{8,4},{12,8},{16,12},{20,16},{24,20},{28,24},{1,29},{... | collective-permute-start | bytes 786440 | tf_op jit(solution)/shard_map/ppermute | solution.py:272
  39.9 0.1 broadcast_in_dim_tile.3.mask_ref
  40.0 0.0 collective-permute-done.12.after_ref
  40.0 0.0 collective-permute-start.7
  40.1 0.9 %copy-done.8 = f32[4,2,64,128]{3,2,1,0:T(8,128)S(1)} copy-done((f32[4,2,64,128]{3,2,1,0:T(8,128)S(1)}, f32[4,2,64,128]{3,2,1,0:T(8,128)}, u32[]{:S(2)}) %copy-start.8) | copy-done | bytes 262168
  41.0 1.6 %shard_map.91 = (f32[32,8,128]{2,1,0:T(8,128)S(1)}, f32[32,8,128]{2,1,0:T(8,128)S(1)}, f32[32,8,128]{2,1,0:T(8,128)S(1)}, f32[32,8,128]{2,1,0:T(8,128)S(1)}) custom-call(f32[12,4,64,128]{3,2,1,0:T(8,128)S(1)} %copy-done.1, f32[4,2,64,128]{3,2,1,0:T(8,128)S(1)} %copy-done.8, f32[4,2,64,128]{3,2,1,0:T(8,128)} %collective-permute-done.12.after_ref, ...), custom_call_target="tpu_custom_call" | custom-call | flops 402653184 | bytes 1572864 | tf_op jit(solution)/shard_map/pallas_call | solution.py:378
  42.6 2.1 %collective-permute-done.7 = f32[24,128]{1,0:T(8,128)S(1)} collective-permute-done((f32[24,128]{1,0:T(8,128)S(1)}, f32[24,128]{1,0:T(8,128)S(1)}, u32[]{:S(2)}, u32[]{:S(2)}) %collective-permute-start.7) | collective-permute-done | bytes 12320 | tf_op jit(solution)/shard_map/ppermute | solution.py:272
  44.7 0.0 collective-permute-start.13
  44.7 0.0 collective-permute-done.before_ref
  44.7 1.5 %collective-permute-start.14 = (f32[32,8,128]{2,1,0:T(8,128)S(1)}, f32[32,8,128]{2,1,0:T(8,128)S(1)}, u32[]{:S(2)}, u32[]{:S(2)}) collective-permute-start(f32[32,8,128]{2,1,0:T(8,128)S(1)} %get-tuple-element.60), channel_id=1, source_target_pairs={{0,2},{1,3},{2,0},{3,1},{4,6},{5,7},{6,4},{7,5},{8,10},{9,11},{10,... | collective-permute-start | bytes 393224 | tf_op jit(solution)/shard_map/ppermute | solution.py:279
  46.3 0.0 collective-permute-done.1.after_ref
  46.3 0.3 collective-permute-start.15
  46.6 3.4 %copy-done.2 = f32[32,256,256]{2,1,0:T(8,128)S(1)} copy-done((f32[32,256,256]{2,1,0:T(8,128)S(1)}, f32[32,256,256]{2,1,0:T(8,128)}, u32[]{:S(2)}) %copy-start.2) | copy-done | bytes 8388632
  50.0 2.9 %split.1 = (bf16[32,256,256]{2,1,0:T(8,128)(2,1)S(1)}, bf16[32,256,256]{2,1,0:T(8,128)(2,1)S(1)}) custom-call(f32[32,256,256]{2,1,0:T(8,128)S(1)} %copy-done.2), custom_call_target="tpu_custom_call" | custom-call | flops 10000000 | bytes 16777216 | tf_op jit(solution)/shard_map/split/pallas_call | solution.py:363
  52.9 0.6 shard_map.87
  53.6 0.0 collective-permute-done.19.before_ref
  53.6 0.3 collective-permute-start.2
  53.9 0.0 collective-permute-done.20.after_ref
  53.9 1.5 %collective-permute-start.3 = (f32[32,8,128]{2,1,0:T(8,128)S(1)}, f32[32,8,128]{2,1,0:T(8,128)S(1)}, u32[]{:S(2)}, u32[]{:S(2)}) collective-permute-start(f32[32,8,128]{2,1,0:T(8,128)S(1)} %get-tuple-element.45), channel_id=1, source_target_pairs={{0,2},{1,3},{2,0},{3,1},{4,6},{5,7},{6,4},{7,5},{8,10},{9,11},{10,... | collective-permute-start | bytes 393224 | tf_op jit(solution)/shard_map/ppermute | solution.py:279
  55.4 1.6 %shard_map.93 = (f32[32,8,128]{2,1,0:T(8,128)S(1)}, f32[32,8,128]{2,1,0:T(8,128)S(1)}, f32[32,8,128]{2,1,0:T(8,128)S(1)}, f32[32,8,128]{2,1,0:T(8,128)S(1)}) custom-call(f32[12,4,64,128]{3,2,1,0:T(8,128)S(1)} %copy-done.1, f32[4,2,64,128]{3,2,1,0:T(8,128)S(1)} %collective-permute-done.19.before_ref, f32[4,2,64,128]{3,2,1,0:T(8,128)} %collective-permute-done.20.after_ref, ...), custom_call_target="tpu_custom_call" | custom-call | flops 402653184 | bytes 1572864 | tf_op jit(solution)/shard_map/pallas_call | solution.py:378
  57.0 0.1 collective-permute-start.21
  57.1 0.6 collective-permute-start.22
  57.7 0.0 collective-permute-done.15.refs_3_
  57.7 1.3 %collective-permute-start.23 = (f32[32,8,128]{2,1,0:T(8,128)S(1)}, f32[32,8,128]{2,1,0:T(8,128)S(1)}, u32[]{:S(2)}, u32[]{:S(2)}) collective-permute-start(f32[32,8,128]{2,1,0:T(8,128)S(1)} %get-tuple-element.71), channel_id=1, source_target_pairs={{0,3},{1,2},{2,1},{3,0},{4,7},{5,6},{6,5},{7,4},{8,11},{9,10},{10,... | collective-permute-start | bytes 393224 | tf_op jit(solution)/shard_map/ppermute | solution.py:279
  59.0 2.5 %shard_map.92 = (f32[34,8,128]{2,1,0:T(8,128)S(1)}, f32[34,8,128]{2,1,0:T(8,128)S(1)}, f32[34,8,128]{2,1,0:T(8,128)S(1)}, f32[34,8,128]{2,1,0:T(8,128)S(1)}) custom-call(f32[32,8,128]{2,1,0:T(8,128)S(1)} %get-tuple-element.58.refs_0_, f32[32,8,128]{2,1,0:T(8,128)S(1)} %collective-permute-done.13.refs_1_, f32[32,8,128]{2,1,0:T(8,128)S(1)} %collective-permute-done.14.refs_2_, ...), custom_call_target="tpu_custom_call" | custom-call | flops 3221225472 | bytes 8388608 | tf_op jit(solution)/shard_map/pallas_call | solution.py:388
  61.5 0.5 collective-permute-start.4
  62.0 1.5 %collective-permute-done.22.refs_2_ = f32[32,8,128]{2,1,0:T(8,128)S(1)} collective-permute-done((f32[32,8,128]{2,1,0:T(8,128)S(1)}, f32[32,8,128]{2,1,0:T(8,128)S(1)}, u32[]{:S(2)}, u32[]{:S(2)}) %collective-permute-start.22) | collective-permute-done | bytes 131104 | tf_op jit(solution)/shard_map/ppermute | solution.py:279
  63.6 0.0 collective-permute-start.16
  63.6 1.7 %collective-permute-done.23.refs_3_ = f32[32,8,128]{2,1,0:T(8,128)S(1)} collective-permute-done((f32[32,8,128]{2,1,0:T(8,128)S(1)}, f32[32,8,128]{2,1,0:T(8,128)S(1)}, u32[]{:S(2)}, u32[]{:S(2)}) %collective-permute-start.23) | collective-permute-done | bytes 131104 | tf_op jit(solution)/shard_map/ppermute | solution.py:279
  65.3 1.1 %collective-permute-start.17 = (f32[34,8,128]{2,1,0:T(8,128)S(1)}, f32[34,8,128]{2,1,0:T(8,128)S(1)}, u32[]{:S(2)}, u32[]{:S(2)}) collective-permute-start(f32[34,8,128]{2,1,0:T(8,128)S(1)} %get-tuple-element.64), channel_id=1, source_target_pairs={{0,2},{1,3},{2,0},{3,1},{4,6},{5,7},{6,4},{7,5},{8,10},{9,11},{10,... | collective-permute-start | bytes 417800 | tf_op jit(solution)/shard_map/ppermute | solution.py:279
  66.3 2.5 %shard_map.94 = (f32[34,8,128]{2,1,0:T(8,128)S(1)}, f32[34,8,128]{2,1,0:T(8,128)S(1)}, f32[34,8,128]{2,1,0:T(8,128)S(1)}, f32[34,8,128]{2,1,0:T(8,128)S(1)}) custom-call(f32[32,8,128]{2,1,0:T(8,128)S(1)} %get-tuple-element.68.refs_0_, f32[32,8,128]{2,1,0:T(8,128)S(1)} %collective-permute-done.21.refs_1_, f32[32,8,128]{2,1,0:T(8,128)S(1)} %collective-permute-done.22.refs_2_, ...), custom_call_target="tpu_custom_call" | custom-call | flops 3221225472 | bytes 8388608 | tf_op jit(solution)/shard_map/pallas_call | solution.py:388
  68.8 0.0 collective-permute-done.2.refs_1_
  68.8 1.6 %collective-permute-start.18 = (f32[34,8,128]{2,1,0:T(8,128)S(1)}, f32[34,8,128]{2,1,0:T(8,128)S(1)}, u32[]{:S(2)}, u32[]{:S(2)}) collective-permute-start(f32[34,8,128]{2,1,0:T(8,128)S(1)} %get-tuple-element.65), channel_id=1, source_target_pairs={{0,3},{1,2},{2,1},{3,0},{4,7},{5,6},{6,5},{7,4},{8,11},{9,10},{10,... | collective-permute-start | bytes 417800 | tf_op jit(solution)/shard_map/ppermute | solution.py:279
  70.4 0.0 collective-permute-start.24
  70.4 0.0 collective-permute-done.4.refs_3_
  70.4 0.7 collective-permute-start.25
  71.1 0.0 collective-permute-done.16.refs_1_
  71.1 1.1 %collective-permute-start.26 = (f32[34,8,128]{2,1,0:T(8,128)S(1)}, f32[34,8,128]{2,1,0:T(8,128)S(1)}, u32[]{:S(2)}, u32[]{:S(2)}) collective-permute-start(f32[34,8,128]{2,1,0:T(8,128)S(1)} %get-tuple-element.75), channel_id=1, source_target_pairs={{0,3},{1,2},{2,1},{3,0},{4,7},{5,6},{6,5},{7,4},{8,11},{9,10},{10,... | collective-permute-start | bytes 417800 | tf_op jit(solution)/shard_map/ppermute | solution.py:279
  72.3 2.5 %shard_map.90 = (f32[34,8,128]{2,1,0:T(8,128)S(1)}, f32[34,8,128]{2,1,0:T(8,128)S(1)}, f32[34,8,128]{2,1,0:T(8,128)S(1)}, f32[34,8,128]{2,1,0:T(8,128)S(1)}) custom-call(f32[32,8,128]{2,1,0:T(8,128)S(1)} %get-tuple-element.43.refs_0_, f32[32,8,128]{2,1,0:T(8,128)S(1)} %collective-permute-done.2.refs_1_, f32[32,8,128]{2,1,0:T(8,128)S(1)} %collective-permute-done.3.refs_2_, ...), custom_call_target="tpu_custom_call" | custom-call | flops 3221225472 | bytes 8388608 | tf_op jit(solution)/shard_map/pallas_call | solution.py:388
  74.8 0.0 collective-permute-done.24.refs_1_
  74.8 0.4 collective-permute-start.8
  75.2 3.4 %collective-permute-done.25.refs_2_ = f32[34,8,128]{2,1,0:T(8,128)S(1)} collective-permute-done((f32[34,8,128]{2,1,0:T(8,128)S(1)}, f32[34,8,128]{2,1,0:T(8,128)S(1)}, u32[]{:S(2)}, u32[]{:S(2)}) %collective-permute-start.25) | collective-permute-done | bytes 139296 | tf_op jit(solution)/shard_map/ppermute | solution.py:279
  78.6 1.4 %collective-permute-start.9 = (f32[34,8,128]{2,1,0:T(8,128)S(1)}, f32[34,8,128]{2,1,0:T(8,128)S(1)}, u32[]{:S(2)}, u32[]{:S(2)}) collective-permute-start(f32[34,8,128]{2,1,0:T(8,128)S(1)} %get-tuple-element.54), channel_id=1, source_target_pairs={{0,2},{1,3},{2,0},{3,1},{4,6},{5,7},{6,4},{7,5},{8,10},{9,11},{10,... | collective-permute-start | bytes 417800 | tf_op jit(solution)/shard_map/ppermute | solution.py:279
  79.9 0.5 collective-permute-done.26.refs_3_
  80.4 1.9 %collective-permute-start.10 = (f32[34,8,128]{2,1,0:T(8,128)S(1)}, f32[34,8,128]{2,1,0:T(8,128)S(1)}, u32[]{:S(2)}, u32[]{:S(2)}) collective-permute-start(f32[34,8,128]{2,1,0:T(8,128)S(1)} %get-tuple-element.55), channel_id=1, source_target_pairs={{0,3},{1,2},{2,1},{3,0},{4,7},{5,6},{6,5},{7,4},{8,11},{9,10},{10,... | collective-permute-start | bytes 417800 | tf_op jit(solution)/shard_map/ppermute | solution.py:279
  82.4 1.3 %shard_map.95 = (f32[12,4,64,128]{3,2,1,0:T(8,128)}, f32[12,2,2,128]{3,2,1,0:T(2,128)}) custom-call(f32[34,8,128]{2,1,0:T(8,128)S(1)} %get-tuple-element.72.refs_0_, f32[34,8,128]{2,1,0:T(8,128)S(1)} %collective-permute-done.24.refs_1_, f32[34,8,128]{2,1,0:T(8,128)S(1)} %collective-permute-done.25.refs_2_, ...), custom_call_target="tpu_custom_call" | custom-call | flops 100663296 | bytes 1048576 | tf_op jit(solution)/shard_map/pallas_call | solution.py:398
  83.6 1.3 %shard_map.96 = (f32[12,4,64,128]{3,2,1,0:T(8,128)}, f32[12,2,2,128]{3,2,1,0:T(2,128)}) custom-call(f32[34,8,128]{2,1,0:T(8,128)S(1)} %get-tuple-element.62.refs_0_, f32[34,8,128]{2,1,0:T(8,128)S(1)} %collective-permute-done.16.refs_1_, f32[34,8,128]{2,1,0:T(8,128)S(1)} %collective-permute-done.17.refs_2_, ...), custom_call_target="tpu_custom_call", output_to_operand_aliasing={{0}: (6, {}), {1}: (7, {})} | custom-call | flops 100663296 | bytes 1048576 | tf_op jit(solution)/shard_map/pallas_call | solution.py:398
  84.9 1.2 %collective-permute-done.10.refs_3_ = f32[34,8,128]{2,1,0:T(8,128)S(1)} collective-permute-done((f32[34,8,128]{2,1,0:T(8,128)S(1)}, f32[34,8,128]{2,1,0:T(8,128)S(1)}, u32[]{:S(2)}, u32[]{:S(2)}) %collective-permute-start.10) | collective-permute-done | bytes 139296 | tf_op jit(solution)/shard_map/ppermute | solution.py:279
  86.1 1.3 %shard_map.97 = (f32[12,4,64,128]{3,2,1,0:T(8,128)}, f32[12,2,2,128]{3,2,1,0:T(2,128)}) custom-call(f32[34,8,128]{2,1,0:T(8,128)S(1)} %get-tuple-element.52.refs_0_, f32[34,8,128]{2,1,0:T(8,128)S(1)} %collective-permute-done.8.refs_1_, f32[34,8,128]{2,1,0:T(8,128)S(1)} %collective-permute-done.9.refs_2_, ...), custom_call_target="tpu_custom_call", output_to_operand_aliasing={{0}: (6, {}), {1}: (7, {})} | custom-call | flops 100663296 | bytes 1048576 | tf_op jit(solution)/shard_map/pallas_call | solution.py:398
  (32 shorter events, 0.1 us)
Async XLA Ops:
  0.6 1.4 %copy-start = (f32[12,4,64,128]{3,2,1,0:T(8,128)S(1)}, f32[12,4,64,128]{3,2,1,0:T(8,128)}, u32[]{:S(2)}) copy-start(f32[12,4,64,128]{3,2,1,0:T(8,128)} %state_ref.11) | copy-start | bytes 4718596
  3.1 41.6 %collective-permute-start = (f32[4,2,64,128]{3,2,1,0:T(8,128)}, f32[4,2,64,128]{3,2,1,0:T(8,128)S(1)}, u32[]{:S(2)}, u32[]{:S(2)}) collective-permute-start(f32[4,2,64,128]{3,2,1,0:T(8,128)} %get-tuple-element.41), channel_id=1, source_target_pairs={{0,4},{4,8},{8,12},{12,16},{16,20},{20,24},{24,28},{28,0},{1,5},{5... | collective-permute-start | bytes 786440 | tf_op jit(solution)/shard_map/ppermute | solution.py:272
  6.1 34.0 %copy-start.1 = (f32[12,4,64,128]{3,2,1,0:T(8,128)S(1)}, f32[12,4,64,128]{3,2,1,0:T(8,128)}, u32[]{:S(2)}) copy-start(f32[12,4,64,128]{3,2,1,0:T(8,128)} %state_ref.11) | copy-start | bytes 4718596
  6.1 34.0 %copy-start.3 = (bf16[2,256,512]{2,1,0:T(8,128)(2,1)S(1)}, bf16[2,256,512]{2,1,0:T(8,128)(2,1)}, u32[]{:S(2)}) copy-start(bf16[2,256,512]{2,1,0:T(8,128)(2,1)} %constant.18.clone.high_ref) | copy-start | bytes 1572868
  6.1 34.0 %copy-start.4 = (bf16[2,256,512]{2,1,0:T(8,128)(2,1)S(1)}, bf16[2,256,512]{2,1,0:T(8,128)(2,1)}, u32[]{:S(2)}) copy-start(bf16[2,256,512]{2,1,0:T(8,128)(2,1)} %constant.19.clone.low_ref) | copy-start | bytes 1572868
  6.1 40.2 %collective-permute-start.1 = (f32[4,2,64,128]{3,2,1,0:T(8,128)}, f32[4,2,64,128]{3,2,1,0:T(8,128)S(1)}, u32[]{:S(2)}, u32[]{:S(2)}) collective-permute-start(f32[4,2,64,128]{3,2,1,0:T(8,128)} %get-tuple-element.42), channel_id=1, source_target_pairs={{0,28},{4,0},{8,4},{12,8},{16,12},{20,16},{24,20},{28,24},{1,29},{... | collective-permute-start | bytes 786440 | tf_op jit(solution)/shard_map/ppermute | solution.py:272
  10.2 26.8 %collective-permute-start.11 = (f32[4,2,64,128]{3,2,1,0:T(8,128)S(1)}, f32[4,2,64,128]{3,2,1,0:T(8,128)S(1)}, u32[]{:S(2)}, u32[]{:S(2)}) collective-permute-start(f32[4,2,64,128]{3,2,1,0:T(8,128)S(1)} %get-tuple-element.56), channel_id=1, source_target_pairs={{0,4},{4,8},{8,12},{12,16},{16,20},{20,24},{24,28},{28,0},{1,5},{5... | collective-permute-start | bytes 786440 | tf_op jit(solution)/shard_map/ppermute | solution.py:272
  10.2 29.8 %collective-permute-start.12 = (f32[4,2,64,128]{3,2,1,0:T(8,128)}, f32[4,2,64,128]{3,2,1,0:T(8,128)}, u32[]{:S(2)}, u32[]{:S(2)}) collective-permute-start(f32[4,2,64,128]{3,2,1,0:T(8,128)} %get-tuple-element.57), channel_id=1, source_target_pairs={{0,28},{4,0},{8,4},{12,8},{16,12},{20,16},{24,20},{28,24},{1,29},{... | collective-permute-start | bytes 786440 | tf_op jit(solution)/shard_map/ppermute | solution.py:272
  16.0 13.0 %collective-permute-start.5 = (f32[24,128]{1,0:T(8,128)S(1)}, f32[24,128]{1,0:T(8,128)S(1)}, u32[]{:S(2)}, u32[]{:S(2)}) collective-permute-start(f32[24,128]{1,0:T(8,128)S(1)} %constant_dynamic-update-slice_fusion), channel_id=1, source_target_pairs={{0,4},{4,8},{8,12},{12,16},{16,20},{20,24},{24,28},{28,0},{1,5},{5... | collective-permute-start | bytes 36872 | tf_op jit(solution)/shard_map/ppermute | solution.py:272
  29.0 5.5 %collective-permute-start.6 = (f32[24,128]{1,0:T(8,128)S(1)}, f32[24,128]{1,0:T(8,128)S(1)}, u32[]{:S(2)}, u32[]{:S(2)}) collective-permute-start(f32[24,128]{1,0:T(8,128)S(1)} %add.21), channel_id=1, source_target_pairs={{0,8},{4,12},{8,16},{12,20},{16,24},{20,28},{24,0},{28,4},{1,9},{5... | collective-permute-start | bytes 36872 | tf_op jit(solution)/shard_map/ppermute | solution.py:272
  34.5 19.1 %collective-permute-start.19 = (f32[4,2,64,128]{3,2,1,0:T(8,128)}, f32[4,2,64,128]{3,2,1,0:T(8,128)S(1)}, u32[]{:S(2)}, u32[]{:S(2)}) collective-permute-start(f32[4,2,64,128]{3,2,1,0:T(8,128)} %get-tuple-element.66), channel_id=1, source_target_pairs={{0,4},{4,8},{8,12},{12,16},{16,20},{20,24},{24,28},{28,0},{1,5},{5... | collective-permute-start | bytes 786440 | tf_op jit(solution)/shard_map/ppermute | solution.py:272
  36.9 0.7 copy-start.7
  37.7 16.3 %collective-permute-start.20 = (f32[4,2,64,128]{3,2,1,0:T(8,128)}, f32[4,2,64,128]{3,2,1,0:T(8,128)}, u32[]{:S(2)}, u32[]{:S(2)}) collective-permute-start(f32[4,2,64,128]{3,2,1,0:T(8,128)} %get-tuple-element.67), channel_id=1, source_target_pairs={{0,28},{4,0},{8,4},{12,8},{16,12},{20,16},{24,20},{28,24},{1,29},{... | collective-permute-start | bytes 786440 | tf_op jit(solution)/shard_map/ppermute | solution.py:272
  40.0 4.7 %collective-permute-start.7 = (f32[24,128]{1,0:T(8,128)S(1)}, f32[24,128]{1,0:T(8,128)S(1)}, u32[]{:S(2)}, u32[]{:S(2)}) collective-permute-start(f32[24,128]{1,0:T(8,128)S(1)} %add.22), channel_id=1, source_target_pairs={{0,16},{4,20},{8,24},{12,28},{16,0},{20,4},{24,8},{28,12},{1,17},{... | collective-permute-start | bytes 36872 | tf_op jit(solution)/shard_map/ppermute | solution.py:272
  40.1 1.0 %copy-start.8 = (f32[4,2,64,128]{3,2,1,0:T(8,128)S(1)}, f32[4,2,64,128]{3,2,1,0:T(8,128)}, u32[]{:S(2)}) copy-start(f32[4,2,64,128]{3,2,1,0:T(8,128)} %copy-done.7) | copy-start | bytes 786436
  44.7 12.3 %collective-permute-start.13 = (f32[32,8,128]{2,1,0:T(8,128)S(1)}, f32[32,8,128]{2,1,0:T(8,128)S(1)}, u32[]{:S(2)}, u32[]{:S(2)}) collective-permute-start(f32[32,8,128]{2,1,0:T(8,128)S(1)} %get-tuple-element.59), channel_id=1, source_target_pairs={{0,1},{1,0},{2,3},{3,2},{4,5},{5,4},{6,7},{7,6},{8,9},{9,8},{10,11... | collective-permute-start | bytes 393224 | tf_op jit(solution)/shard_map/ppermute | solution.py:279
  44.7 12.4 %collective-permute-start.14 = (f32[32,8,128]{2,1,0:T(8,128)S(1)}, f32[32,8,128]{2,1,0:T(8,128)S(1)}, u32[]{:S(2)}, u32[]{:S(2)}) collective-permute-start(f32[32,8,128]{2,1,0:T(8,128)S(1)} %get-tuple-element.60), channel_id=1, source_target_pairs={{0,2},{1,3},{2,0},{3,1},{4,6},{5,7},{6,4},{7,5},{8,10},{9,11},{10,... | collective-permute-start | bytes 393224 | tf_op jit(solution)/shard_map/ppermute | solution.py:279
  46.3 11.4 %collective-permute-start.15 = (f32[32,8,128]{2,1,0:T(8,128)S(1)}, f32[32,8,128]{2,1,0:T(8,128)S(1)}, u32[]{:S(2)}, u32[]{:S(2)}) collective-permute-start(f32[32,8,128]{2,1,0:T(8,128)S(1)} %get-tuple-element.61), channel_id=1, source_target_pairs={{0,3},{1,2},{2,1},{3,0},{4,7},{5,6},{6,5},{7,4},{8,11},{9,10},{10,... | collective-permute-start | bytes 393224 | tf_op jit(solution)/shard_map/ppermute | solution.py:279
  46.6 3.4 %copy-start.2 = (f32[32,256,256]{2,1,0:T(8,128)S(1)}, f32[32,256,256]{2,1,0:T(8,128)}, u32[]{:S(2)}) copy-start(f32[32,256,256]{2,1,0:T(8,128)} %inverse_ref.1) | copy-start | bytes 25165828
  53.6 15.3 %collective-permute-start.2 = (f32[32,8,128]{2,1,0:T(8,128)S(1)}, f32[32,8,128]{2,1,0:T(8,128)S(1)}, u32[]{:S(2)}, u32[]{:S(2)}) collective-permute-start(f32[32,8,128]{2,1,0:T(8,128)S(1)} %get-tuple-element.44), channel_id=1, source_target_pairs={{0,1},{1,0},{2,3},{3,2},{4,5},{5,4},{6,7},{7,6},{8,9},{9,8},{10,11... | collective-permute-start | bytes 393224 | tf_op jit(solution)/shard_map/ppermute | solution.py:279
  53.9 5.1 %copy-start.9 = (f32[8,256]{1,0:T(8,128)S(1)}, f32[8,256]{1,0:T(8,128)}, u32[]{:S(2)}) copy-start(f32[8,256]{1,0:T(8,128)} %constant.22.clone.refs_6_) | copy-start | bytes 24580
  53.9 16.5 %collective-permute-start.3 = (f32[32,8,128]{2,1,0:T(8,128)S(1)}, f32[32,8,128]{2,1,0:T(8,128)S(1)}, u32[]{:S(2)}, u32[]{:S(2)}) collective-permute-start(f32[32,8,128]{2,1,0:T(8,128)S(1)} %get-tuple-element.45), channel_id=1, source_target_pairs={{0,2},{1,3},{2,0},{3,1},{4,6},{5,7},{6,4},{7,5},{8,10},{9,11},{10,... | collective-permute-start | bytes 393224 | tf_op jit(solution)/shard_map/ppermute | solution.py:279
  57.0 4.4 %collective-permute-start.21 = (f32[32,8,128]{2,1,0:T(8,128)S(1)}, f32[32,8,128]{2,1,0:T(8,128)S(1)}, u32[]{:S(2)}, u32[]{:S(2)}) collective-permute-start(f32[32,8,128]{2,1,0:T(8,128)S(1)} %get-tuple-element.69), channel_id=1, source_target_pairs={{0,1},{1,0},{2,3},{3,2},{4,5},{5,4},{6,7},{7,6},{8,9},{9,8},{10,11... | collective-permute-start | bytes 393224 | tf_op jit(solution)/shard_map/ppermute | solution.py:279
  57.1 6.4 %collective-permute-start.22 = (f32[32,8,128]{2,1,0:T(8,128)S(1)}, f32[32,8,128]{2,1,0:T(8,128)S(1)}, u32[]{:S(2)}, u32[]{:S(2)}) collective-permute-start(f32[32,8,128]{2,1,0:T(8,128)S(1)} %get-tuple-element.70), channel_id=1, source_target_pairs={{0,2},{1,3},{2,0},{3,1},{4,6},{5,7},{6,4},{7,5},{8,10},{9,11},{10,... | collective-permute-start | bytes 393224 | tf_op jit(solution)/shard_map/ppermute | solution.py:279
  57.7 7.6 %collective-permute-start.23 = (f32[32,8,128]{2,1,0:T(8,128)S(1)}, f32[32,8,128]{2,1,0:T(8,128)S(1)}, u32[]{:S(2)}, u32[]{:S(2)}) collective-permute-start(f32[32,8,128]{2,1,0:T(8,128)S(1)} %get-tuple-element.71), channel_id=1, source_target_pairs={{0,3},{1,2},{2,1},{3,0},{4,7},{5,6},{6,5},{7,4},{8,11},{9,10},{10,... | collective-permute-start | bytes 393224 | tf_op jit(solution)/shard_map/ppermute | solution.py:279
  61.5 8.9 %collective-permute-start.4 = (f32[32,8,128]{2,1,0:T(8,128)S(1)}, f32[32,8,128]{2,1,0:T(8,128)S(1)}, u32[]{:S(2)}, u32[]{:S(2)}) collective-permute-start(f32[32,8,128]{2,1,0:T(8,128)S(1)} %get-tuple-element.46), channel_id=1, source_target_pairs={{0,3},{1,2},{2,1},{3,0},{4,7},{5,6},{6,5},{7,4},{8,11},{9,10},{10,... | collective-permute-start | bytes 393224 | tf_op jit(solution)/shard_map/ppermute | solution.py:279
  63.6 7.6 %collective-permute-start.16 = (f32[34,8,128]{2,1,0:T(8,128)S(1)}, f32[34,8,128]{2,1,0:T(8,128)S(1)}, u32[]{:S(2)}, u32[]{:S(2)}) collective-permute-start(f32[34,8,128]{2,1,0:T(8,128)S(1)} %get-tuple-element.63), channel_id=1, source_target_pairs={{0,1},{1,0},{2,3},{3,2},{4,5},{5,4},{6,7},{7,6},{8,9},{9,8},{10,11... | collective-permute-start | bytes 417800 | tf_op jit(solution)/shard_map/ppermute | solution.py:279
  65.3 18.3 %collective-permute-start.17 = (f32[34,8,128]{2,1,0:T(8,128)S(1)}, f32[34,8,128]{2,1,0:T(8,128)S(1)}, u32[]{:S(2)}, u32[]{:S(2)}) collective-permute-start(f32[34,8,128]{2,1,0:T(8,128)S(1)} %get-tuple-element.64), channel_id=1, source_target_pairs={{0,2},{1,3},{2,0},{3,1},{4,6},{5,7},{6,4},{7,5},{8,10},{9,11},{10,... | collective-permute-start | bytes 417800 | tf_op jit(solution)/shard_map/ppermute | solution.py:279
  68.8 14.8 %collective-permute-start.18 = (f32[34,8,128]{2,1,0:T(8,128)S(1)}, f32[34,8,128]{2,1,0:T(8,128)S(1)}, u32[]{:S(2)}, u32[]{:S(2)}) collective-permute-start(f32[34,8,128]{2,1,0:T(8,128)S(1)} %get-tuple-element.65), channel_id=1, source_target_pairs={{0,3},{1,2},{2,1},{3,0},{4,7},{5,6},{6,5},{7,4},{8,11},{9,10},{10,... | collective-permute-start | bytes 417800 | tf_op jit(solution)/shard_map/ppermute | solution.py:279
  70.4 4.4 %collective-permute-start.24 = (f32[34,8,128]{2,1,0:T(8,128)S(1)}, f32[34,8,128]{2,1,0:T(8,128)S(1)}, u32[]{:S(2)}, u32[]{:S(2)}) collective-permute-start(f32[34,8,128]{2,1,0:T(8,128)S(1)} %get-tuple-element.73), channel_id=1, source_target_pairs={{0,1},{1,0},{2,3},{3,2},{4,5},{5,4},{6,7},{7,6},{8,9},{9,8},{10,11... | collective-permute-start | bytes 417800 | tf_op jit(solution)/shard_map/ppermute | solution.py:279
  70.4 8.2 %collective-permute-start.25 = (f32[34,8,128]{2,1,0:T(8,128)S(1)}, f32[34,8,128]{2,1,0:T(8,128)S(1)}, u32[]{:S(2)}, u32[]{:S(2)}) collective-permute-start(f32[34,8,128]{2,1,0:T(8,128)S(1)} %get-tuple-element.74), channel_id=1, source_target_pairs={{0,2},{1,3},{2,0},{3,1},{4,6},{5,7},{6,4},{7,5},{8,10},{9,11},{10,... | collective-permute-start | bytes 417800 | tf_op jit(solution)/shard_map/ppermute | solution.py:279
  71.1 9.3 %collective-permute-start.26 = (f32[34,8,128]{2,1,0:T(8,128)S(1)}, f32[34,8,128]{2,1,0:T(8,128)S(1)}, u32[]{:S(2)}, u32[]{:S(2)}) collective-permute-start(f32[34,8,128]{2,1,0:T(8,128)S(1)} %get-tuple-element.75), channel_id=1, source_target_pairs={{0,3},{1,2},{2,1},{3,0},{4,7},{5,6},{6,5},{7,4},{8,11},{9,10},{10,... | collective-permute-start | bytes 417800 | tf_op jit(solution)/shard_map/ppermute | solution.py:279
  72.3 10.1 %copy-start.5 = (bf16[128,128]{1,0:T(8,128)(2,1)S(1)}, bf16[128,128]{1,0:T(8,128)(2,1)}, u32[]{:S(2)}) copy-start(bf16[128,128]{1,0:T(8,128)(2,1)} %constant.20.clone.refs_4_) | copy-start | bytes 98308
  72.3 10.1 %copy-start.6 = (bf16[128,128]{1,0:T(8,128)(2,1)S(1)}, bf16[128,128]{1,0:T(8,128)(2,1)}, u32[]{:S(2)}) copy-start(bf16[128,128]{1,0:T(8,128)(2,1)} %constant.21.clone.refs_5_) | copy-start | bytes 98308
  74.8 10.1 %collective-permute-start.8 = (f32[34,8,128]{2,1,0:T(8,128)S(1)}, f32[34,8,128]{2,1,0:T(8,128)S(1)}, u32[]{:S(2)}, u32[]{:S(2)}) collective-permute-start(f32[34,8,128]{2,1,0:T(8,128)S(1)} %get-tuple-element.53), channel_id=1, source_target_pairs={{0,1},{1,0},{2,3},{3,2},{4,5},{5,4},{6,7},{7,6},{8,9},{9,8},{10,11... | collective-permute-start | bytes 417800 | tf_op jit(solution)/shard_map/ppermute | solution.py:279
  78.6 6.3 %collective-permute-start.9 = (f32[34,8,128]{2,1,0:T(8,128)S(1)}, f32[34,8,128]{2,1,0:T(8,128)S(1)}, u32[]{:S(2)}, u32[]{:S(2)}) collective-permute-start(f32[34,8,128]{2,1,0:T(8,128)S(1)} %get-tuple-element.54), channel_id=1, source_target_pairs={{0,2},{1,3},{2,0},{3,1},{4,6},{5,7},{6,4},{7,5},{8,10},{9,11},{10,... | collective-permute-start | bytes 417800 | tf_op jit(solution)/shard_map/ppermute | solution.py:279
  80.4 5.7 %collective-permute-start.10 = (f32[34,8,128]{2,1,0:T(8,128)S(1)}, f32[34,8,128]{2,1,0:T(8,128)S(1)}, u32[]{:S(2)}, u32[]{:S(2)}) collective-permute-start(f32[34,8,128]{2,1,0:T(8,128)S(1)} %get-tuple-element.55), channel_id=1, source_target_pairs={{0,3},{1,2},{2,1},{3,0},{4,7},{5,6},{6,5},{7,4},{8,11},{9,10},{10,... | collective-permute-start | bytes 417800 | tf_op jit(solution)/shard_map/ppermute | solution.py:279

commit v3 on v2

--- a/solution.py
+++ b/solution.py
@@ -97,8 +97,9 @@
     return pltpu.roll(x, LANES // 2, len(x.shape) - 1)
 
 
-def pack_kernel(base, state_ref, last_ref, first_ref, sums_ref):
+def pack_kernel(base, state_ref, near_ref, far_ref, sums_ref):
     rows = state_ref.shape[2]
+    even = jnp.bitwise_and(lax.axis_index("gx"), 1) == 0
     left = left_lanes((rows, LANES))
     totals = []
     for e in range(GROUP):
@@ -107,8 +108,10 @@
             a = state_ref[base + e, p]
             b = state_ref[base + e, p + 2]
             acc += a * a + b * b
-            last_ref[e, p] = jnp.where(left, swap(a), b)
-            first_ref[e, p] = jnp.where(left, a, swap(b))
+            last = jnp.where(left, swap(a), b)
+            first = jnp.where(left, a, swap(b))
+            near_ref[e, p] = jnp.where(even, last, first)
+            far_ref[e, p] = jnp.where(even, first, last)
         totals.append(jnp.sum(acc))
     half = left_lanes((4, LANES))
     for q in range(GROUP // 2):
@@ -139,20 +142,25 @@
             high_ref[at], low_ref[at] = split(x)
 
 
-def project_kernel(base, state_ref, before_ref, after_ref, high_ref, low_ref, mask_ref, *out_refs):
+def project_kernel(base, state_ref, near_ref, far_ref, high_ref, low_ref, *out_refs):
     parts = len(out_refs)
     slots, rows, _ = out_refs[0].shape
     coef = state_ref.shape[2]
     count = slots * parts
-    mask = mask_ref[...]
+    lane = lax.broadcasted_iota(jnp.int32, (1, GROUP * coef), 1)
+    index = lax.axis_index("gy") * coef + lax.rem(lane, coef)
+    interior = index < coef * parts - 2
+    even = jnp.bitwise_and(lax.axis_index("gx"), 1) == 0
     where = [pl.multiple_of(peer * slots, slots) for peer in peers(parts)]
     for p in range(2):
+        near = near_ref[:, p].reshape(GROUP * coef, LANES)
+        far = far_ref[:, p].reshape(GROUP * coef, LANES)
         x = jnp.concatenate(
             [
                 state_ref[base : base + GROUP, p].reshape(GROUP * coef, LANES),
                 state_ref[base : base + GROUP, p + 2].reshape(GROUP * coef, LANES),
-                before_ref[:, p].reshape(GROUP * coef, LANES),
-                after_ref[:, p].reshape(GROUP * coef, LANES),
+                jnp.where(even, far, near),
+                jnp.where(even, near, far),
             ],
             axis=1,
         )
@@ -164,7 +172,7 @@
             for ref in (high_ref, low_ref)
         ]
         t = dot(w_high, x_high, NT) + (dot(w_high, x_low, NT) + dot(w_low, x_high, NT))
-        t = t * mask
+        t = jnp.where(interior, t, 0.0)
         for d in range(parts):
             flat = out_refs[d].reshape(slots * rows, LANES)
             for f in range(2):
@@ -175,10 +183,10 @@
                     ]
 
 
-def solve_kernel(base, parts, *refs):
+def solve_kernel(parts, *refs):
     recv_refs = refs[:parts]
-    high_ref, low_ref, wall_ref, sums_ref = refs[parts : parts + 4]
-    out_refs = refs[parts + 4 :]
+    high_ref, low_ref, wall_ref = refs[parts : parts + 3]
+    out_refs = refs[parts + 3 :]
     slots, rows, _ = recv_refs[0].shape
     left = left_lanes((rows, LANES))
     lane = lax.broadcasted_iota(jnp.int32, (rows, LANES), 1)
@@ -210,28 +218,24 @@
                 sums = jnp.where(lane == at, q[e * rows : (e + 1) * rows], sums)
     for ref in out_refs:
         ref[slots] = sums
-        ref[slots + 1] = sums_ref[base : base + rows]
-
-
-def back_kernel(total, parts, *refs):
+
+
+def back_kernel(total, base, parts, *refs):
     recv_refs = refs[:parts]
-    high_ref, low_ref = refs[parts : parts + 2]
+    high_ref, low_ref, sums_ref = refs[parts : parts + 3]
     out_ref, wall_ref = refs[-2:]
     slots, rows, _ = recv_refs[0].shape
     coef = out_ref.shape[2]
-    width = slots - 2
+    width = slots - 1
     where = [pl.multiple_of(peer * width, width) for peer in peers(parts)]
     b_high, b_low = [
         jnp.concatenate([ref[pl.ds(at, width), :] for at in where], axis=0)
         for ref in (high_ref, low_ref)
     ]
-    n = [ref[slots - 1] for ref in recv_refs]
     me = lax.axis_index("gy")
     near = jnp.bitwise_and(me, 1) != 0
     far = jnp.bitwise_and(me, 2) != 0
-    n = [jnp.where(near, n[d ^ 1], n[d]) for d in range(parts)]
-    n = [jnp.where(far, n[d ^ 2], n[d]) for d in range(parts)]
-    scale = lax.rsqrt(sum(n[1:], n[0]) / total + EPSILON)
+    scale = lax.rsqrt(sums_ref[base : base + rows] / total + EPSILON)
     for r in range(rows):
         q, f = r // 4, r % 4
         s = jnp.concatenate(
@@ -247,7 +251,7 @@
         for e in range(2):
             out_ref[2 * q + e, f] = o[e * coef : (e + 1) * coef]
     lane = lax.broadcasted_iota(jnp.int32, (rows, LANES), 1)
-    tiles = [ref[slots - 2] for ref in recv_refs]
+    tiles = [ref[slots - 1] for ref in recv_refs]
     tiles = [jnp.where(near, tiles[d ^ 1], tiles[d]) for d in range(parts)]
     tiles = [jnp.where(far, tiles[d ^ 2], tiles[d]) * scale for d in range(parts)]
     b_high = high_ref[...]
@@ -267,11 +271,6 @@
                     wall_ref[2 * q + e, w, c : c + 1] = o[row : row + 1]
 
 
-def shifted(x, axis, by):
-    n = lax.axis_size(axis)
-    return lax.ppermute(x, axis, [(i, (i + by) % n) for i in range(n)])
-
-
 def exchanged(pieces, axis):
     n = lax.axis_size(axis)
     got = list(pieces)
@@ -280,15 +279,22 @@
     return got
 
 
-def ring_sum(x, axis):
-    n = lax.axis_size(axis)
-    if n & (n - 1):
-        return lax.psum(x, axis)
-    hop = 1
-    while hop < n:
-        other = shifted(x, axis, hop)
-        x = x + other
-        hop *= 2
+def halo_pairs(n):
+    near = [(i, i ^ 1) for i in range(n)]
+    far = [(i, (i + (1 if i % 2 else -1)) % n) for i in range(n)]
+    return near, far
+
+
+def axis_hops(n):
+    return [1 << i for i in range(n.bit_length() - 1)]
+
+
+def full_sum(x):
+    for axis in ("gx", "gy"):
+        n = lax.axis_size(axis)
+        for hop in axis_hops(n):
+            other = lax.ppermute(x, axis, [(i, i ^ hop) for i in range(n)])
+            x = x + other
     return x
 
 
@@ -312,10 +318,6 @@
     wall[1] = np.where(k % 2 == 0, -1.0, 1.0) * curvature
     wall = jnp.asarray(wall)
 
-    coef_global = lax.axis_index("gy") * coef + jnp.arange(coef, dtype=jnp.int32)
-    keep = (coef_global < coef_count - 2).astype(jnp.float32)
-    mask = jnp.tile(keep, GROUP)[None, :]
-
     def grouped(g, shape):
         return pl.BlockSpec((GROUP,) + shape, lambda i: (g,) + (0,) * len(shape))
 
@@ -332,7 +334,7 @@
     halo_bytes = 4 * int(np.prod(halo))
     small = (group_rows, LANES)
     sent_shape = (mine, group_rows, LANES)
-    back_shape = (mine + 2, group_rows, LANES)
+    back_shape = (mine + 1, group_rows, LANES)
 
     packed = []
     for g in range(groups):
@@ -352,11 +354,12 @@
             )(state)
         )
     halos = []
-    for last, first, _ in packed:
-        before = shifted(last, "gx", 1)
-        after = shifted(first, "gx", -1)
-        halos.append((before, after))
-    sums = ring_sum(jnp.concatenate([p[2] for p in packed], axis=0), "gx")
+    near_pairs, far_pairs = halo_pairs(lax.axis_size("gx"))
+    for near, far, _ in packed:
+        near = lax.ppermute(near, "gx", near_pairs)
+        far = lax.ppermute(far, "gx", far_pairs)
+        halos.append((near, far))
+    sums = full_sum(jnp.concatenate([p[2] for p in packed], axis=0))
 
     per_step = 4
     split_shape = (per_step, coef_count, coef_count)
@@ -380,36 +383,36 @@
             8,
             2 * 3 * 2 * 256 * 512 * GROUP * coef,
             6 * halo_bytes,
-            in_specs=[VMEM] * 6,
+            in_specs=[VMEM] * 5,
             out_specs=[VMEM] * parts,
             out_shape=[jax.ShapeDtypeStruct(sent_shape, jnp.float32)] * parts,
-        )(state, *halos[g], step_high, step_low, mask)
+        )(state, *halos[g], step_high, step_low)
         got = exchanged(sent, "gy")
         solved = call(
-            functools.partial(solve_kernel, g * group_rows, parts),
-            24,
+            functools.partial(solve_kernel, parts),
+            6,
             2 * 3 * mine * coef_count**2 * 256,
             4 * mine * coef_count**2,
-            in_specs=[VMEM] * (parts + 4),
+            in_specs=[VMEM] * (parts + 3),
             out_specs=[VMEM] * parts,
             out_shape=[jax.ShapeDtypeStruct(back_shape, jnp.float32)] * parts,
-        )(*got, inverse_high, inverse_low, wall, sums)
+        )(*got, inverse_high, inverse_low, wall)
         returned = exchanged(solved, "gy")
         outputs = call(
-            functools.partial(back_kernel, float(fields * coef_count * grid_x), parts),
+            functools.partial(back_kernel, float(fields * coef_count * grid_x), g * group_rows, parts),
             8,
             2 * 3 * 128 * 128 * GROUP * fields * coef,
             4 * halo_bytes,
             grid=(1,),
-            in_specs=[VMEM] * (parts + 2)
+            in_specs=[VMEM] * (parts + 3)
             + [pl.BlockSpec(memory_space=pl.ANY)] * len(outputs),
             out_specs=[grouped(g, block), grouped(g, (2, 2, points))],
             out_shape=[
                 jax.ShapeDtypeStruct(state.shape, jnp.float32),
                 jax.ShapeDtypeStruct((members, 2, 2, points), jnp.float32),
             ],
-            input_output_aliases={parts + 2 + i: i for i in range(len(outputs))},
-        )(*returned, back_high, back_low, *outputs)
+            input_output_aliases={parts + 3 + i: i for i in range(len(outputs))},
+        )(*returned, back_high, back_low, sums, *outputs)
     return tuple(outputs)
 
 

time: 87.7 us -> 87.8 us (level)
  Pallas kernels: 21.1 us -> 16.9 us
  waiting for transfers between devices: 27.3 us -> 31.2 us
  starting transfers between devices: 31.5 us -> 33.6 us
  local copies, waits for them, and re-layouts: 6.56 us -> 4.82 us
    ppermute x9 -> x11, starting transfers between devices: 17.1 us -> 20.8 us  [the longest x3 9.06 us: per_device(): far = lax.ppermute(far, 'gx', far_pairs)]
    pallas_call x3, Pallas kernels: 3.14 us -> 0.82 us  [per_device(): call(functools.partial(pack_kernel, g * GROUP), 6, 10 ** 6, 4 * halo_byte...]
    ppermute x18, waiting for transfers between devices: 8.37 us -> 10.4 us  [exchanged(): got[d] = lax.ppermute(pieces[d], axis, [(i, i ^ d) for i in range(n)])]
    pallas_call x3, Pallas kernels: 3.82 us -> 1.93 us  [per_device(): call(functools.partial(project_kernel, g * GROUP), 8, 2 * 3 * 2 * 256 * 5...]
    ppermute x9 -> x11, waiting for transfers between devices: 19 us -> 20.7 us  [the longest x5 20.7 us: full_sum(): other = lax.ppermute(x, axis, [(i, i ^ hop) for i in range(n)])]
    unnamed x22 -> x18, local copies, waits for them, and re-layouts: 6.47 us -> 4.81 us
    ppermute x18, starting transfers between devices: 14.4 us -> 12.8 us  [exchanged(): got[d] = lax.ppermute(pieces[d], axis, [(i, i ^ d) for i in range(n)])]
  transfers between devices with their start and end apart: 27 -> 29, of which waited for: 8 -> 10; matrix products, arithmetic and copies ran while one was open for 0% -> 0% of each run, Pallas kernels for 22% -> 18%
where the time goes in v3:
time: 87.8 us; the launch traced here: 87.3 us
  starting transfers between devices  33.6 us (38%)
  waiting for transfers between devices  31.2 us (36%)
  Pallas kernels  16.9 us (19%)
  local copies, waits for them, and re-layouts  4.82 us (5%)
    ppermute x5, waiting for transfers between devices, full_sum(): other = lax.ppermute(x, axis, [(i, i ^ hop) for i in range(n)])  20.7 us
    ppermute x18, starting transfers between devices, exchanged(): got[d] = lax.ppermute(pieces[d], axis, [(i, i ^ d) for i in range(n)])  12.8 us
    ppermute x18, waiting for transfers between devices, exchanged(): got[d] = lax.ppermute(pieces[d], axis, [(i, i ^ d) for i in range(n)])  10.4 us
    ppermute x3, starting transfers between devices, per_device(): far = lax.ppermute(far, 'gx', far_pairs)  9.06 us
    pallas_call x3, Pallas kernels, per_device(): call(functools.partial(solve_kernel, parts), 6, 2 * 3 * mine * coef_count...  7.46 us
    ppermute x5, starting transfers between devices, full_sum(): other = lax.ppermute(x, axis, [(i, i ^ hop) for i in range(n)])  6.91 us
    ppermute x3, starting transfers between devices, per_device(): near = lax.ppermute(near, 'gx', near_pairs)  4.84 us
    unnamed x18, local copies, waits for them, and re-layouts  4.81 us
  transfers between devices with their start and end apart: 29, of which 10 were waited for; matrix products, arithmetic and copies ran while one was open for 0% of the time, Pallas kernels for 18%

profile of v3, /device:TPU:0, one launch (start us, length us, event | category | flops | bytes accessed | tf_op | source)
XLA Modules:
  0.0 87.3 jit_solution(12786294054212227849)
XLA Ops:
  0.6 0.0 copy-start
  0.6 1.4 %copy-done = f32[12,4,64,128]{3,2,1,0:T(8,128)S(1)} copy-done((f32[12,4,64,128]{3,2,1,0:T(8,128)S(1)}, f32[12,4,64,128]{3,2,1,0:T(8,128)}, u32[]{:S(2)}) %copy-start) | copy-done | bytes 1572888
  2.0 0.3 shard_map.86
  2.3 3.0 %collective-permute-start = (f32[4,2,64,128]{3,2,1,0:T(8,128)S(1)}, f32[4,2,64,128]{3,2,1,0:T(8,128)S(1)}, u32[]{:S(2)}, u32[]{:S(2)}) collective-permute-start(f32[4,2,64,128]{3,2,1,0:T(8,128)S(1)} %get-tuple-element.41), channel_id=1, source_target_pairs={{0,4},{4,0},{8,12},{12,8},{16,20},{20,16},{24,28},{28,24},{1,5},{5... | collective-permute-start | bytes 786440 | tf_op jit(solution)/shard_map/ppermute | solution.py:359
  5.4 3.6 %collective-permute-start.1 = (f32[4,2,64,128]{3,2,1,0:T(8,128)S(1)}, f32[4,2,64,128]{3,2,1,0:T(8,128)S(1)}, u32[]{:S(2)}, u32[]{:S(2)}) collective-permute-start(f32[4,2,64,128]{3,2,1,0:T(8,128)S(1)} %get-tuple-element.42), channel_id=1, source_target_pairs={{0,28},{4,8},{8,4},{12,16},{16,12},{20,24},{24,20},{28,0},{1,29},{... | collective-permute-start | bytes 786440 | tf_op jit(solution)/shard_map/ppermute | solution.py:360
  8.9 0.3 shard_map.90
  9.2 0.1 collective-permute-start.13
  9.3 1.9 %collective-permute-start.14 = (f32[4,2,64,128]{3,2,1,0:T(8,128)S(1)}, f32[4,2,64,128]{3,2,1,0:T(8,128)S(1)}, u32[]{:S(2)}, u32[]{:S(2)}) collective-permute-start(f32[4,2,64,128]{3,2,1,0:T(8,128)S(1)} %get-tuple-element.57), channel_id=1, source_target_pairs={{0,28},{4,8},{8,4},{12,16},{16,12},{20,24},{24,20},{28,0},{1,29},{... | collective-permute-start | bytes 786440 | tf_op jit(solution)/shard_map/ppermute | solution.py:360
  11.2 0.3 shard_map.89
  11.5 0.7 collective-permute-start.8
  12.2 16.6 %collective-permute-done.8 = f32[24,128]{1,0:T(8,128)S(1)} collective-permute-done((f32[24,128]{1,0:T(8,128)S(1)}, f32[24,128]{1,0:T(8,128)S(1)}, u32[]{:S(2)}, u32[]{:S(2)}) %collective-permute-start.8) | collective-permute-done | bytes 12320 | tf_op jit(solution)/shard_map/ppermute | solution.py:296
  28.8 1.8 %collective-permute-start.9 = (f32[24,128]{1,0:T(8,128)S(1)}, f32[24,128]{1,0:T(8,128)S(1)}, u32[]{:S(2)}, u32[]{:S(2)}) collective-permute-start(f32[24,128]{1,0:T(8,128)S(1)} %add.15), channel_id=1, source_target_pairs={{0,8},{4,12},{8,0},{12,4},{16,24},{20,28},{24,16},{28,20},{1,9},{5... | collective-permute-start | bytes 36872 | tf_op jit(solution)/shard_map/ppermute | solution.py:296
  30.6 1.9 %collective-permute-done.9 = f32[24,128]{1,0:T(8,128)S(1)} collective-permute-done((f32[24,128]{1,0:T(8,128)S(1)}, f32[24,128]{1,0:T(8,128)S(1)}, u32[]{:S(2)}, u32[]{:S(2)}) %collective-permute-start.9) | collective-permute-done | bytes 12320 | tf_op jit(solution)/shard_map/ppermute | solution.py:296
  32.5 2.8 %collective-permute-start.10 = (f32[24,128]{1,0:T(8,128)S(1)}, f32[24,128]{1,0:T(8,128)S(1)}, u32[]{:S(2)}, u32[]{:S(2)}) collective-permute-start(f32[24,128]{1,0:T(8,128)S(1)} %add.16), channel_id=1, source_target_pairs={{0,16},{4,20},{8,24},{12,28},{16,0},{20,4},{24,8},{28,12},{1,17},{... | collective-permute-start | bytes 36872 | tf_op jit(solution)/shard_map/ppermute | solution.py:296
  35.3 1.8 %collective-permute-done.10 = f32[24,128]{1,0:T(8,128)S(1)} collective-permute-done((f32[24,128]{1,0:T(8,128)S(1)}, f32[24,128]{1,0:T(8,128)S(1)}, u32[]{:S(2)}, u32[]{:S(2)}) %collective-permute-start.10) | collective-permute-done | bytes 12320 | tf_op jit(solution)/shard_map/ppermute | solution.py:296
  37.1 1.7 %collective-permute-start.21 = (f32[4,2,64,128]{3,2,1,0:T(8,128)S(1)}, f32[4,2,64,128]{3,2,1,0:T(8,128)S(1)}, u32[]{:S(2)}, u32[]{:S(2)}) collective-permute-start(f32[4,2,64,128]{3,2,1,0:T(8,128)S(1)} %get-tuple-element.66), channel_id=1, source_target_pairs={{0,4},{4,0},{8,12},{12,8},{16,20},{20,16},{24,28},{28,24},{1,5},{5... | collective-permute-start | bytes 786440 | tf_op jit(solution)/shard_map/ppermute | solution.py:359
  38.8 0.0 collective-permute-done.13.near_ref
  38.8 3.6 %collective-permute-start.22 = (f32[4,2,64,128]{3,2,1,0:T(8,128)S(1)}, f32[4,2,64,128]{3,2,1,0:T(8,128)S(1)}, u32[]{:S(2)}, u32[]{:S(2)}) collective-permute-start(f32[4,2,64,128]{3,2,1,0:T(8,128)S(1)} %get-tuple-element.67), channel_id=1, source_target_pairs={{0,28},{4,8},{8,4},{12,16},{16,12},{20,24},{24,20},{28,0},{1,29},{... | collective-permute-start | bytes 786440 | tf_op jit(solution)/shard_map/ppermute | solution.py:360
  42.4 0.0 collective-permute-done.14.far_ref
  42.4 0.0 collective-permute-start.11
  42.5 0.6 shard_map.91
  43.1 0.5 collective-permute-done.11
  43.6 0.2 collective-permute-start.15
  43.8 1.5 %collective-permute-start.16 = (f32[32,8,128]{2,1,0:T(8,128)S(1)}, f32[32,8,128]{2,1,0:T(8,128)S(1)}, u32[]{:S(2)}, u32[]{:S(2)}) collective-permute-start(f32[32,8,128]{2,1,0:T(8,128)S(1)} %get-tuple-element.60), channel_id=1, source_target_pairs={{0,2},{1,3},{2,0},{3,1},{4,6},{5,7},{6,4},{7,5},{8,10},{9,11},{10,... | collective-permute-start | bytes 393224 | tf_op jit(solution)/shard_map/ppermute | solution.py:278
  45.3 0.0 collective-permute-done.1.far_ref
  45.3 0.2 collective-permute-start.17
  45.5 3.4 %copy-done.2 = f32[32,256,256]{2,1,0:T(8,128)S(1)} copy-done((f32[32,256,256]{2,1,0:T(8,128)S(1)}, f32[32,256,256]{2,1,0:T(8,128)}, u32[]{:S(2)}) %copy-start.2) | copy-done | bytes 8388632
  48.8 2.9 %split.1 = (bf16[32,256,256]{2,1,0:T(8,128)(2,1)S(1)}, bf16[32,256,256]{2,1,0:T(8,128)(2,1)S(1)}) custom-call(f32[32,256,256]{2,1,0:T(8,128)S(1)} %copy-done.2), custom_call_target="tpu_custom_call" | custom-call | flops 10000000 | bytes 16777216 | tf_op jit(solution)/shard_map/split/pallas_call | solution.py:366
  51.8 0.6 shard_map.87
  52.4 0.0 collective-permute-done.21.near_ref
  52.4 1.6 %collective-permute-start.12 = (f32[24,128]{1,0:T(8,128)S(1)}, f32[24,128]{1,0:T(8,128)S(1)}, u32[]{:S(2)}, u32[]{:S(2)}) collective-permute-start(f32[24,128]{1,0:T(8,128)S(1)} %add.18), channel_id=1, source_target_pairs={{0,2},{1,3},{2,0},{3,1},{4,6},{5,7},{6,4},{7,5},{8,10},{9,11},{10,... | collective-permute-start | bytes 36872 | tf_op jit(solution)/shard_map/ppermute | solution.py:296
  54.0 0.2 collective-permute-start.2
  54.2 0.6 shard_map.93
  54.9 0.0 collective-permute-done.15.refs_1_
  54.9 0.4 collective-permute-start.23
  55.3 0.0 collective-permute-done.16.refs_2_
  55.3 0.5 collective-permute-start.24
  55.8 1.0 %collective-permute-start.25 = (f32[32,8,128]{2,1,0:T(8,128)S(1)}, f32[32,8,128]{2,1,0:T(8,128)S(1)}, u32[]{:S(2)}, u32[]{:S(2)}) collective-permute-start(f32[32,8,128]{2,1,0:T(8,128)S(1)} %get-tuple-element.71), channel_id=1, source_target_pairs={{0,3},{1,2},{2,1},{3,0},{4,7},{5,6},{6,5},{7,4},{8,11},{9,10},{10,... | collective-permute-start | bytes 393224 | tf_op jit(solution)/shard_map/ppermute | solution.py:278
  56.8 2.5 %shard_map.92 = (f32[33,8,128]{2,1,0:T(8,128)S(1)}, f32[33,8,128]{2,1,0:T(8,128)S(1)}, f32[33,8,128]{2,1,0:T(8,128)S(1)}, f32[33,8,128]{2,1,0:T(8,128)S(1)}) custom-call(f32[32,8,128]{2,1,0:T(8,128)S(1)} %get-tuple-element.58.refs_0_, f32[32,8,128]{2,1,0:T(8,128)S(1)} %collective-permute-done.15.refs_1_, f32[32,8,128]{2,1,0:T(8,128)S(1)} %collective-permute-done.16.refs_2_, ...), custom_call_target="tpu_custom_call" | custom-call | flops 3221225472 | bytes 8388608 | tf_op jit(solution)/shard_map/pallas_call | solution.py:391
  59.3 0.6 collective-permute-start.3
  59.9 1.8 %collective-permute-done.24.refs_2_ = f32[32,8,128]{2,1,0:T(8,128)S(1)} collective-permute-done((f32[32,8,128]{2,1,0:T(8,128)S(1)}, f32[32,8,128]{2,1,0:T(8,128)S(1)}, u32[]{:S(2)}, u32[]{:S(2)}) %collective-permute-start.24) | collective-permute-done | bytes 131104 | tf_op jit(solution)/shard_map/ppermute | solution.py:278
  61.6 0.0 collective-permute-start.4
  61.6 1.2 %collective-permute-done.25.refs_3_ = f32[32,8,128]{2,1,0:T(8,128)S(1)} collective-permute-done((f32[32,8,128]{2,1,0:T(8,128)S(1)}, f32[32,8,128]{2,1,0:T(8,128)S(1)}, u32[]{:S(2)}, u32[]{:S(2)}) %collective-permute-start.25) | collective-permute-done | bytes 131104 | tf_op jit(solution)/shard_map/ppermute | solution.py:278
  62.8 1.4 %collective-permute-start.18 = (f32[33,8,128]{2,1,0:T(8,128)S(1)}, f32[33,8,128]{2,1,0:T(8,128)S(1)}, u32[]{:S(2)}, u32[]{:S(2)}) collective-permute-start(f32[33,8,128]{2,1,0:T(8,128)S(1)} %get-tuple-element.63), channel_id=1, source_target_pairs={{0,1},{1,0},{2,3},{3,2},{4,5},{5,4},{6,7},{7,6},{8,9},{9,8},{10,11... | collective-permute-start | bytes 405512 | tf_op jit(solution)/shard_map/ppermute | solution.py:278
  64.3 2.5 %shard_map.94 = (f32[33,8,128]{2,1,0:T(8,128)S(1)}, f32[33,8,128]{2,1,0:T(8,128)S(1)}, f32[33,8,128]{2,1,0:T(8,128)S(1)}, f32[33,8,128]{2,1,0:T(8,128)S(1)}) custom-call(f32[32,8,128]{2,1,0:T(8,128)S(1)} %get-tuple-element.68.refs_0_, f32[32,8,128]{2,1,0:T(8,128)S(1)} %collective-permute-done.23.refs_1_, f32[32,8,128]{2,1,0:T(8,128)S(1)} %collective-permute-done.24.refs_2_, ...), custom_call_target="tpu_custom_call" | custom-call | flops 3221225472 | bytes 8388608 | tf_op jit(solution)/shard_map/pallas_call | solution.py:391
  66.8 0.6 collective-permute-start.19
  67.4 0.0 collective-permute-done.2.refs_1_
  67.4 0.8 collective-permute-start.20
  68.2 0.0 collective-permute-done.3.refs_2_
  68.2 0.8 collective-permute-start.26
  69.0 0.0 collective-permute-done.4.refs_3_
  69.0 0.5 collective-permute-start.27
  69.5 0.9 %collective-permute-start.28 = (f32[33,8,128]{2,1,0:T(8,128)S(1)}, f32[33,8,128]{2,1,0:T(8,128)S(1)}, u32[]{:S(2)}, u32[]{:S(2)}) collective-permute-start(f32[33,8,128]{2,1,0:T(8,128)S(1)} %get-tuple-element.75), channel_id=1, source_target_pairs={{0,3},{1,2},{2,1},{3,0},{4,7},{5,6},{6,5},{7,4},{8,11},{9,10},{10,... | collective-permute-start | bytes 405512 | tf_op jit(solution)/shard_map/ppermute | solution.py:278
  70.5 2.5 %shard_map.88 = (f32[33,8,128]{2,1,0:T(8,128)S(1)}, f32[33,8,128]{2,1,0:T(8,128)S(1)}, f32[33,8,128]{2,1,0:T(8,128)S(1)}, f32[33,8,128]{2,1,0:T(8,128)S(1)}) custom-call(f32[32,8,128]{2,1,0:T(8,128)S(1)} %get-tuple-element.43.refs_0_, f32[32,8,128]{2,1,0:T(8,128)S(1)} %collective-permute-done.2.refs_1_, f32[32,8,128]{2,1,0:T(8,128)S(1)} %collective-permute-done.3.refs_2_, ...), custom_call_target="tpu_custom_call" | custom-call | flops 3221225472 | bytes 8388608 | tf_op jit(solution)/shard_map/pallas_call | solution.py:391
  73.0 0.8 collective-permute-start.5
  73.7 5.4 %collective-permute-done.27.refs_2_ = f32[33,8,128]{2,1,0:T(8,128)S(1)} collective-permute-done((f32[33,8,128]{2,1,0:T(8,128)S(1)}, f32[33,8,128]{2,1,0:T(8,128)S(1)}, u32[]{:S(2)}, u32[]{:S(2)}) %collective-permute-start.27) | collective-permute-done | bytes 135200 | tf_op jit(solution)/shard_map/ppermute | solution.py:278
  79.1 0.5 collective-permute-start.6
  79.6 0.5 collective-permute-done.28.refs_3_
  80.1 1.9 %collective-permute-start.7 = (f32[33,8,128]{2,1,0:T(8,128)S(1)}, f32[33,8,128]{2,1,0:T(8,128)S(1)}, u32[]{:S(2)}, u32[]{:S(2)}) collective-permute-start(f32[33,8,128]{2,1,0:T(8,128)S(1)} %get-tuple-element.52), channel_id=1, source_target_pairs={{0,3},{1,2},{2,1},{3,0},{4,7},{5,6},{6,5},{7,4},{8,11},{9,10},{10,... | collective-permute-start | bytes 405512 | tf_op jit(solution)/shard_map/ppermute | solution.py:278
  81.9 1.3 %shard_map.95 = (f32[12,4,64,128]{3,2,1,0:T(8,128)}, f32[12,2,2,128]{3,2,1,0:T(2,128)}) custom-call(f32[33,8,128]{2,1,0:T(8,128)S(1)} %get-tuple-element.72.refs_0_, f32[33,8,128]{2,1,0:T(8,128)S(1)} %collective-permute-done.26.refs_1_, f32[33,8,128]{2,1,0:T(8,128)S(1)} %collective-permute-done.27.refs_2_, ...), custom_call_target="tpu_custom_call" | custom-call | flops 100663296 | bytes 1048576 | tf_op jit(solution)/shard_map/pallas_call | solution.py:401
  83.2 1.3 %shard_map.96 = (f32[12,4,64,128]{3,2,1,0:T(8,128)}, f32[12,2,2,128]{3,2,1,0:T(2,128)}) custom-call(f32[33,8,128]{2,1,0:T(8,128)S(1)} %get-tuple-element.62.refs_0_, f32[33,8,128]{2,1,0:T(8,128)S(1)} %collective-permute-done.18.refs_1_, f32[33,8,128]{2,1,0:T(8,128)S(1)} %collective-permute-done.19.refs_2_, ...), custom_call_target="tpu_custom_call", output_to_operand_aliasing={{0}: (7, {}), {1}: (8, {})} | custom-call | flops 100663296 | bytes 1048576 | tf_op jit(solution)/shard_map/pallas_call | solution.py:401
  84.5 0.6 collective-permute-done.6.refs_2_
  85.0 1.0 %collective-permute-done.7.refs_3_ = f32[33,8,128]{2,1,0:T(8,128)S(1)} collective-permute-done((f32[33,8,128]{2,1,0:T(8,128)S(1)}, f32[33,8,128]{2,1,0:T(8,128)S(1)}, u32[]{:S(2)}, u32[]{:S(2)}) %collective-permute-start.7) | collective-permute-done | bytes 135200 | tf_op jit(solution)/shard_map/ppermute | solution.py:278
  86.1 1.3 %shard_map.97 = (f32[12,4,64,128]{3,2,1,0:T(8,128)}, f32[12,2,2,128]{3,2,1,0:T(2,128)}) custom-call(f32[33,8,128]{2,1,0:T(8,128)S(1)} %get-tuple-element.49.refs_0_, f32[33,8,128]{2,1,0:T(8,128)S(1)} %collective-permute-done.5.refs_1_, f32[33,8,128]{2,1,0:T(8,128)S(1)} %collective-permute-done.6.refs_2_, ...), custom_call_target="tpu_custom_call", output_to_operand_aliasing={{0}: (7, {}), {1}: (8, {})} | custom-call | flops 100663296 | bytes 1048576 | tf_op jit(solution)/shard_map/pallas_call | solution.py:401
  (31 shorter events, 0.1 us)
Async XLA Ops:
  0.6 1.4 %copy-start = (f32[12,4,64,128]{3,2,1,0:T(8,128)S(1)}, f32[12,4,64,128]{3,2,1,0:T(8,128)}, u32[]{:S(2)}) copy-start(f32[12,4,64,128]{3,2,1,0:T(8,128)} %state_ref.11) | copy-start | bytes 4718596
  2.3 41.4 %collective-permute-start = (f32[4,2,64,128]{3,2,1,0:T(8,128)S(1)}, f32[4,2,64,128]{3,2,1,0:T(8,128)S(1)}, u32[]{:S(2)}, u32[]{:S(2)}) collective-permute-start(f32[4,2,64,128]{3,2,1,0:T(8,128)S(1)} %get-tuple-element.41), channel_id=1, source_target_pairs={{0,4},{4,0},{8,12},{12,8},{16,20},{20,16},{24,28},{28,24},{1,5},{5... | collective-permute-start | bytes 786440 | tf_op jit(solution)/shard_map/ppermute | solution.py:359
  5.4 37.1 %copy-start.1 = (f32[12,4,64,128]{3,2,1,0:T(8,128)S(1)}, f32[12,4,64,128]{3,2,1,0:T(8,128)}, u32[]{:S(2)}) copy-start(f32[12,4,64,128]{3,2,1,0:T(8,128)} %state_ref.11) | copy-start | bytes 4718596
  5.4 37.1 %copy-start.3 = (bf16[2,256,512]{2,1,0:T(8,128)(2,1)S(1)}, bf16[2,256,512]{2,1,0:T(8,128)(2,1)}, u32[]{:S(2)}) copy-start(bf16[2,256,512]{2,1,0:T(8,128)(2,1)} %constant.10.clone.high_ref) | copy-start | bytes 1572868
  5.4 37.1 %copy-start.4 = (bf16[2,256,512]{2,1,0:T(8,128)(2,1)S(1)}, bf16[2,256,512]{2,1,0:T(8,128)(2,1)}, u32[]{:S(2)}) copy-start(bf16[2,256,512]{2,1,0:T(8,128)(2,1)} %constant.11.clone.low_ref) | copy-start | bytes 1572868
  5.4 39.9 %collective-permute-start.1 = (f32[4,2,64,128]{3,2,1,0:T(8,128)S(1)}, f32[4,2,64,128]{3,2,1,0:T(8,128)S(1)}, u32[]{:S(2)}, u32[]{:S(2)}) collective-permute-start(f32[4,2,64,128]{3,2,1,0:T(8,128)S(1)} %get-tuple-element.42), channel_id=1, source_target_pairs={{0,28},{4,8},{8,4},{12,16},{16,12},{20,24},{24,20},{28,0},{1,29},{... | collective-permute-start | bytes 786440 | tf_op jit(solution)/shard_map/ppermute | solution.py:360
  9.2 29.6 %collective-permute-start.13 = (f32[4,2,64,128]{3,2,1,0:T(8,128)S(1)}, f32[4,2,64,128]{3,2,1,0:T(8,128)S(1)}, u32[]{:S(2)}, u32[]{:S(2)}) collective-permute-start(f32[4,2,64,128]{3,2,1,0:T(8,128)S(1)} %get-tuple-element.56), channel_id=1, source_target_pairs={{0,4},{4,0},{8,12},{12,8},{16,20},{20,16},{24,28},{28,24},{1,5},{5... | collective-permute-start | bytes 786440 | tf_op jit(solution)/shard_map/ppermute | solution.py:359
  9.3 33.1 %collective-permute-start.14 = (f32[4,2,64,128]{3,2,1,0:T(8,128)S(1)}, f32[4,2,64,128]{3,2,1,0:T(8,128)S(1)}, u32[]{:S(2)}, u32[]{:S(2)}) collective-permute-start(f32[4,2,64,128]{3,2,1,0:T(8,128)S(1)} %get-tuple-element.57), channel_id=1, source_target_pairs={{0,28},{4,8},{8,4},{12,16},{16,12},{20,24},{24,20},{28,0},{1,29},{... | collective-permute-start | bytes 786440 | tf_op jit(solution)/shard_map/ppermute | solution.py:360
  11.5 17.3 %collective-permute-start.8 = (f32[24,128]{1,0:T(8,128)S(1)}, f32[24,128]{1,0:T(8,128)S(1)}, u32[]{:S(2)}, u32[]{:S(2)}) collective-permute-start(f32[24,128]{1,0:T(8,128)S(1)} %constant_dynamic-update-slice_fusion), channel_id=1, source_target_pairs={{0,4},{4,0},{8,12},{12,8},{16,20},{20,16},{24,28},{28,24},{1,5},{5... | collective-permute-start | bytes 36872 | tf_op jit(solution)/shard_map/ppermute | solution.py:296
  28.8 3.7 %collective-permute-start.9 = (f32[24,128]{1,0:T(8,128)S(1)}, f32[24,128]{1,0:T(8,128)S(1)}, u32[]{:S(2)}, u32[]{:S(2)}) collective-permute-start(f32[24,128]{1,0:T(8,128)S(1)} %add.15), channel_id=1, source_target_pairs={{0,8},{4,12},{8,0},{12,4},{16,24},{20,28},{24,16},{28,20},{1,9},{5... | collective-permute-start | bytes 36872 | tf_op jit(solution)/shard_map/ppermute | solution.py:296
  32.5 4.6 %collective-permute-start.10 = (f32[24,128]{1,0:T(8,128)S(1)}, f32[24,128]{1,0:T(8,128)S(1)}, u32[]{:S(2)}, u32[]{:S(2)}) collective-permute-start(f32[24,128]{1,0:T(8,128)S(1)} %add.16), channel_id=1, source_target_pairs={{0,16},{4,20},{8,24},{12,28},{16,0},{20,4},{24,8},{28,12},{1,17},{... | collective-permute-start | bytes 36872 | tf_op jit(solution)/shard_map/ppermute | solution.py:296
  37.1 15.4 %collective-permute-start.21 = (f32[4,2,64,128]{3,2,1,0:T(8,128)S(1)}, f32[4,2,64,128]{3,2,1,0:T(8,128)S(1)}, u32[]{:S(2)}, u32[]{:S(2)}) collective-permute-start(f32[4,2,64,128]{3,2,1,0:T(8,128)S(1)} %get-tuple-element.66), channel_id=1, source_target_pairs={{0,4},{4,0},{8,12},{12,8},{16,20},{20,16},{24,28},{28,24},{1,5},{5... | collective-permute-start | bytes 786440 | tf_op jit(solution)/shard_map/ppermute | solution.py:359
  38.8 15.2 %collective-permute-start.22 = (f32[4,2,64,128]{3,2,1,0:T(8,128)S(1)}, f32[4,2,64,128]{3,2,1,0:T(8,128)S(1)}, u32[]{:S(2)}, u32[]{:S(2)}) collective-permute-start(f32[4,2,64,128]{3,2,1,0:T(8,128)S(1)} %get-tuple-element.67), channel_id=1, source_target_pairs={{0,28},{4,8},{8,4},{12,16},{16,12},{20,24},{24,20},{28,0},{1,29},{... | collective-permute-start | bytes 786440 | tf_op jit(solution)/shard_map/ppermute | solution.py:360
  42.4 1.2 %collective-permute-start.11 = (f32[24,128]{1,0:T(8,128)S(1)}, f32[24,128]{1,0:T(8,128)S(1)}, u32[]{:S(2)}, u32[]{:S(2)}) collective-permute-start(f32[24,128]{1,0:T(8,128)S(1)} %add.17), channel_id=1, source_target_pairs={{0,1},{1,0},{2,3},{3,2},{4,5},{5,4},{6,7},{7,6},{8,9},{9,8},{10,11... | collective-permute-start | bytes 36872 | tf_op jit(solution)/shard_map/ppermute | solution.py:296
  43.6 11.3 %collective-permute-start.15 = (f32[32,8,128]{2,1,0:T(8,128)S(1)}, f32[32,8,128]{2,1,0:T(8,128)S(1)}, u32[]{:S(2)}, u32[]{:S(2)}) collective-permute-start(f32[32,8,128]{2,1,0:T(8,128)S(1)} %get-tuple-element.59), channel_id=1, source_target_pairs={{0,1},{1,0},{2,3},{3,2},{4,5},{5,4},{6,7},{7,6},{8,9},{9,8},{10,11... | collective-permute-start | bytes 393224 | tf_op jit(solution)/shard_map/ppermute | solution.py:278
  43.8 11.5 %collective-permute-start.16 = (f32[32,8,128]{2,1,0:T(8,128)S(1)}, f32[32,8,128]{2,1,0:T(8,128)S(1)}, u32[]{:S(2)}, u32[]{:S(2)}) collective-permute-start(f32[32,8,128]{2,1,0:T(8,128)S(1)} %get-tuple-element.60), channel_id=1, source_target_pairs={{0,2},{1,3},{2,0},{3,1},{4,6},{5,7},{6,4},{7,5},{8,10},{9,11},{10,... | collective-permute-start | bytes 393224 | tf_op jit(solution)/shard_map/ppermute | solution.py:278
  45.3 10.5 %collective-permute-start.17 = (f32[32,8,128]{2,1,0:T(8,128)S(1)}, f32[32,8,128]{2,1,0:T(8,128)S(1)}, u32[]{:S(2)}, u32[]{:S(2)}) collective-permute-start(f32[32,8,128]{2,1,0:T(8,128)S(1)} %get-tuple-element.61), channel_id=1, source_target_pairs={{0,3},{1,2},{2,1},{3,0},{4,7},{5,6},{6,5},{7,4},{8,11},{9,10},{10,... | collective-permute-start | bytes 393224 | tf_op jit(solution)/shard_map/ppermute | solution.py:278
  45.5 3.4 %copy-start.2 = (f32[32,256,256]{2,1,0:T(8,128)S(1)}, f32[32,256,256]{2,1,0:T(8,128)}, u32[]{:S(2)}) copy-start(f32[32,256,256]{2,1,0:T(8,128)} %inverse_ref.1) | copy-start | bytes 25165828
  52.4 14.3 %collective-permute-start.12 = (f32[24,128]{1,0:T(8,128)S(1)}, f32[24,128]{1,0:T(8,128)S(1)}, u32[]{:S(2)}, u32[]{:S(2)}) collective-permute-start(f32[24,128]{1,0:T(8,128)S(1)} %add.18), channel_id=1, source_target_pairs={{0,2},{1,3},{2,0},{3,1},{4,6},{5,7},{6,4},{7,5},{8,10},{9,11},{10,... | collective-permute-start | bytes 36872 | tf_op jit(solution)/shard_map/ppermute | solution.py:296
  54.0 2.8 %copy-start.7 = (f32[8,256]{1,0:T(8,128)S(1)}, f32[8,256]{1,0:T(8,128)}, u32[]{:S(2)}) copy-start(f32[8,256]{1,0:T(8,128)} %constant.14.clone.refs_6_) | copy-start | bytes 24580
  54.0 13.3 %collective-permute-start.2 = (f32[32,8,128]{2,1,0:T(8,128)S(1)}, f32[32,8,128]{2,1,0:T(8,128)S(1)}, u32[]{:S(2)}, u32[]{:S(2)}) collective-permute-start(f32[32,8,128]{2,1,0:T(8,128)S(1)} %get-tuple-element.44), channel_id=1, source_target_pairs={{0,1},{1,0},{2,3},{3,2},{4,5},{5,4},{6,7},{7,6},{8,9},{9,8},{10,11... | collective-permute-start | bytes 393224 | tf_op jit(solution)/shard_map/ppermute | solution.py:278
  54.9 4.4 %collective-permute-start.23 = (f32[32,8,128]{2,1,0:T(8,128)S(1)}, f32[32,8,128]{2,1,0:T(8,128)S(1)}, u32[]{:S(2)}, u32[]{:S(2)}) collective-permute-start(f32[32,8,128]{2,1,0:T(8,128)S(1)} %get-tuple-element.69), channel_id=1, source_target_pairs={{0,1},{1,0},{2,3},{3,2},{4,5},{5,4},{6,7},{7,6},{8,9},{9,8},{10,11... | collective-permute-start | bytes 393224 | tf_op jit(solution)/shard_map/ppermute | solution.py:278
  55.3 6.4 %collective-permute-start.24 = (f32[32,8,128]{2,1,0:T(8,128)S(1)}, f32[32,8,128]{2,1,0:T(8,128)S(1)}, u32[]{:S(2)}, u32[]{:S(2)}) collective-permute-start(f32[32,8,128]{2,1,0:T(8,128)S(1)} %get-tuple-element.70), channel_id=1, source_target_pairs={{0,2},{1,3},{2,0},{3,1},{4,6},{5,7},{6,4},{7,5},{8,10},{9,11},{10,... | collective-permute-start | bytes 393224 | tf_op jit(solution)/shard_map/ppermute | solution.py:278
  55.8 7.1 %collective-permute-start.25 = (f32[32,8,128]{2,1,0:T(8,128)S(1)}, f32[32,8,128]{2,1,0:T(8,128)S(1)}, u32[]{:S(2)}, u32[]{:S(2)}) collective-permute-start(f32[32,8,128]{2,1,0:T(8,128)S(1)} %get-tuple-element.71), channel_id=1, source_target_pairs={{0,3},{1,2},{2,1},{3,0},{4,7},{5,6},{6,5},{7,4},{8,11},{9,10},{10,... | collective-permute-start | bytes 393224 | tf_op jit(solution)/shard_map/ppermute | solution.py:278
  59.3 8.9 %collective-permute-start.3 = (f32[32,8,128]{2,1,0:T(8,128)S(1)}, f32[32,8,128]{2,1,0:T(8,128)S(1)}, u32[]{:S(2)}, u32[]{:S(2)}) collective-permute-start(f32[32,8,128]{2,1,0:T(8,128)S(1)} %get-tuple-element.45), channel_id=1, source_target_pairs={{0,2},{1,3},{2,0},{3,1},{4,6},{5,7},{6,4},{7,5},{8,10},{9,11},{10,... | collective-permute-start | bytes 393224 | tf_op jit(solution)/shard_map/ppermute | solution.py:278
  61.6 7.4 %collective-permute-start.4 = (f32[32,8,128]{2,1,0:T(8,128)S(1)}, f32[32,8,128]{2,1,0:T(8,128)S(1)}, u32[]{:S(2)}, u32[]{:S(2)}) collective-permute-start(f32[32,8,128]{2,1,0:T(8,128)S(1)} %get-tuple-element.46), channel_id=1, source_target_pairs={{0,3},{1,2},{2,1},{3,0},{4,7},{5,6},{6,5},{7,4},{8,11},{9,10},{10,... | collective-permute-start | bytes 393224 | tf_op jit(solution)/shard_map/ppermute | solution.py:278
  62.8 6.7 %collective-permute-start.18 = (f32[33,8,128]{2,1,0:T(8,128)S(1)}, f32[33,8,128]{2,1,0:T(8,128)S(1)}, u32[]{:S(2)}, u32[]{:S(2)}) collective-permute-start(f32[33,8,128]{2,1,0:T(8,128)S(1)} %get-tuple-element.63), channel_id=1, source_target_pairs={{0,1},{1,0},{2,3},{3,2},{4,5},{5,4},{6,7},{7,6},{8,9},{9,8},{10,11... | collective-permute-start | bytes 405512 | tf_op jit(solution)/shard_map/ppermute | solution.py:278
  66.8 16.4 %collective-permute-start.19 = (f32[33,8,128]{2,1,0:T(8,128)S(1)}, f32[33,8,128]{2,1,0:T(8,128)S(1)}, u32[]{:S(2)}, u32[]{:S(2)}) collective-permute-start(f32[33,8,128]{2,1,0:T(8,128)S(1)} %get-tuple-element.64), channel_id=1, source_target_pairs={{0,2},{1,3},{2,0},{3,1},{4,6},{5,7},{6,4},{7,5},{8,10},{9,11},{10,... | collective-permute-start | bytes 405512 | tf_op jit(solution)/shard_map/ppermute | solution.py:278
  67.4 15.8 %collective-permute-start.20 = (f32[33,8,128]{2,1,0:T(8,128)S(1)}, f32[33,8,128]{2,1,0:T(8,128)S(1)}, u32[]{:S(2)}, u32[]{:S(2)}) collective-permute-start(f32[33,8,128]{2,1,0:T(8,128)S(1)} %get-tuple-element.65), channel_id=1, source_target_pairs={{0,3},{1,2},{2,1},{3,0},{4,7},{5,6},{6,5},{7,4},{8,11},{9,10},{10,... | collective-permute-start | bytes 405512 | tf_op jit(solution)/shard_map/ppermute | solution.py:278
  68.2 4.7 %collective-permute-start.26 = (f32[33,8,128]{2,1,0:T(8,128)S(1)}, f32[33,8,128]{2,1,0:T(8,128)S(1)}, u32[]{:S(2)}, u32[]{:S(2)}) collective-permute-start(f32[33,8,128]{2,1,0:T(8,128)S(1)} %get-tuple-element.73), channel_id=1, source_target_pairs={{0,1},{1,0},{2,3},{3,2},{4,5},{5,4},{6,7},{7,6},{8,9},{9,8},{10,11... | collective-permute-start | bytes 405512 | tf_op jit(solution)/shard_map/ppermute | solution.py:278
  69.0 10.1 %collective-permute-start.27 = (f32[33,8,128]{2,1,0:T(8,128)S(1)}, f32[33,8,128]{2,1,0:T(8,128)S(1)}, u32[]{:S(2)}, u32[]{:S(2)}) collective-permute-start(f32[33,8,128]{2,1,0:T(8,128)S(1)} %get-tuple-element.74), channel_id=1, source_target_pairs={{0,2},{1,3},{2,0},{3,1},{4,6},{5,7},{6,4},{7,5},{8,10},{9,11},{10,... | collective-permute-start | bytes 405512 | tf_op jit(solution)/shard_map/ppermute | solution.py:278
  69.5 10.6 %collective-permute-start.28 = (f32[33,8,128]{2,1,0:T(8,128)S(1)}, f32[33,8,128]{2,1,0:T(8,128)S(1)}, u32[]{:S(2)}, u32[]{:S(2)}) collective-permute-start(f32[33,8,128]{2,1,0:T(8,128)S(1)} %get-tuple-element.75), channel_id=1, source_target_pairs={{0,3},{1,2},{2,1},{3,0},{4,7},{5,6},{6,5},{7,4},{8,11},{9,10},{10,... | collective-permute-start | bytes 405512 | tf_op jit(solution)/shard_map/ppermute | solution.py:278
  70.4 11.5 %copy-start.5 = (bf16[128,128]{1,0:T(8,128)(2,1)S(1)}, bf16[128,128]{1,0:T(8,128)(2,1)}, u32[]{:S(2)}) copy-start(bf16[128,128]{1,0:T(8,128)(2,1)} %constant.12.clone.refs_4_) | copy-start | bytes 98308
  70.5 11.5 %copy-start.6 = (bf16[128,128]{1,0:T(8,128)(2,1)S(1)}, bf16[128,128]{1,0:T(8,128)(2,1)}, u32[]{:S(2)}) copy-start(bf16[128,128]{1,0:T(8,128)(2,1)} %constant.13.clone.refs_5_) | copy-start | bytes 98308
  73.0 11.5 %collective-permute-start.5 = (f32[33,8,128]{2,1,0:T(8,128)S(1)}, f32[33,8,128]{2,1,0:T(8,128)S(1)}, u32[]{:S(2)}, u32[]{:S(2)}) collective-permute-start(f32[33,8,128]{2,1,0:T(8,128)S(1)} %get-tuple-element.50), channel_id=1, source_target_pairs={{0,1},{1,0},{2,3},{3,2},{4,5},{5,4},{6,7},{7,6},{8,9},{9,8},{10,11... | collective-permute-start | bytes 405512 | tf_op jit(solution)/shard_map/ppermute | solution.py:278
  79.1 5.9 %collective-permute-start.6 = (f32[33,8,128]{2,1,0:T(8,128)S(1)}, f32[33,8,128]{2,1,0:T(8,128)S(1)}, u32[]{:S(2)}, u32[]{:S(2)}) collective-permute-start(f32[33,8,128]{2,1,0:T(8,128)S(1)} %get-tuple-element.51), channel_id=1, source_target_pairs={{0,2},{1,3},{2,0},{3,1},{4,6},{5,7},{6,4},{7,5},{8,10},{9,11},{10,... | collective-permute-start | bytes 405512 | tf_op jit(solution)/shard_map/ppermute | solution.py:278
  80.1 6.0 %collective-permute-start.7 = (f32[33,8,128]{2,1,0:T(8,128)S(1)}, f32[33,8,128]{2,1,0:T(8,128)S(1)}, u32[]{:S(2)}, u32[]{:S(2)}) collective-permute-start(f32[33,8,128]{2,1,0:T(8,128)S(1)} %get-tuple-element.52), channel_id=1, source_target_pairs={{0,3},{1,2},{2,1},{3,0},{4,7},{5,6},{6,5},{7,4},{8,11},{9,10},{10,... | collective-permute-start | bytes 405512 | tf_op jit(solution)/shard_map/ppermute | solution.py:278

commit v4 on v3

v4 whole, which is shorter than its diff:
```python
import functools
import math

import jax
import jax.numpy as jnp
import numpy as np
from jax import lax
from jax.experimental import pallas as pl
from jax.experimental.pallas import tpu as pltpu
from jax.sharding import PartitionSpec as P


MODES = 128
HALO = 64

EPSILON = 1e-06
TIME_STEP = 0.5
MEAN_FLOW = 0.8
CORIOLIS = 0.6
STRATIFICATION = 0.9

LANES = 128
MIB = 1 << 20
TILE = 8
VMEM = pl.BlockSpec(memory_space=pltpu.VMEM)
ANY = pl.BlockSpec(memory_space=pl.ANY)
NT = (((1,), (1,)), ((), ()))
NN = (((1,), (0,)), ((), ()))


def window_tables(window, rim_width, points, mode_count):
    position = np.arange(window)
    mode_index = np.arange(mode_count)
    half_count = mode_count // 2
    is_cosine = mode_index <= half_count
    wave_index = np.where(is_cosine, mode_index, mode_index - half_count)
    product_index = position[:, None] * wave_index[None, :] % window
    phases = 2.0 * np.pi * product_index / window
    weights_norm = np.where(wave_index == 0, np.sqrt(1.0 / window), np.sqrt(2.0 / window))
    basis = np.where(is_cosine[None, :], np.cos(phases), np.sin(phases)) * weights_norm[None, :]
    wavenumber = 2.0 * np.pi * wave_index / window
    paired = wave_index[:, None] == wave_index[None, :]
    to_sine = is_cosine[:, None] & ~is_cosine[None, :] & paired
    to_cosine = ~is_cosine[:, None] & is_cosine[None, :] & paired
    derivative = np.where(to_sine, -wavenumber[:, None], 0.0) + np.where(
        to_cosine, wavenumber[:, None], 0.0
    )
    taper = 0.25 + 0.75 * np.sin(np.pi * (position + 0.5) / window) ** 2
    values = basis * taper[:, None]
    slopes = (basis @ derivative) * taper[:, None]
    back_table = (
        basis[rim_width : rim_width + points, :] / taper[rim_width : rim_width + points, None]
    ).T
    return values, slopes, back_table


def step_tables(values, slopes, rim, points):
    direct = values - TIME_STEP * MEAN_FLOW * slopes
    couplings = (
        (TIME_STEP * CORIOLIS, -TIME_STEP * CORIOLIS),
        (TIME_STEP, -TIME_STEP * STRATIFICATION),
    )
    tables = []
    for to_first, to_second in couplings:
        first = (direct, to_first * values)
        second = (to_second * values, direct)
        rows = []
        for part in (first, second):
            pieces = []
            for begin, end in ((rim, rim + points), (0, rim), (rim + points, points + 2 * rim)):
                pieces += [part[0][begin:end].T, part[1][begin:end].T]
            rows.append(np.concatenate(pieces, axis=1))
        tables.append(np.concatenate(rows, axis=0))
    return np.stack(tables)


def split_table(table):
    table = np.asarray(table, np.float32)
    high = table.astype(jnp.bfloat16)
    low = (table - high.astype(np.float32)).astype(jnp.bfloat16)
    return jnp.asarray(high), jnp.asarray(low)


def split(x):
    high = x.astype(jnp.bfloat16)
    low = (x - high.astype(jnp.float32)).astype(jnp.bfloat16)
    return high, low


def dot(a, b, dims):
    return lax.dot_general(a, b, dims, preferred_element_type=jnp.float32)


def left_lanes(shape):
    return lax.broadcasted_iota(jnp.int32, shape, len(shape) - 1) < LANES // 2


def swap(x):
    return pltpu.roll(x, LANES // 2, len(x.shape) - 1)


def pack_kernel(base, state_ref, near_ref, far_ref):
    rows = state_ref.shape[2]
    even = jnp.bitwise_and(lax.axis_index("gx"), 1) == 0
    left = left_lanes((rows, LANES))
    for e in range(near_ref.shape[0]):
        for p in range(2):
            a = state_ref[base + e, p]
            b = state_ref[base + e, p + 2]
            last = jnp.where(left, swap(a), b)
            first = jnp.where(left, a, swap(b))
            near_ref[e, p] = jnp.where(even, last, first)
            far_ref[e, p] = jnp.where(even, first, last)


def squares_kernel(state_ref, sums_ref):
    members, fields, rows, _ = state_ref.shape
    half = left_lanes((fields, LANES))
    for q in range(members // 2):
        totals = []
        for e in range(2):
            acc = jnp.zeros((rows, LANES), jnp.float32)
            for f in range(fields):
                a = state_ref[2 * q + e, f]
                acc += a * a
            totals.append(jnp.sum(acc))
        sums_ref[fields * q : fields * (q + 1)] = jnp.where(half, totals[0], totals[1])


def peers(parts):
    me = lax.axis_index("gy")
    return [jnp.bitwise_xor(me, d) for d in range(parts)]


def reorder_lanes(x):
    me = lax.axis_index("gy")
    far = jnp.bitwise_and(me, 2) != 0
    near = jnp.bitwise_and(me, 1) != 0
    a, b = x[..., :LANES], x[..., LANES:]
    a, b = jnp.where(far, b, a), jnp.where(far, a, b)
    return jnp.where(near, swap(a), a), jnp.where(near, swap(b), b)


def split_kernel(inverse_ref, high_ref, low_ref):
    coef_count = inverse_ref.shape[1]
    coef = LANES // 2
    for d, peer in enumerate(peers(coef_count // coef)):
        rows = pl.ds(pl.multiple_of(peer * coef, coef), coef)
        for h, x in enumerate(reorder_lanes(inverse_ref[:, rows, :])):
            at = (slice(None), slice(d * coef, (d + 1) * coef), slice(h * LANES, (h + 1) * LANES))
            high_ref[at], low_ref[at] = split(x)


def project_kernel(base, state_ref, near_ref, far_ref, high_ref, low_ref, *out_refs):
    parts = len(out_refs)
    members, _, coef, _ = near_ref.shape
    rows = 2 * members
    slots = out_refs[0].shape[0] // rows
    count = slots * parts
    lane = lax.broadcasted_iota(jnp.int32, (1, members * coef), 1)
    index = lax.axis_index("gy") * coef + lax.rem(lane, coef)
    interior = index < coef * parts - 2
    even = jnp.bitwise_and(lax.axis_index("gx"), 1) == 0
    where = [pl.multiple_of(peer * slots, slots) for peer in peers(parts)]
    for p in range(2):
        near = near_ref[:, p].reshape(members * coef, LANES)
        far = far_ref[:, p].reshape(members * coef, LANES)
        x = jnp.concatenate(
            [
                state_ref[base : base + members, p].reshape(members * coef, LANES),
                state_ref[base : base + members, p + 2].reshape(members * coef, LANES),
                jnp.where(even, far, near),
                jnp.where(even, near, far),
            ],
            axis=1,
        )
        x_high, x_low = split(x)
        w_high, w_low = [
            jnp.concatenate(
                [ref[p, pl.ds(f * count + at, slots), :] for f in range(2) for at in where], axis=0
            )
            for ref in (high_ref, low_ref)
        ]
        t = dot(w_high, x_high, NT) + (dot(w_high, x_low, NT) + dot(w_low, x_high, NT))
        t = jnp.where(interior, t, 0.0)
        for d in range(parts):
            for f in range(2):
                first = f * count + d * slots
                for q in range(members // 2):
                    out_refs[d][pl.ds(4 * q + p + 2 * f, slots, stride=rows), :] = t[
                        first : first + slots, q * LANES : (q + 1) * LANES
                    ]


def solve_kernel(parts, rows, *refs):
    recv_refs = refs[:parts]
    high_refs, low_refs = refs[parts : parts + 2], refs[parts + 2 : parts + 4]
    wall_ref = refs[parts + 4]
    out_refs = refs[parts + 5 :]
    slots = recv_refs[0].shape[0] // rows
    modes = TILE // math.gcd(rows, TILE)
    unit = rows * modes
    left = left_lanes((unit, LANES))
    lane = lax.broadcasted_iota(jnp.int32, (unit, LANES), 1)
    mode = lax.broadcasted_iota(jnp.int32, (unit, LANES), 0) // rows
    wall = jnp.concatenate(reorder_lanes(wall_ref[...]), axis=1)
    sums = jnp.zeros((unit, LANES), jnp.float32)
    for i in range(slots // modes):
        tile = slice(i * unit, (i + 1) * unit)
        t = [ref[tile] for ref in recv_refs]
        even, odd = [], []
        for d in range(0, parts, 2):
            even.append(jnp.where(left, t[d], swap(t[d + 1])))
            odd.append(jnp.where(left, swap(t[d]), t[d + 1]))
        even = jnp.concatenate(even, axis=1)
        odd = jnp.concatenate(odd, axis=1)
        solved = []
        for j in range(modes):
            r = jnp.concatenate([x[j * rows : (j + 1) * rows] for x in (even, odd)], axis=0)
            half, at = divmod(i * modes + j, high_refs[0].shape[0])
            v_high = high_refs[half][at]
            v_low = low_refs[half][at]
            r_high, r_low = split(r)
            both = dot(jnp.concatenate([r_high, r_low], axis=0), v_high, NT)
            solved.append(both[: 2 * rows] + (both[2 * rows :] + dot(r_high, v_low, NT)))
        even = jnp.concatenate([o[:rows] for o in solved], axis=0)
        odd = jnp.concatenate([o[rows:] for o in solved], axis=0)
        for d in range(0, parts, 2):
            a = even[:, d * LANES // 2 : d * LANES // 2 + LANES]
            b = odd[:, d * LANES // 2 : d * LANES // 2 + LANES]
            out_refs[d][tile] = jnp.where(left, a, swap(b))
            out_refs[d + 1][tile] = jnp.where(left, swap(a), b)
        for e, o in enumerate((even, odd)):
            for w in range(2):
                q = jnp.sum(o * wall[w : w + 1], axis=1, keepdims=True)
                sums = jnp.where(lane == (2 * e + w) * slots + i * modes + mode, q, sums)
    total = sums[:rows]
    for j in range(1, modes):
        total = total + sums[j * rows : (j + 1) * rows]
    for ref in out_refs:
        ref[slots * rows : slots * rows + rows] = total
        if rows % TILE:
            spare = ref.shape[0] - (slots + 1) * rows
            ref[(slots + 1) * rows :] = jnp.zeros((spare, LANES), jnp.float32)


def back_kernel(count, first, slots, parts, *refs):
    recv_refs = refs[:parts]
    high_ref, low_ref, sums_ref = refs[parts : parts + 3]
    out_ref, wall_ref, values_ref, stress_ref, sems = refs[-5:]
    members, fields, coef, _ = values_ref.shape
    rows = 2 * members
    base = 2 * first
    where = [pl.multiple_of(peer * slots, slots) for peer in peers(parts)]
    b_high, b_low = [
        jnp.concatenate([ref[pl.ds(at, slots), :] for at in where], axis=0)
        for ref in (high_ref, low_ref)
    ]
    scale = lax.rsqrt(sums_ref[base : base + rows] / count + EPSILON)
    copies = []
    for r in range(rows):
        q, f = divmod(r, fields)
        s = jnp.concatenate([ref[pl.ds(r, slots, stride=rows), :] for ref in recv_refs], axis=0)
        s = (s * scale[r : r + 1]).T
        s_high, s_low = split(s)
        o = dot(s_high, b_high, NN) + (dot(s_high, b_low, NN) + dot(s_low, b_high, NN))
        for e in range(2):
            values_ref[2 * q + e, f] = o[e * coef : (e + 1) * coef]
        if f == fields - 1:
            pair = pl.ds(2 * q, 2)
            copies.append(
                pltpu.make_async_copy(
                    values_ref.at[pair], out_ref.at[pl.ds(first + 2 * q, 2)], sems.at[q]
                )
            )
            copies[-1].start()
    me = lax.axis_index("gy")
    near = jnp.bitwise_and(me, 1) != 0
    far = jnp.bitwise_and(me, 2) != 0
    lane = lax.broadcasted_iota(jnp.int32, (rows, LANES), 1)
    tiles = [ref[slots * rows : slots * rows + rows] for ref in recv_refs]
    tiles = [jnp.where(near, tiles[d ^ 1], tiles[d]) for d in range(parts)]
    tiles = [jnp.where(far, tiles[d ^ 2], tiles[d]) * scale for d in range(parts)]
    b_high = high_ref[...]
    b_low = low_ref[...]
    for e in range(2):
        for w in range(2):
            g = jnp.zeros((rows, LANES), jnp.float32)
            for k in range(parts):
                shift = (k * slots - (e * 2 + w) * slots) % LANES
                tile = pltpu.roll(tiles[k], shift, 1) if shift else tiles[k]
                g = jnp.where((lane >= k * slots) & (lane < (k + 1) * slots), tile, g)
            g_high, g_low = split(g)
            o = dot(g_high, b_high, NN) + (dot(g_high, b_low, NN) + dot(g_low, b_high, NN))
            for q in range(members // 2):
                for c in range(2):
                    row = fields * q + 2 * c
                    stress_ref[2 * q + e, w, c : c + 1] = o[row : row + 1]
    copies.append(
        pltpu.make_async_copy(
            stress_ref, wall_ref.at[pl.ds(first, members)], sems.at[members // 2]
        )
    )
    copies[-1].start()
    for copy in copies:
        copy.wait()


def exchanged(pieces, axis):
    n = lax.axis_size(axis)
    got = list(pieces)
    for d in range(n - 1, 0, -1):
        got[d] = lax.ppermute(pieces[d], axis, [(i, i ^ d) for i in range(n)])
    return got


def halo_pairs(n):
    near = [(i, i ^ 1) for i in range(n)]
    far = [(i, (i + (1 if i % 2 else -1)) % n) for i in range(n)]
    return near, far


def axis_hops(n):
    return [1 << i for i in range(n.bit_length() - 1)]


def full_sum(x):
    for axis in ("gy", "gx"):
        n = lax.axis_size(axis)
        for hop in axis_hops(n):
            other = lax.ppermute(x, axis, [(i, i ^ hop) for i in range(n)])
            x = x + other
    return x


SIZES = (4, 4, 4)


def chunks(members):
    sizes = SIZES if sum(SIZES) == members else (2,) * (members // 2)
    return [(sum(sizes[:g]), count) for g, count in enumerate(sizes)]


def per_device(state, inverse):
    members, fields, coef, points = state.shape
    parts = lax.axis_size("gy")
    coef_count = coef * parts
    grid_x = points * lax.axis_size("gx")
    window = points + 2 * HALO
    mine = MODES // parts
    plan = chunks(members)

    values, slopes, back_table = window_tables(window, HALO, points, MODES)
    step_high, step_low = split_table(step_tables(values, slopes, HALO, points))
    back_high, back_low = split_table(back_table)
    k = np.arange(coef_count)
    curvature = k * k / (coef_count * coef_count)
    wall = np.zeros((TILE, coef_count), np.float32)
    wall[0] = curvature
    wall[1] = np.where(k % 2 == 0, -1.0, 1.0) * curvature
    wall = jnp.asarray(wall)

    def call(kernel, vmem, flops, moved, **kwargs):
        return pl.pallas_call(
            kernel,
            compiler_params=pltpu.CompilerParams(vmem_limit_bytes=vmem * MIB),
            cost_estimate=pl.CostEstimate(flops=flops, bytes_accessed=moved, transcendentals=0),
            **kwargs,
        )

    def array(*shape):
        return jax.ShapeDtypeStruct(shape, jnp.float32)

    member_bytes = 4 * fields * coef * points
    packed = []
    for first, count in plan:
        packed.append(
            call(
                functools.partial(pack_kernel, first),
                6,
                10**6,
                2 * count * member_bytes,
                in_specs=[VMEM],
                out_specs=[VMEM] * 2,
                out_shape=[array(count, 2, coef, LANES)] * 2,
            )(state)
        )
    squares = call(
        squares_kernel,
        6,
        10**9,
        10**7,
        in_specs=[VMEM],
        out_specs=VMEM,
        out_shape=array(2 * members, LANES),
    )(state)
    halos = []
    near_pairs, far_pairs = halo_pairs(lax.axis_size("gx"))
    for near, far in packed:
        near = lax.ppermute(near, "gx", near_pairs)
        far = lax.ppermute(far, "gx", far_pairs)
        halos.append((near, far))
    sums = full_sum(squares)

    per_step = 4
    steps = mine // per_step // 2
    split_shape = (per_step, coef_count, coef_count)
    high, low = [], []
    for h in range(2):
        out = call(
            split_kernel,
            8,
            10**7,
            4 * mine * coef_count**2,
            grid=(steps,),
            in_specs=[pl.BlockSpec(split_shape, lambda i, h=h: (h * steps + i, 0, 0))],
            out_specs=[pl.BlockSpec(split_shape, lambda i: (i, 0, 0))] * 2,
            out_shape=[jax.ShapeDtypeStruct((mine // 2,) + split_shape[1:], jnp.bfloat16)] * 2,
        )(inverse)
        high.append(out[0])
        low.append(out[1])

    outputs = []
    for g, (first, count) in enumerate(plan):
        rows = count * fields // 2
        sent = call(
            functools.partial(project_kernel, first),
            8,
            3 * 2 * 2 * (2 * MODES) * (4 * LANES) * count * coef,
            3 * count * member_bytes,
            in_specs=[VMEM] * 5,
            out_specs=[VMEM] * parts,
            out_shape=[array(mine * rows, LANES)] * parts,
        )(state, *halos[g], step_high, step_low)
        got = exchanged(sent, "gy")
        solved = call(
            functools.partial(solve_kernel, parts, rows),
            6,
            3 * 2 * mine * coef_count**2 * 256,
            4 * mine * coef_count**2,
            in_specs=[VMEM] * (parts + 5),
            out_specs=[VMEM] * parts,
            out_shape=[array((mine + 1) * rows + -(mine + 1) * rows % TILE, LANES)] * parts,
        )(*got, *high, *low, wall)
        returned = exchanged(solved, "gy")

        outputs = call(
            functools.partial(
                back_kernel, float(fields * coef_count * grid_x), first, mine, parts
            ),
            8,
            3 * 2 * MODES * points * count * fields * coef,
            2 * count * member_bytes,
            in_specs=[VMEM] * (parts + 3) + [ANY] * len(outputs),
            out_specs=[ANY] * 2,
            out_shape=[array(*state.shape), array(members, 2, 2, points)],
            scratch_shapes=[
                pltpu.VMEM((count, fields, coef, points), jnp.float32),
                pltpu.VMEM((count, 2, 2, points), jnp.float32),
                pltpu.SemaphoreType.DMA((count // 2 + 1,)),
            ],
            input_output_aliases={parts + 3 + i: i for i in range(len(outputs))},
        )(*returned, back_high, back_low, sums, *outputs)
    return tuple(outputs)


def solution(mesh):
    placed = (P(None, None, "gy", "gx"), P("gy", None, None))

    return jax.shard_map(
        per_device,
        mesh=mesh,
        in_specs=placed,
        out_specs=(P(None, None, "gy", "gx"), P(None, None, None, "gx")),
        check_vma=False,
    )
```

time: 87.8 us -> 82.9 us (0.944)
  waiting for transfers between devices: 31.2 us -> 28.4 us
  starting transfers between devices: 33.6 us -> 31.7 us
    ppermute x5, starting transfers between devices: 6.91 us -> 3.77 us  [full_sum(): other = lax.ppermute(x, axis, [(i, i ^ hop) for i in range(n)])]
    ppermute x5, waiting for transfers between devices: 20.7 us -> 19 us  [full_sum(): other = lax.ppermute(x, axis, [(i, i ^ hop) for i in range(n)])]
    ppermute x18, starting transfers between devices: 12.8 us -> 14.1 us  [exchanged(): got[d] = lax.ppermute(pieces[d], axis, [(i, i ^ d) for i in range(n)])]
    ppermute x18, waiting for transfers between devices: 10.4 us -> 9.36 us  [exchanged(): got[d] = lax.ppermute(pieces[d], axis, [(i, i ^ d) for i in range(n)])]
    pallas_call x10 -> x12, Pallas kernels: 13.1 us -> 13.2 us  [the longest x3 7.52 us: per_device(): call(functools.partial(solve_kernel, parts, rows), 6, 3 * 2 * mine * coef...]
    unnamed x18 -> x16, local copies, waits for them, and re-layouts: 4.81 us -> 4.82 us
  transfers between devices with their start and end apart: 29 -> 29, of which waited for: 10 -> 9; matrix products, arithmetic and copies ran while one was open for 0% -> 0% of each run, Pallas kernels for 18% -> 19%
where the time goes in v4:
time: 82.9 us; the launch traced here: 82.6 us
  starting transfers between devices  31.7 us (38%)
  waiting for transfers between devices  28.4 us (34%)
  Pallas kernels  16.8 us (20%)
  local copies, waits for them, and re-layouts  4.82 us (6%)
  between operations  0.94 us (1%)
    ppermute x5, waiting for transfers between devices, full_sum(): other = lax.ppermute(x, axis, [(i, i ^ hop) for i in range(n)])  19 us
    ppermute x18, starting transfers between devices, exchanged(): got[d] = lax.ppermute(pieces[d], axis, [(i, i ^ d) for i in range(n)])  14.1 us
    ppermute x18, waiting for transfers between devices, exchanged(): got[d] = lax.ppermute(pieces[d], axis, [(i, i ^ d) for i in range(n)])  9.36 us
    ppermute x3, starting transfers between devices, per_device(): far = lax.ppermute(far, 'gx', far_pairs)  9.02 us
    pallas_call x3, Pallas kernels, per_device(): call(functools.partial(solve_kernel, parts, rows), 6, 3 * 2 * mine * coef...  7.52 us
    ppermute x3, starting transfers between devices, per_device(): near = lax.ppermute(near, 'gx', near_pairs)  4.84 us
    unnamed x16, local copies, waits for them, and re-layouts  4.82 us
    ppermute x5, starting transfers between devices, full_sum(): other = lax.ppermute(x, axis, [(i, i ^ hop) for i in range(n)])  3.77 us
  transfers between devices with their start and end apart: 29, of which 9 were waited for; matrix products, arithmetic and copies ran while one was open for 0% of the time, Pallas kernels for 19%

profile of v4, /device:TPU:0, one launch (start us, length us, event | category | flops | bytes accessed | tf_op | source)
XLA Modules:
  0.0 82.6 jit_solution(9401847983791576442)
XLA Ops:
  0.6 0.0 copy-start
  0.6 1.4 %copy-done = f32[12,4,64,128]{3,2,1,0:T(8,128)S(1)} copy-done((f32[12,4,64,128]{3,2,1,0:T(8,128)S(1)}, f32[12,4,64,128]{3,2,1,0:T(8,128)}, u32[]{:S(2)}) %copy-start) | copy-done | bytes 1572888
  2.0 0.2 shard_map.92
  2.2 3.0 %collective-permute-start.13 = (f32[4,2,64,128]{3,2,1,0:T(8,128)S(1)}, f32[4,2,64,128]{3,2,1,0:T(8,128)S(1)}, u32[]{:S(2)}, u32[]{:S(2)}) collective-permute-start(f32[4,2,64,128]{3,2,1,0:T(8,128)S(1)} %get-tuple-element.54), channel_id=1, source_target_pairs={{0,4},{4,0},{8,12},{12,8},{16,20},{20,16},{24,28},{28,24},{1,5},{5... | collective-permute-start | bytes 786440 | tf_op jit(solution)/shard_map/ppermute | solution.py:400
  5.3 3.6 %collective-permute-start.14 = (f32[4,2,64,128]{3,2,1,0:T(8,128)S(1)}, f32[4,2,64,128]{3,2,1,0:T(8,128)S(1)}, u32[]{:S(2)}, u32[]{:S(2)}) collective-permute-start(f32[4,2,64,128]{3,2,1,0:T(8,128)S(1)} %get-tuple-element.55), channel_id=1, source_target_pairs={{0,28},{4,8},{8,4},{12,16},{16,12},{20,24},{24,20},{28,0},{1,29},{... | collective-permute-start | bytes 786440 | tf_op jit(solution)/shard_map/ppermute | solution.py:401
  8.9 0.2 shard_map.86
  9.1 0.0 copy-start.1
  9.1 0.1 collective-permute-start
  9.1 0.0 copy-start.3
  9.2 0.0 copy-start.4
  9.2 1.9 %collective-permute-start.1 = (f32[4,2,64,128]{3,2,1,0:T(8,128)S(1)}, f32[4,2,64,128]{3,2,1,0:T(8,128)S(1)}, u32[]{:S(2)}, u32[]{:S(2)}) collective-permute-start(f32[4,2,64,128]{3,2,1,0:T(8,128)S(1)} %get-tuple-element.41), channel_id=1, source_target_pairs={{0,28},{4,8},{8,4},{12,16},{16,12},{20,24},{24,20},{28,0},{1,29},{... | collective-permute-start | bytes 786440 | tf_op jit(solution)/shard_map/ppermute | solution.py:401
  11.1 0.2 shard_map.91
  11.3 0.1 collective-permute-start.8
  11.4 1.2 %collective-permute-done.8 = f32[24,128]{1,0:T(8,128)S(1)} collective-permute-done((f32[24,128]{1,0:T(8,128)S(1)}, f32[24,128]{1,0:T(8,128)S(1)}, u32[]{:S(2)}, u32[]{:S(2)}) %collective-permute-start.8) | collective-permute-done | bytes 12320 | tf_op jit(solution)/shard_map/ppermute | solution.py:331
  12.5 1.5 %collective-permute-start.9 = (f32[24,128]{1,0:T(8,128)S(1)}, f32[24,128]{1,0:T(8,128)S(1)}, u32[]{:S(2)}, u32[]{:S(2)}) collective-permute-start(f32[24,128]{1,0:T(8,128)S(1)} %add.15), channel_id=1, source_target_pairs={{0,2},{1,3},{2,0},{3,1},{4,6},{5,7},{6,4},{7,5},{8,10},{9,11},{10,... | collective-permute-start | bytes 36872 | tf_op jit(solution)/shard_map/ppermute | solution.py:331
  14.1 2.2 %collective-permute-done.9 = f32[24,128]{1,0:T(8,128)S(1)} collective-permute-done((f32[24,128]{1,0:T(8,128)S(1)}, f32[24,128]{1,0:T(8,128)S(1)}, u32[]{:S(2)}, u32[]{:S(2)}) %collective-permute-start.9) | collective-permute-done | bytes 12320 | tf_op jit(solution)/shard_map/ppermute | solution.py:331
  16.2 0.6 collective-permute-start.10
  16.8 0.2 shard_map.95
  17.0 11.7 %collective-permute-done.10 = f32[24,128]{1,0:T(8,128)S(1)} collective-permute-done((f32[24,128]{1,0:T(8,128)S(1)}, f32[24,128]{1,0:T(8,128)S(1)}, u32[]{:S(2)}, u32[]{:S(2)}) %collective-permute-start.10) | collective-permute-done | bytes 12320 | tf_op jit(solution)/shard_map/ppermute | solution.py:331
  28.7 1.7 %collective-permute-start.21 = (f32[4,2,64,128]{3,2,1,0:T(8,128)S(1)}, f32[4,2,64,128]{3,2,1,0:T(8,128)S(1)}, u32[]{:S(2)}, u32[]{:S(2)}) collective-permute-start(f32[4,2,64,128]{3,2,1,0:T(8,128)S(1)} %get-tuple-element.64), channel_id=1, source_target_pairs={{0,4},{4,0},{8,12},{12,8},{16,20},{20,16},{24,28},{28,24},{1,5},{5... | collective-permute-start | bytes 786440 | tf_op jit(solution)/shard_map/ppermute | solution.py:400
  30.4 0.0 collective-permute-done.13.near_ref
  30.4 3.6 %collective-permute-start.22 = (f32[4,2,64,128]{3,2,1,0:T(8,128)S(1)}, f32[4,2,64,128]{3,2,1,0:T(8,128)S(1)}, u32[]{:S(2)}, u32[]{:S(2)}) collective-permute-start(f32[4,2,64,128]{3,2,1,0:T(8,128)S(1)} %get-tuple-element.65), channel_id=1, source_target_pairs={{0,28},{4,8},{8,4},{12,16},{16,12},{20,24},{24,20},{28,0},{1,29},{... | collective-permute-start | bytes 786440 | tf_op jit(solution)/shard_map/ppermute | solution.py:401
  34.0 0.0 collective-permute-done.14.far_ref
  34.0 0.0 collective-permute-start.11
  34.1 0.6 shard_map.93
  34.7 4.0 %collective-permute-done.11 = f32[24,128]{1,0:T(8,128)S(1)} collective-permute-done((f32[24,128]{1,0:T(8,128)S(1)}, f32[24,128]{1,0:T(8,128)S(1)}, u32[]{:S(2)}, u32[]{:S(2)}) %collective-permute-start.11) | collective-permute-done | bytes 12320 | tf_op jit(solution)/shard_map/ppermute | solution.py:331
  38.7 0.0 collective-permute-start.15
  38.7 0.0 collective-permute-done.near_ref
  38.7 1.5 %collective-permute-start.16 = (f32[256,128]{1,0:T(8,128)S(1)}, f32[256,128]{1,0:T(8,128)S(1)}, u32[]{:S(2)}, u32[]{:S(2)}) collective-permute-start(f32[256,128]{1,0:T(8,128)S(1)} %get-tuple-element.58), channel_id=1, source_target_pairs={{0,2},{1,3},{2,0},{3,1},{4,6},{5,7},{6,4},{7,5},{8,10},{9,11},{10,... | collective-permute-start | bytes 393224 | tf_op jit(solution)/shard_map/ppermute | solution.py:313
  40.2 0.3 collective-permute-start.17
  40.6 3.4 %copy-done.2 = f32[32,256,256]{2,1,0:T(8,128)S(1)} copy-done((f32[32,256,256]{2,1,0:T(8,128)S(1)}, f32[32,256,256]{2,1,0:T(8,128)}, u32[]{:S(2)}) %copy-start.2) | copy-done | bytes 8388632
  44.0 1.5 %shard_map.88 = (bf16[16,256,256]{2,1,0:T(8,128)(2,1)S(1)}, bf16[16,256,256]{2,1,0:T(8,128)(2,1)S(1)}) custom-call(f32[32,256,256]{2,1,0:T(8,128)S(1)} %copy-done.2), custom_call_target="tpu_custom_call" | custom-call | flops 10000000 | bytes 8388608 | tf_op jit(solution)/shard_map/pallas_call | solution.py:410
  45.4 1.5 %shard_map.89 = (bf16[16,256,256]{2,1,0:T(8,128)(2,1)S(1)}, bf16[16,256,256]{2,1,0:T(8,128)(2,1)S(1)}) custom-call(f32[32,256,256]{2,1,0:T(8,128)S(1)} %copy-done.2), custom_call_target="tpu_custom_call" | custom-call | flops 10000000 | bytes 8388608 | tf_op jit(solution)/shard_map/pallas_call | solution.py:410
  46.9 0.6 shard_map.87
  47.6 0.0 copy-start.7
  47.6 1.6 %collective-permute-start.12 = (f32[24,128]{1,0:T(8,128)S(1)}, f32[24,128]{1,0:T(8,128)S(1)}, u32[]{:S(2)}, u32[]{:S(2)}) collective-permute-start(f32[24,128]{1,0:T(8,128)S(1)} %add.18), channel_id=1, source_target_pairs={{0,16},{4,20},{8,24},{12,28},{16,0},{20,4},{24,8},{28,12},{1,17},{... | collective-permute-start | bytes 36872 | tf_op jit(solution)/shard_map/ppermute | solution.py:331
  49.2 0.0 collective-permute-start.2
  49.2 0.6 shard_map.96
  49.8 0.0 collective-permute-done.15.refs_1_
  49.9 0.6 collective-permute-start.23
  50.4 1.5 %collective-permute-start.24 = (f32[256,128]{1,0:T(8,128)S(1)}, f32[256,128]{1,0:T(8,128)S(1)}, u32[]{:S(2)}, u32[]{:S(2)}) collective-permute-start(f32[256,128]{1,0:T(8,128)S(1)} %get-tuple-element.68), channel_id=1, source_target_pairs={{0,2},{1,3},{2,0},{3,1},{4,6},{5,7},{6,4},{7,5},{8,10},{9,11},{10,... | collective-permute-start | bytes 393224 | tf_op jit(solution)/shard_map/ppermute | solution.py:313
  51.9 0.0 collective-permute-done.17.refs_3_
  52.0 2.5 %shard_map.94 = (f32[264,128]{1,0:T(8,128)S(1)}, f32[264,128]{1,0:T(8,128)S(1)}, f32[264,128]{1,0:T(8,128)S(1)}, f32[264,128]{1,0:T(8,128)S(1)}) custom-call(f32[256,128]{1,0:T(8,128)S(1)} %get-tuple-element.56.refs_0_, f32[256,128]{1,0:T(8,128)S(1)} %collective-permute-done.15.refs_1_, f32[256,128]{1,0:T(8,128)S(1)} %collective-permute-done.16.refs_2_, ...), custom_call_target="tpu_custom_call" | custom-call | flops 3221225472 | bytes 8388608 | tf_op jit(solution)/shard_map/pallas_call | solution.py:436
  54.5 0.0 collective-permute-done.23.refs_1_
  54.5 1.5 %collective-permute-start.3 = (f32[256,128]{1,0:T(8,128)S(1)}, f32[256,128]{1,0:T(8,128)S(1)}, u32[]{:S(2)}, u32[]{:S(2)}) collective-permute-start(f32[256,128]{1,0:T(8,128)S(1)} %get-tuple-element.44), channel_id=1, source_target_pairs={{0,2},{1,3},{2,0},{3,1},{4,6},{5,7},{6,4},{7,5},{8,10},{9,11},{10,... | collective-permute-start | bytes 393224 | tf_op jit(solution)/shard_map/ppermute | solution.py:313
  56.0 0.8 collective-permute-done.24.refs_2_
  56.8 1.8 %collective-permute-done.25.refs_3_ = f32[256,128]{1,0:T(8,128)S(1)} collective-permute-done((f32[256,128]{1,0:T(8,128)S(1)}, f32[256,128]{1,0:T(8,128)S(1)}, u32[]{:S(2)}, u32[]{:S(2)}) %collective-permute-start.25) | collective-permute-done | bytes 131104 | tf_op jit(solution)/shard_map/ppermute | solution.py:313
  58.6 0.8 collective-permute-start.18
  59.4 2.5 %shard_map.97 = (f32[264,128]{1,0:T(8,128)S(1)}, f32[264,128]{1,0:T(8,128)S(1)}, f32[264,128]{1,0:T(8,128)S(1)}, f32[264,128]{1,0:T(8,128)S(1)}) custom-call(f32[256,128]{1,0:T(8,128)S(1)} %get-tuple-element.66.refs_0_, f32[256,128]{1,0:T(8,128)S(1)} %collective-permute-done.23.refs_1_, f32[256,128]{1,0:T(8,128)S(1)} %collective-permute-done.24.refs_2_, ...), custom_call_target="tpu_custom_call" | custom-call | flops 3221225472 | bytes 8388608 | tf_op jit(solution)/shard_map/pallas_call | solution.py:436
  61.9 0.0 collective-permute-done.12
  61.9 1.6 %collective-permute-start.19 = (f32[264,128]{1,0:T(8,128)S(1)}, f32[264,128]{1,0:T(8,128)S(1)}, u32[]{:S(2)}, u32[]{:S(2)}) collective-permute-start(f32[264,128]{1,0:T(8,128)S(1)} %get-tuple-element.62), channel_id=1, source_target_pairs={{0,2},{1,3},{2,0},{3,1},{4,6},{5,7},{6,4},{7,5},{8,10},{9,11},{10,... | collective-permute-start | bytes 405512 | tf_op jit(solution)/shard_map/ppermute | solution.py:313
  63.5 0.6 collective-permute-start.26
  64.2 1.5 %collective-permute-start.27 = (f32[264,128]{1,0:T(8,128)S(1)}, f32[264,128]{1,0:T(8,128)S(1)}, u32[]{:S(2)}, u32[]{:S(2)}) collective-permute-start(f32[264,128]{1,0:T(8,128)S(1)} %get-tuple-element.72), channel_id=1, source_target_pairs={{0,2},{1,3},{2,0},{3,1},{4,6},{5,7},{6,4},{7,5},{8,10},{9,11},{10,... | collective-permute-start | bytes 405512 | tf_op jit(solution)/shard_map/ppermute | solution.py:313
  65.7 0.0 copy-start.6
  65.7 2.5 %shard_map.90 = (f32[264,128]{1,0:T(8,128)S(1)}, f32[264,128]{1,0:T(8,128)S(1)}, f32[264,128]{1,0:T(8,128)S(1)}, f32[264,128]{1,0:T(8,128)S(1)}) custom-call(f32[256,128]{1,0:T(8,128)S(1)} %get-tuple-element.42.refs_0_, f32[256,128]{1,0:T(8,128)S(1)} %collective-permute-done.2.refs_1_, f32[256,128]{1,0:T(8,128)S(1)} %collective-permute-done.3.refs_2_, ...), custom_call_target="tpu_custom_call" | custom-call | flops 3221225472 | bytes 8388608 | tf_op jit(solution)/shard_map/pallas_call | solution.py:436
  68.2 0.7 collective-permute-start.5
  68.9 5.4 %collective-permute-done.27.refs_2_ = f32[264,128]{1,0:T(8,128)S(1)} collective-permute-done((f32[264,128]{1,0:T(8,128)S(1)}, f32[264,128]{1,0:T(8,128)S(1)}, u32[]{:S(2)}, u32[]{:S(2)}) %collective-permute-start.27) | collective-permute-done | bytes 135200 | tf_op jit(solution)/shard_map/ppermute | solution.py:313
  74.3 1.5 %collective-permute-start.6 = (f32[264,128]{1,0:T(8,128)S(1)}, f32[264,128]{1,0:T(8,128)S(1)}, u32[]{:S(2)}, u32[]{:S(2)}) collective-permute-start(f32[264,128]{1,0:T(8,128)S(1)} %get-tuple-element.52), channel_id=1, source_target_pairs={{0,2},{1,3},{2,0},{3,1},{4,6},{5,7},{6,4},{7,5},{8,10},{9,11},{10,... | collective-permute-start | bytes 405512 | tf_op jit(solution)/shard_map/ppermute | solution.py:313
  75.8 0.4 collective-permute-done.28.refs_3_
  76.2 1.9 %collective-permute-start.7 = (f32[264,128]{1,0:T(8,128)S(1)}, f32[264,128]{1,0:T(8,128)S(1)}, u32[]{:S(2)}, u32[]{:S(2)}) collective-permute-start(f32[264,128]{1,0:T(8,128)S(1)} %get-tuple-element.53), channel_id=1, source_target_pairs={{0,3},{1,2},{2,1},{3,0},{4,7},{5,6},{6,5},{7,4},{8,11},{9,10},{10,... | collective-permute-start | bytes 405512 | tf_op jit(solution)/shard_map/ppermute | solution.py:313
  78.1 1.2 %shard_map.98 = (f32[12,4,64,128]{3,2,1,0:T(8,128)}, f32[12,2,2,128]{3,2,1,0:T(2,128)}) custom-call(f32[264,128]{1,0:T(8,128)S(1)} %get-tuple-element.70.refs_0_, f32[264,128]{1,0:T(8,128)S(1)} %collective-permute-done.26.refs_1_, f32[264,128]{1,0:T(8,128)S(1)} %collective-permute-done.27.refs_2_, f32[264,128]{1,0:T(8,128)S(1)} %collective-permute-done.28.refs_3_, ...), custom_call_target="tpu_custom_call" | custom-call | flops 100663296 | bytes 1048576 | tf_op jit(solution)/shard_map/pallas_call | solution.py:447
  79.3 1.2 %shard_map.99 = (f32[12,4,64,128]{3,2,1,0:T(8,128)}, f32[12,2,2,128]{3,2,1,0:T(2,128)}) custom-call(f32[264,128]{1,0:T(8,128)S(1)} %get-tuple-element.60.refs_0_, f32[264,128]{1,0:T(8,128)S(1)} %collective-permute-done.18.refs_1_, f32[264,128]{1,0:T(8,128)S(1)} %collective-permute-done.19.refs_2_, ...), custom_call_target="tpu_custom_call", output_to_operand_aliasing={{0}: (7, {}), {1}: (8, {})} | custom-call | flops 100663296 | bytes 1048576 | tf_op jit(solution)/shard_map/pallas_call | solution.py:447
  80.6 0.9 %collective-permute-done.7.refs_3_ = f32[264,128]{1,0:T(8,128)S(1)} collective-permute-done((f32[264,128]{1,0:T(8,128)S(1)}, f32[264,128]{1,0:T(8,128)S(1)}, u32[]{:S(2)}, u32[]{:S(2)}) %collective-permute-start.7) | collective-permute-done | bytes 135200 | tf_op jit(solution)/shard_map/ppermute | solution.py:313
  81.4 1.2 %shard_map.100 = (f32[12,4,64,128]{3,2,1,0:T(8,128)}, f32[12,2,2,128]{3,2,1,0:T(2,128)}) custom-call(f32[264,128]{1,0:T(8,128)S(1)} %get-tuple-element.50.refs_0_, f32[264,128]{1,0:T(8,128)S(1)} %collective-permute-done.5.refs_1_, f32[264,128]{1,0:T(8,128)S(1)} %collective-permute-done.6.refs_2_, ...), custom_call_target="tpu_custom_call", output_to_operand_aliasing={{0}: (7, {}), {1}: (8, {})} | custom-call | flops 100663296 | bytes 1048576 | tf_op jit(solution)/shard_map/pallas_call | solution.py:447
  (30 shorter events, 0.1 us)
Async XLA Ops:
  0.6 1.4 %copy-start = (f32[12,4,64,128]{3,2,1,0:T(8,128)S(1)}, f32[12,4,64,128]{3,2,1,0:T(8,128)}, u32[]{:S(2)}) copy-start(f32[12,4,64,128]{3,2,1,0:T(8,128)} %state_ref.13) | copy-start | bytes 4718596
  2.2 28.2 %collective-permute-start.13 = (f32[4,2,64,128]{3,2,1,0:T(8,128)S(1)}, f32[4,2,64,128]{3,2,1,0:T(8,128)S(1)}, u32[]{:S(2)}, u32[]{:S(2)}) collective-permute-start(f32[4,2,64,128]{3,2,1,0:T(8,128)S(1)} %get-tuple-element.54), channel_id=1, source_target_pairs={{0,4},{4,0},{8,12},{12,8},{16,20},{20,16},{24,28},{28,24},{1,5},{5... | collective-permute-start | bytes 786440 | tf_op jit(solution)/shard_map/ppermute | solution.py:400
  5.3 28.7 %collective-permute-start.14 = (f32[4,2,64,128]{3,2,1,0:T(8,128)S(1)}, f32[4,2,64,128]{3,2,1,0:T(8,128)S(1)}, u32[]{:S(2)}, u32[]{:S(2)}) collective-permute-start(f32[4,2,64,128]{3,2,1,0:T(8,128)S(1)} %get-tuple-element.55), channel_id=1, source_target_pairs={{0,28},{4,8},{8,4},{12,16},{16,12},{20,24},{24,20},{28,0},{1,29},{... | collective-permute-start | bytes 786440 | tf_op jit(solution)/shard_map/ppermute | solution.py:401
  9.1 7.8 %copy-start.1 = (f32[12,4,64,128]{3,2,1,0:T(8,128)S(1)}, f32[12,4,64,128]{3,2,1,0:T(8,128)}, u32[]{:S(2)}) copy-start(f32[12,4,64,128]{3,2,1,0:T(8,128)} %state_ref.13) | copy-start | bytes 4718596
  9.1 29.6 %collective-permute-start = (f32[4,2,64,128]{3,2,1,0:T(8,128)S(1)}, f32[4,2,64,128]{3,2,1,0:T(8,128)S(1)}, u32[]{:S(2)}, u32[]{:S(2)}) collective-permute-start(f32[4,2,64,128]{3,2,1,0:T(8,128)S(1)} %get-tuple-element.40), channel_id=1, source_target_pairs={{0,4},{4,0},{8,12},{12,8},{16,20},{20,16},{24,28},{28,24},{1,5},{5... | collective-permute-start | bytes 786440 | tf_op jit(solution)/shard_map/ppermute | solution.py:400
  9.1 24.9 %copy-start.3 = (bf16[2,256,512]{2,1,0:T(8,128)(2,1)S(1)}, bf16[2,256,512]{2,1,0:T(8,128)(2,1)}, u32[]{:S(2)}) copy-start(bf16[2,256,512]{2,1,0:T(8,128)(2,1)} %constant.10.clone.high_ref) | copy-start | bytes 1572868
  9.2 24.9 %copy-start.4 = (bf16[2,256,512]{2,1,0:T(8,128)(2,1)S(1)}, bf16[2,256,512]{2,1,0:T(8,128)(2,1)}, u32[]{:S(2)}) copy-start(bf16[2,256,512]{2,1,0:T(8,128)(2,1)} %constant.11.clone.low_ref) | copy-start | bytes 1572868
  9.2 31.1 %collective-permute-start.1 = (f32[4,2,64,128]{3,2,1,0:T(8,128)S(1)}, f32[4,2,64,128]{3,2,1,0:T(8,128)S(1)}, u32[]{:S(2)}, u32[]{:S(2)}) collective-permute-start(f32[4,2,64,128]{3,2,1,0:T(8,128)S(1)} %get-tuple-element.41), channel_id=1, source_target_pairs={{0,28},{4,8},{8,4},{12,16},{16,12},{20,24},{24,20},{28,0},{1,29},{... | collective-permute-start | bytes 786440 | tf_op jit(solution)/shard_map/ppermute | solution.py:401
  11.3 1.2 %collective-permute-start.8 = (f32[24,128]{1,0:T(8,128)S(1)}, f32[24,128]{1,0:T(8,128)S(1)}, u32[]{:S(2)}, u32[]{:S(2)}) collective-permute-start(f32[24,128]{1,0:T(8,128)S(1)} %shard_map.91), channel_id=1, source_target_pairs={{0,1},{1,0},{2,3},{3,2},{4,5},{5,4},{6,7},{7,6},{8,9},{9,8},{10,11... | collective-permute-start | bytes 36872 | tf_op jit(solution)/shard_map/ppermute | solution.py:331
  12.5 3.7 %collective-permute-start.9 = (f32[24,128]{1,0:T(8,128)S(1)}, f32[24,128]{1,0:T(8,128)S(1)}, u32[]{:S(2)}, u32[]{:S(2)}) collective-permute-start(f32[24,128]{1,0:T(8,128)S(1)} %add.15), channel_id=1, source_target_pairs={{0,2},{1,3},{2,0},{3,1},{4,6},{5,7},{6,4},{7,5},{8,10},{9,11},{10,... | collective-permute-start | bytes 36872 | tf_op jit(solution)/shard_map/ppermute | solution.py:331
  16.2 12.5 %collective-permute-start.10 = (f32[24,128]{1,0:T(8,128)S(1)}, f32[24,128]{1,0:T(8,128)S(1)}, u32[]{:S(2)}, u32[]{:S(2)}) collective-permute-start(f32[24,128]{1,0:T(8,128)S(1)} %add.16), channel_id=1, source_target_pairs={{0,4},{4,0},{8,12},{12,8},{16,20},{20,16},{24,28},{28,24},{1,5},{5... | collective-permute-start | bytes 36872 | tf_op jit(solution)/shard_map/ppermute | solution.py:331
  28.7 18.9 %collective-permute-start.21 = (f32[4,2,64,128]{3,2,1,0:T(8,128)S(1)}, f32[4,2,64,128]{3,2,1,0:T(8,128)S(1)}, u32[]{:S(2)}, u32[]{:S(2)}) collective-permute-start(f32[4,2,64,128]{3,2,1,0:T(8,128)S(1)} %get-tuple-element.64), channel_id=1, source_target_pairs={{0,4},{4,0},{8,12},{12,8},{16,20},{20,16},{24,28},{28,24},{1,5},{5... | collective-permute-start | bytes 786440 | tf_op jit(solution)/shard_map/ppermute | solution.py:400
  30.4 18.7 %collective-permute-start.22 = (f32[4,2,64,128]{3,2,1,0:T(8,128)S(1)}, f32[4,2,64,128]{3,2,1,0:T(8,128)S(1)}, u32[]{:S(2)}, u32[]{:S(2)}) collective-permute-start(f32[4,2,64,128]{3,2,1,0:T(8,128)S(1)} %get-tuple-element.65), channel_id=1, source_target_pairs={{0,28},{4,8},{8,4},{12,16},{16,12},{20,24},{24,20},{28,0},{1,29},{... | collective-permute-start | bytes 786440 | tf_op jit(solution)/shard_map/ppermute | solution.py:401
  34.0 4.7 %collective-permute-start.11 = (f32[24,128]{1,0:T(8,128)S(1)}, f32[24,128]{1,0:T(8,128)S(1)}, u32[]{:S(2)}, u32[]{:S(2)}) collective-permute-start(f32[24,128]{1,0:T(8,128)S(1)} %add.17), channel_id=1, source_target_pairs={{0,8},{4,12},{8,0},{12,4},{16,24},{20,28},{24,16},{28,20},{1,9},{5... | collective-permute-start | bytes 36872 | tf_op jit(solution)/shard_map/ppermute | solution.py:331
  38.7 11.1 %collective-permute-start.15 = (f32[256,128]{1,0:T(8,128)S(1)}, f32[256,128]{1,0:T(8,128)S(1)}, u32[]{:S(2)}, u32[]{:S(2)}) collective-permute-start(f32[256,128]{1,0:T(8,128)S(1)} %get-tuple-element.57), channel_id=1, source_target_pairs={{0,1},{1,0},{2,3},{3,2},{4,5},{5,4},{6,7},{7,6},{8,9},{9,8},{10,11... | collective-permute-start | bytes 393224 | tf_op jit(solution)/shard_map/ppermute | solution.py:313
  38.7 11.7 %collective-permute-start.16 = (f32[256,128]{1,0:T(8,128)S(1)}, f32[256,128]{1,0:T(8,128)S(1)}, u32[]{:S(2)}, u32[]{:S(2)}) collective-permute-start(f32[256,128]{1,0:T(8,128)S(1)} %get-tuple-element.58), channel_id=1, source_target_pairs={{0,2},{1,3},{2,0},{3,1},{4,6},{5,7},{6,4},{7,5},{8,10},{9,11},{10,... | collective-permute-start | bytes 393224 | tf_op jit(solution)/shard_map/ppermute | solution.py:313
  40.2 11.7 %collective-permute-start.17 = (f32[256,128]{1,0:T(8,128)S(1)}, f32[256,128]{1,0:T(8,128)S(1)}, u32[]{:S(2)}, u32[]{:S(2)}) collective-permute-start(f32[256,128]{1,0:T(8,128)S(1)} %get-tuple-element.59), channel_id=1, source_target_pairs={{0,3},{1,2},{2,1},{3,0},{4,7},{5,6},{6,5},{7,4},{8,11},{9,10},{10,... | collective-permute-start | bytes 393224 | tf_op jit(solution)/shard_map/ppermute | solution.py:313
  40.6 3.4 %copy-start.2 = (f32[32,256,256]{2,1,0:T(8,128)S(1)}, f32[32,256,256]{2,1,0:T(8,128)}, u32[]{:S(2)}) copy-start(f32[32,256,256]{2,1,0:T(8,128)} %inverse_ref.3) | copy-start | bytes 25165828
  47.6 4.4 %copy-start.7 = (f32[8,256]{1,0:T(8,128)S(1)}, f32[8,256]{1,0:T(8,128)}, u32[]{:S(2)}) copy-start(f32[8,256]{1,0:T(8,128)} %constant.14.clone.refs_8_) | copy-start | bytes 24580
  47.6 14.3 %collective-permute-start.12 = (f32[24,128]{1,0:T(8,128)S(1)}, f32[24,128]{1,0:T(8,128)S(1)}, u32[]{:S(2)}, u32[]{:S(2)}) collective-permute-start(f32[24,128]{1,0:T(8,128)S(1)} %add.18), channel_id=1, source_target_pairs={{0,16},{4,20},{8,24},{12,28},{16,0},{20,4},{24,8},{28,12},{1,17},{... | collective-permute-start | bytes 36872 | tf_op jit(solution)/shard_map/ppermute | solution.py:331
  49.2 14.3 %collective-permute-start.2 = (f32[256,128]{1,0:T(8,128)S(1)}, f32[256,128]{1,0:T(8,128)S(1)}, u32[]{:S(2)}, u32[]{:S(2)}) collective-permute-start(f32[256,128]{1,0:T(8,128)S(1)} %get-tuple-element.43), channel_id=1, source_target_pairs={{0,1},{1,0},{2,3},{3,2},{4,5},{5,4},{6,7},{7,6},{8,9},{9,8},{10,11... | collective-permute-start | bytes 393224 | tf_op jit(solution)/shard_map/ppermute | solution.py:313
  49.9 4.6 %collective-permute-start.23 = (f32[256,128]{1,0:T(8,128)S(1)}, f32[256,128]{1,0:T(8,128)S(1)}, u32[]{:S(2)}, u32[]{:S(2)}) collective-permute-start(f32[256,128]{1,0:T(8,128)S(1)} %get-tuple-element.67), channel_id=1, source_target_pairs={{0,1},{1,0},{2,3},{3,2},{4,5},{5,4},{6,7},{7,6},{8,9},{9,8},{10,11... | collective-permute-start | bytes 393224 | tf_op jit(solution)/shard_map/ppermute | solution.py:313
  50.4 6.4 %collective-permute-start.24 = (f32[256,128]{1,0:T(8,128)S(1)}, f32[256,128]{1,0:T(8,128)S(1)}, u32[]{:S(2)}, u32[]{:S(2)}) collective-permute-start(f32[256,128]{1,0:T(8,128)S(1)} %get-tuple-element.68), channel_id=1, source_target_pairs={{0,2},{1,3},{2,0},{3,1},{4,6},{5,7},{6,4},{7,5},{8,10},{9,11},{10,... | collective-permute-start | bytes 393224 | tf_op jit(solution)/shard_map/ppermute | solution.py:313
  51.9 6.7 %collective-permute-start.25 = (f32[256,128]{1,0:T(8,128)S(1)}, f32[256,128]{1,0:T(8,128)S(1)}, u32[]{:S(2)}, u32[]{:S(2)}) collective-permute-start(f32[256,128]{1,0:T(8,128)S(1)} %get-tuple-element.69), channel_id=1, source_target_pairs={{0,3},{1,2},{2,1},{3,0},{4,7},{5,6},{6,5},{7,4},{8,11},{9,10},{10,... | collective-permute-start | bytes 393224 | tf_op jit(solution)/shard_map/ppermute | solution.py:313
  54.5 9.1 %collective-permute-start.3 = (f32[256,128]{1,0:T(8,128)S(1)}, f32[256,128]{1,0:T(8,128)S(1)}, u32[]{:S(2)}, u32[]{:S(2)}) collective-permute-start(f32[256,128]{1,0:T(8,128)S(1)} %get-tuple-element.44), channel_id=1, source_target_pairs={{0,2},{1,3},{2,0},{3,1},{4,6},{5,7},{6,4},{7,5},{8,10},{9,11},{10,... | collective-permute-start | bytes 393224 | tf_op jit(solution)/shard_map/ppermute | solution.py:313
  56.8 7.4 %collective-permute-start.4 = (f32[256,128]{1,0:T(8,128)S(1)}, f32[256,128]{1,0:T(8,128)S(1)}, u32[]{:S(2)}, u32[]{:S(2)}) collective-permute-start(f32[256,128]{1,0:T(8,128)S(1)} %get-tuple-element.45), channel_id=1, source_target_pairs={{0,3},{1,2},{2,1},{3,0},{4,7},{5,6},{6,5},{7,4},{8,11},{9,10},{10,... | collective-permute-start | bytes 393224 | tf_op jit(solution)/shard_map/ppermute | solution.py:313
  58.6 7.0 %collective-permute-start.18 = (f32[264,128]{1,0:T(8,128)S(1)}, f32[264,128]{1,0:T(8,128)S(1)}, u32[]{:S(2)}, u32[]{:S(2)}) collective-permute-start(f32[264,128]{1,0:T(8,128)S(1)} %get-tuple-element.61), channel_id=1, source_target_pairs={{0,1},{1,0},{2,3},{3,2},{4,5},{5,4},{6,7},{7,6},{8,9},{9,8},{10,11... | collective-permute-start | bytes 405512 | tf_op jit(solution)/shard_map/ppermute | solution.py:313
  61.9 17.4 %collective-permute-start.19 = (f32[264,128]{1,0:T(8,128)S(1)}, f32[264,128]{1,0:T(8,128)S(1)}, u32[]{:S(2)}, u32[]{:S(2)}) collective-permute-start(f32[264,128]{1,0:T(8,128)S(1)} %get-tuple-element.62), channel_id=1, source_target_pairs={{0,2},{1,3},{2,0},{3,1},{4,6},{5,7},{6,4},{7,5},{8,10},{9,11},{10,... | collective-permute-start | bytes 405512 | tf_op jit(solution)/shard_map/ppermute | solution.py:313
  63.5 15.8 %collective-permute-start.20 = (f32[264,128]{1,0:T(8,128)S(1)}, f32[264,128]{1,0:T(8,128)S(1)}, u32[]{:S(2)}, u32[]{:S(2)}) collective-permute-start(f32[264,128]{1,0:T(8,128)S(1)} %get-tuple-element.63), channel_id=1, source_target_pairs={{0,3},{1,2},{2,1},{3,0},{4,7},{5,6},{6,5},{7,4},{8,11},{9,10},{10,... | collective-permute-start | bytes 405512 | tf_op jit(solution)/shard_map/ppermute | solution.py:313
  63.5 4.7 %collective-permute-start.26 = (f32[264,128]{1,0:T(8,128)S(1)}, f32[264,128]{1,0:T(8,128)S(1)}, u32[]{:S(2)}, u32[]{:S(2)}) collective-permute-start(f32[264,128]{1,0:T(8,128)S(1)} %get-tuple-element.71), channel_id=1, source_target_pairs={{0,1},{1,0},{2,3},{3,2},{4,5},{5,4},{6,7},{7,6},{8,9},{9,8},{10,11... | collective-permute-start | bytes 405512 | tf_op jit(solution)/shard_map/ppermute | solution.py:313
  64.2 10.1 %collective-permute-start.27 = (f32[264,128]{1,0:T(8,128)S(1)}, f32[264,128]{1,0:T(8,128)S(1)}, u32[]{:S(2)}, u32[]{:S(2)}) collective-permute-start(f32[264,128]{1,0:T(8,128)S(1)} %get-tuple-element.72), channel_id=1, source_target_pairs={{0,2},{1,3},{2,0},{3,1},{4,6},{5,7},{6,4},{7,5},{8,10},{9,11},{10,... | collective-permute-start | bytes 405512 | tf_op jit(solution)/shard_map/ppermute | solution.py:313
  65.7 10.5 %collective-permute-start.28 = (f32[264,128]{1,0:T(8,128)S(1)}, f32[264,128]{1,0:T(8,128)S(1)}, u32[]{:S(2)}, u32[]{:S(2)}) collective-permute-start(f32[264,128]{1,0:T(8,128)S(1)} %get-tuple-element.73), channel_id=1, source_target_pairs={{0,3},{1,2},{2,1},{3,0},{4,7},{5,6},{6,5},{7,4},{8,11},{9,10},{10,... | collective-permute-start | bytes 405512 | tf_op jit(solution)/shard_map/ppermute | solution.py:313
  65.7 12.4 %copy-start.5 = (bf16[128,128]{1,0:T(8,128)(2,1)S(1)}, bf16[128,128]{1,0:T(8,128)(2,1)}, u32[]{:S(2)}) copy-start(bf16[128,128]{1,0:T(8,128)(2,1)} %constant.12.clone.refs_4_) | copy-start | bytes 98308
  65.7 12.4 %copy-start.6 = (bf16[128,128]{1,0:T(8,128)(2,1)S(1)}, bf16[128,128]{1,0:T(8,128)(2,1)}, u32[]{:S(2)}) copy-start(bf16[128,128]{1,0:T(8,128)(2,1)} %constant.13.clone.refs_5_) | copy-start | bytes 98308
  68.2 12.3 %collective-permute-start.5 = (f32[264,128]{1,0:T(8,128)S(1)}, f32[264,128]{1,0:T(8,128)S(1)}, u32[]{:S(2)}, u32[]{:S(2)}) collective-permute-start(f32[264,128]{1,0:T(8,128)S(1)} %get-tuple-element.51), channel_id=1, source_target_pairs={{0,1},{1,0},{2,3},{3,2},{4,5},{5,4},{6,7},{7,6},{8,9},{9,8},{10,11... | collective-permute-start | bytes 405512 | tf_op jit(solution)/shard_map/ppermute | solution.py:313
  74.3 6.3 %collective-permute-start.6 = (f32[264,128]{1,0:T(8,128)S(1)}, f32[264,128]{1,0:T(8,128)S(1)}, u32[]{:S(2)}, u32[]{:S(2)}) collective-permute-start(f32[264,128]{1,0:T(8,128)S(1)} %get-tuple-element.52), channel_id=1, source_target_pairs={{0,2},{1,3},{2,0},{3,1},{4,6},{5,7},{6,4},{7,5},{8,10},{9,11},{10,... | collective-permute-start | bytes 405512 | tf_op jit(solution)/shard_map/ppermute | solution.py:313
  76.2 5.2 %collective-permute-start.7 = (f32[264,128]{1,0:T(8,128)S(1)}, f32[264,128]{1,0:T(8,128)S(1)}, u32[]{:S(2)}, u32[]{:S(2)}) collective-permute-start(f32[264,128]{1,0:T(8,128)S(1)} %get-tuple-element.53), channel_id=1, source_target_pairs={{0,3},{1,2},{2,1},{3,0},{4,7},{5,6},{6,5},{7,4},{8,11},{9,10},{10,... | collective-permute-start | bytes 405512 | tf_op jit(solution)/shard_map/ppermute | solution.py:313

commit v5 on v4

--- a/solution.py
+++ b/solution.py
@@ -192,11 +192,38 @@
                     ]
 
 
+def products(i, h, rows, modes, recv_refs, high_refs, low_refs):
+    unit = rows * modes
+    left = left_lanes((unit, LANES))
+    a, b = [ref[i * unit : (i + 1) * unit] for ref in recv_refs]
+    even = jnp.where(left, a, swap(b))
+    odd = jnp.where(left, swap(a), b)
+    columns = slice(h * LANES, (h + 1) * LANES)
+    found = []
+    for j in range(modes):
+        r = jnp.concatenate([x[j * rows : (j + 1) * rows] for x in (even, odd)], axis=0)
+        half, at = divmod(i * modes + j, high_refs[0].shape[0])
+        v_high = high_refs[half][at, :, columns]
+        v_low = low_refs[half][at, :, columns]
+        r_high, r_low = split(r)
+        both = dot(jnp.concatenate([r_high, r_low], axis=0), v_high, NT)
+        found.append(both[: 2 * rows] + (both[2 * rows :] + dot(r_high, v_low, NT)))
+    return found
+
+
+def begin_kernel(rows, *refs):
+    recv_refs, high_refs, low_refs, out_ref = refs[:2], refs[2:4], refs[4:6], refs[6]
+    modes = TILE // math.gcd(rows, TILE)
+    for i in range(recv_refs[0].shape[0] // (rows * modes)):
+        for j, o in enumerate(products(i, 0, rows, modes, recv_refs, high_refs, low_refs)):
+            m = i * modes + j
+            out_ref[m * 2 * rows : (m + 1) * 2 * rows] = o
+
+
 def solve_kernel(parts, rows, *refs):
-    recv_refs = refs[:parts]
-    high_refs, low_refs = refs[parts : parts + 2], refs[parts + 2 : parts + 4]
-    wall_ref = refs[parts + 4]
-    out_refs = refs[parts + 5 :]
+    recv_refs, high_refs, low_refs = refs[:2], refs[2:4], refs[4:6]
+    begun_ref, wall_ref = refs[6:8]
+    out_refs = refs[8:]
     slots = recv_refs[0].shape[0] // rows
     modes = TILE // math.gcd(rows, TILE)
     unit = rows * modes
@@ -207,22 +234,10 @@
     sums = jnp.zeros((unit, LANES), jnp.float32)
     for i in range(slots // modes):
         tile = slice(i * unit, (i + 1) * unit)
-        t = [ref[tile] for ref in recv_refs]
-        even, odd = [], []
-        for d in range(0, parts, 2):
-            even.append(jnp.where(left, t[d], swap(t[d + 1])))
-            odd.append(jnp.where(left, swap(t[d]), t[d + 1]))
-        even = jnp.concatenate(even, axis=1)
-        odd = jnp.concatenate(odd, axis=1)
         solved = []
-        for j in range(modes):
-            r = jnp.concatenate([x[j * rows : (j + 1) * rows] for x in (even, odd)], axis=0)
-            half, at = divmod(i * modes + j, high_refs[0].shape[0])
-            v_high = high_refs[half][at]
-            v_low = low_refs[half][at]
-            r_high, r_low = split(r)
-            both = dot(jnp.concatenate([r_high, r_low], axis=0), v_high, NT)
-            solved.append(both[: 2 * rows] + (both[2 * rows :] + dot(r_high, v_low, NT)))
+        for j, o in enumerate(products(i, 1, rows, modes, recv_refs, high_refs, low_refs)):
+            m = i * modes + j
+            solved.append(o + begun_ref[m * 2 * rows : (m + 1) * 2 * rows])
         even = jnp.concatenate([o[:rows] for o in solved], axis=0)
         odd = jnp.concatenate([o[rows:] for o in solved], axis=0)
         for d in range(0, parts, 2):
@@ -433,15 +448,25 @@
             out_shape=[array(mine * rows, LANES)] * parts,
         )(state, *halos[g], step_high, step_low)
         got = exchanged(sent, "gy")
+        flops = 3 * mine * coef_count**2 * 256
+        begun = call(
+            functools.partial(begin_kernel, rows),
+            6,
+            flops,
+            2 * mine * coef_count**2,
+            in_specs=[VMEM] * 6,
+            out_specs=VMEM,
+            out_shape=array(mine * 2 * rows, coef_count),
+        )(*got[:2], *high, *low)
         solved = call(
             functools.partial(solve_kernel, parts, rows),
             6,
-            3 * 2 * mine * coef_count**2 * 256,
-            4 * mine * coef_count**2,
-            in_specs=[VMEM] * (parts + 5),
+            flops,
+            2 * mine * coef_count**2,
+            in_specs=[VMEM] * 8,
             out_specs=[VMEM] * parts,
             out_shape=[array((mine + 1) * rows + -(mine + 1) * rows % TILE, LANES)] * parts,
-        )(*got, *high, *low, wall)
+        )(*got[2:], *high, *low, begun, wall)
         returned = exchanged(solved, "gy")
 
         outputs = call(

time: 82.9 us -> 86 us (1.037)
  waiting for transfers between devices: 28.4 us -> 30.2 us
  Pallas kernels: 16.8 us -> 17.8 us
    ppermute x18, waiting for transfers between devices: 9.36 us -> 11.2 us  [exchanged(): got[d] = lax.ppermute(pieces[d], axis, [(i, i ^ d) for i in range(n)])]
    pallas_call x3 -> x6, Pallas kernels: 7.52 us -> 8.53 us  [the longest x3 4.49 us: per_device(): call(functools.partial(solve_kernel, parts, rows), 6, flops, 2 * mine * c...]
  transfers between devices with their start and end apart: 29 -> 29, of which waited for: 9 -> 11; matrix products, arithmetic and copies ran while one was open for 0% -> 0% of each run, Pallas kernels for 19% -> 19%
where the time goes in v5:
time: 86 us; the launch traced here: 85.8 us
  starting transfers between devices  32 us (37%)
  waiting for transfers between devices  30.2 us (35%)
  Pallas kernels  17.8 us (21%)
  local copies, waits for them, and re-layouts  4.82 us (6%)
  between operations  0.92 us (1%)
    ppermute x5, waiting for transfers between devices, full_sum(): other = lax.ppermute(x, axis, [(i, i ^ hop) for i in range(n)])  19 us
    ppermute x18, starting transfers between devices, exchanged(): got[d] = lax.ppermute(pieces[d], axis, [(i, i ^ d) for i in range(n)])  14.4 us
    ppermute x18, waiting for transfers between devices, exchanged(): got[d] = lax.ppermute(pieces[d], axis, [(i, i ^ d) for i in range(n)])  11.2 us
    ppermute x3, starting transfers between devices, per_device(): far = lax.ppermute(far, 'gx', far_pairs)  9.02 us
    ppermute x3, starting transfers between devices, per_device(): near = lax.ppermute(near, 'gx', near_pairs)  4.84 us
    unnamed x16, local copies, waits for them, and re-layouts  4.82 us
    pallas_call x3, Pallas kernels, per_device(): call(functools.partial(solve_kernel, parts, rows), 6, flops, 2 * mine * c...  4.49 us
    pallas_call x3, Pallas kernels, per_device(): call(functools.partial(begin_kernel, rows), 6, flops, 2 * mine * coef_cou...  4.04 us
  transfers between devices with their start and end apart: 29, of which 11 were waited for; matrix products, arithmetic and copies ran while one was open for 0% of the time, Pallas kernels for 19%

profile of v5, /device:TPU:0, one launch (start us, length us, event | category | flops | bytes accessed | tf_op | source)
XLA Modules:
  0.0 85.8 jit_solution(17863125520506919636)
XLA Ops:
  0.6 0.0 copy-start
  0.6 1.4 %copy-done = f32[12,4,64,128]{3,2,1,0:T(8,128)S(1)} copy-done((f32[12,4,64,128]{3,2,1,0:T(8,128)S(1)}, f32[12,4,64,128]{3,2,1,0:T(8,128)}, u32[]{:S(2)}) %copy-start) | copy-done | bytes 1572888
  2.0 0.2 shard_map.97
  2.2 3.0 %collective-permute-start.21 = (f32[4,2,64,128]{3,2,1,0:T(8,128)S(1)}, f32[4,2,64,128]{3,2,1,0:T(8,128)S(1)}, u32[]{:S(2)}, u32[]{:S(2)}) collective-permute-start(f32[4,2,64,128]{3,2,1,0:T(8,128)S(1)} %get-tuple-element.64), channel_id=1, source_target_pairs={{0,4},{4,0},{8,12},{12,8},{16,20},{20,16},{24,28},{28,24},{1,5},{5... | collective-permute-start | bytes 786440 | tf_op jit(solution)/shard_map/ppermute | solution.py:415
  5.3 3.6 %collective-permute-start.22 = (f32[4,2,64,128]{3,2,1,0:T(8,128)S(1)}, f32[4,2,64,128]{3,2,1,0:T(8,128)S(1)}, u32[]{:S(2)}, u32[]{:S(2)}) collective-permute-start(f32[4,2,64,128]{3,2,1,0:T(8,128)S(1)} %get-tuple-element.65), channel_id=1, source_target_pairs={{0,28},{4,8},{8,4},{12,16},{16,12},{20,24},{24,20},{28,0},{1,29},{... | collective-permute-start | bytes 786440 | tf_op jit(solution)/shard_map/ppermute | solution.py:416
  8.9 0.2 shard_map.93
  9.1 0.0 copy-start.1
  9.1 0.1 collective-permute-start.13
  9.1 0.0 copy-start.3
  9.2 0.0 copy-start.4
  9.2 1.9 %collective-permute-start.14 = (f32[4,2,64,128]{3,2,1,0:T(8,128)S(1)}, f32[4,2,64,128]{3,2,1,0:T(8,128)S(1)}, u32[]{:S(2)}, u32[]{:S(2)}) collective-permute-start(f32[4,2,64,128]{3,2,1,0:T(8,128)S(1)} %get-tuple-element.55), channel_id=1, source_target_pairs={{0,28},{4,8},{8,4},{12,16},{16,12},{20,24},{24,20},{28,0},{1,29},{... | collective-permute-start | bytes 786440 | tf_op jit(solution)/shard_map/ppermute | solution.py:416
  11.1 0.2 shard_map.92
  11.3 0.1 collective-permute-start.8
  11.4 1.2 %collective-permute-done.8 = f32[24,128]{1,0:T(8,128)S(1)} collective-permute-done((f32[24,128]{1,0:T(8,128)S(1)}, f32[24,128]{1,0:T(8,128)S(1)}, u32[]{:S(2)}, u32[]{:S(2)}) %collective-permute-start.8) | collective-permute-done | bytes 12320 | tf_op jit(solution)/shard_map/ppermute | solution.py:346
  12.5 1.5 %collective-permute-start.9 = (f32[24,128]{1,0:T(8,128)S(1)}, f32[24,128]{1,0:T(8,128)S(1)}, u32[]{:S(2)}, u32[]{:S(2)}) collective-permute-start(f32[24,128]{1,0:T(8,128)S(1)} %add.15), channel_id=1, source_target_pairs={{0,2},{1,3},{2,0},{3,1},{4,6},{5,7},{6,4},{7,5},{8,10},{9,11},{10,... | collective-permute-start | bytes 36872 | tf_op jit(solution)/shard_map/ppermute | solution.py:346
  14.1 2.2 %collective-permute-done.9 = f32[24,128]{1,0:T(8,128)S(1)} collective-permute-done((f32[24,128]{1,0:T(8,128)S(1)}, f32[24,128]{1,0:T(8,128)S(1)}, u32[]{:S(2)}, u32[]{:S(2)}) %collective-permute-start.9) | collective-permute-done | bytes 12320 | tf_op jit(solution)/shard_map/ppermute | solution.py:346
  16.2 0.6 collective-permute-start.10
  16.8 0.2 shard_map.86
  17.0 11.7 %collective-permute-done.10 = f32[24,128]{1,0:T(8,128)S(1)} collective-permute-done((f32[24,128]{1,0:T(8,128)S(1)}, f32[24,128]{1,0:T(8,128)S(1)}, u32[]{:S(2)}, u32[]{:S(2)}) %collective-permute-start.10) | collective-permute-done | bytes 12320 | tf_op jit(solution)/shard_map/ppermute | solution.py:346
  28.7 1.7 %collective-permute-start = (f32[4,2,64,128]{3,2,1,0:T(8,128)S(1)}, f32[4,2,64,128]{3,2,1,0:T(8,128)S(1)}, u32[]{:S(2)}, u32[]{:S(2)}) collective-permute-start(f32[4,2,64,128]{3,2,1,0:T(8,128)S(1)} %get-tuple-element.40), channel_id=1, source_target_pairs={{0,4},{4,0},{8,12},{12,8},{16,20},{20,16},{24,28},{28,24},{1,5},{5... | collective-permute-start | bytes 786440 | tf_op jit(solution)/shard_map/ppermute | solution.py:415
  30.4 3.6 %collective-permute-start.1 = (f32[4,2,64,128]{3,2,1,0:T(8,128)S(1)}, f32[4,2,64,128]{3,2,1,0:T(8,128)S(1)}, u32[]{:S(2)}, u32[]{:S(2)}) collective-permute-start(f32[4,2,64,128]{3,2,1,0:T(8,128)S(1)} %get-tuple-element.41), channel_id=1, source_target_pairs={{0,28},{4,8},{8,4},{12,16},{16,12},{20,24},{24,20},{28,0},{1,29},{... | collective-permute-start | bytes 786440 | tf_op jit(solution)/shard_map/ppermute | solution.py:416
  34.1 0.6 shard_map.98
  34.7 4.0 %collective-permute-done.11 = f32[24,128]{1,0:T(8,128)S(1)} collective-permute-done((f32[24,128]{1,0:T(8,128)S(1)}, f32[24,128]{1,0:T(8,128)S(1)}, u32[]{:S(2)}, u32[]{:S(2)}) %collective-permute-start.11) | collective-permute-done | bytes 12320 | tf_op jit(solution)/shard_map/ppermute | solution.py:346
  38.7 3.4 %copy-done.2 = f32[32,256,256]{2,1,0:T(8,128)S(1)} copy-done((f32[32,256,256]{2,1,0:T(8,128)S(1)}, f32[32,256,256]{2,1,0:T(8,128)}, u32[]{:S(2)}) %copy-start.2) | copy-done | bytes 8388632
  42.1 1.5 %shard_map.89 = (bf16[16,256,256]{2,1,0:T(8,128)(2,1)S(1)}, bf16[16,256,256]{2,1,0:T(8,128)(2,1)S(1)}) custom-call(f32[32,256,256]{2,1,0:T(8,128)S(1)} %copy-done.2), custom_call_target="tpu_custom_call" | custom-call | flops 10000000 | bytes 8388608 | tf_op jit(solution)/shard_map/pallas_call | solution.py:425
  43.6 1.5 %shard_map.88 = (bf16[16,256,256]{2,1,0:T(8,128)(2,1)S(1)}, bf16[16,256,256]{2,1,0:T(8,128)(2,1)S(1)}) custom-call(f32[32,256,256]{2,1,0:T(8,128)S(1)} %copy-done.2), custom_call_target="tpu_custom_call" | custom-call | flops 10000000 | bytes 8388608 | tf_op jit(solution)/shard_map/pallas_call | solution.py:425
  45.1 1.6 %collective-permute-start.12 = (f32[24,128]{1,0:T(8,128)S(1)}, f32[24,128]{1,0:T(8,128)S(1)}, u32[]{:S(2)}, u32[]{:S(2)}) collective-permute-start(f32[24,128]{1,0:T(8,128)S(1)} %add.18), channel_id=1, source_target_pairs={{0,16},{4,20},{8,24},{12,28},{16,0},{20,4},{24,8},{28,12},{1,17},{... | collective-permute-start | bytes 36872 | tf_op jit(solution)/shard_map/ppermute | solution.py:346
  46.7 0.6 shard_map.94
  47.3 1.6 %collective-permute-start.15 = (f32[256,128]{1,0:T(8,128)S(1)}, f32[256,128]{1,0:T(8,128)S(1)}, u32[]{:S(2)}, u32[]{:S(2)}) collective-permute-start(f32[256,128]{1,0:T(8,128)S(1)} %get-tuple-element.56), channel_id=1, source_target_pairs={{0,2},{1,3},{2,0},{3,1},{4,6},{5,7},{6,4},{7,5},{8,10},{9,11},{10,... | collective-permute-start | bytes 393224 | tf_op jit(solution)/shard_map/ppermute | solution.py:328
  48.9 0.1 collective-permute-start.16
  49.0 0.6 collective-permute-start.17
  49.5 0.6 shard_map.87
  50.2 0.1 collective-permute-start.4
  50.3 1.3 %shard_map.99.refs_6_ = f32[512,256]{1,0:T(8,128)S(1)} custom-call(f32[256,128]{1,0:T(8,128)S(1)} %get-tuple-element.68.refs_0_, f32[256,128]{1,0:T(8,128)S(1)} %collective-permute-done.25.refs_1_, bf16[16,256,256]{2,1,0:T(8,128)(2,1)S(1)} %get-tuple-element.44.refs_2_, bf16[16,256,256]{2,1,0:T(8,128)(2,1)S(1)} %get-tuple-element.45.refs_3_, ...), custom_call_target="tpu_custom_call" | custom-call | flops 1610612736 | bytes 4194304 | tf_op jit(solution)/shard_map/pallas_call | solution.py:452
  51.6 1.5 %collective-permute-start.23 = (f32[256,128]{1,0:T(8,128)S(1)}, f32[256,128]{1,0:T(8,128)S(1)}, u32[]{:S(2)}, u32[]{:S(2)}) collective-permute-start(f32[256,128]{1,0:T(8,128)S(1)} %get-tuple-element.66), channel_id=1, source_target_pairs={{0,2},{1,3},{2,0},{3,1},{4,6},{5,7},{6,4},{7,5},{8,10},{9,11},{10,... | collective-permute-start | bytes 393224 | tf_op jit(solution)/shard_map/ppermute | solution.py:328
  53.2 1.3 %shard_map.95.refs_6_ = f32[512,256]{1,0:T(8,128)S(1)} custom-call(f32[256,128]{1,0:T(8,128)S(1)} %get-tuple-element.58.refs_0_, f32[256,128]{1,0:T(8,128)S(1)} %collective-permute-done.17.refs_1_, bf16[16,256,256]{2,1,0:T(8,128)(2,1)S(1)} %get-tuple-element.44.refs_2_, bf16[16,256,256]{2,1,0:T(8,128)(2,1)S(1)} %get-tuple-element.45.refs_3_, ...), custom_call_target="tpu_custom_call" | custom-call | flops 1610612736 | bytes 4194304 | tf_op jit(solution)/shard_map/pallas_call | solution.py:452
  54.5 0.3 collective-permute-start.24
  54.9 1.4 %shard_map.90.refs_6_ = f32[512,256]{1,0:T(8,128)S(1)} custom-call(f32[256,128]{1,0:T(8,128)S(1)} %get-tuple-element.48.refs_0_, f32[256,128]{1,0:T(8,128)S(1)} %collective-permute-done.4.refs_1_, bf16[16,256,256]{2,1,0:T(8,128)(2,1)S(1)} %get-tuple-element.44.refs_2_, bf16[16,256,256]{2,1,0:T(8,128)(2,1)S(1)} %get-tuple-element.45.refs_3_, ...), custom_call_target="tpu_custom_call" | custom-call | flops 1610612736 | bytes 4194304 | tf_op jit(solution)/shard_map/pallas_call | solution.py:452
  56.2 3.2 %collective-permute-done.23.refs_0_ = f32[256,128]{1,0:T(8,128)S(1)} collective-permute-done((f32[256,128]{1,0:T(8,128)S(1)}, f32[256,128]{1,0:T(8,128)S(1)}, u32[]{:S(2)}, u32[]{:S(2)}) %collective-permute-start.23) | collective-permute-done | bytes 131104 | tf_op jit(solution)/shard_map/ppermute | solution.py:328
  59.4 1.5 %collective-permute-start.2 = (f32[256,128]{1,0:T(8,128)S(1)}, f32[256,128]{1,0:T(8,128)S(1)}, u32[]{:S(2)}, u32[]{:S(2)}) collective-permute-start(f32[256,128]{1,0:T(8,128)S(1)} %get-tuple-element.42), channel_id=1, source_target_pairs={{0,2},{1,3},{2,0},{3,1},{4,6},{5,7},{6,4},{7,5},{8,10},{9,11},{10,... | collective-permute-start | bytes 393224 | tf_op jit(solution)/shard_map/ppermute | solution.py:328
  60.9 0.3 collective-permute-done.24.refs_1_
  61.2 1.9 %collective-permute-start.3 = (f32[256,128]{1,0:T(8,128)S(1)}, f32[256,128]{1,0:T(8,128)S(1)}, u32[]{:S(2)}, u32[]{:S(2)}) collective-permute-start(f32[256,128]{1,0:T(8,128)S(1)} %get-tuple-element.43), channel_id=1, source_target_pairs={{0,3},{1,2},{2,1},{3,0},{4,7},{5,6},{6,5},{7,4},{8,11},{9,10},{10,... | collective-permute-start | bytes 393224 | tf_op jit(solution)/shard_map/ppermute | solution.py:328
  63.1 1.5 %shard_map.100 = (f32[264,128]{1,0:T(8,128)S(1)}, f32[264,128]{1,0:T(8,128)S(1)}, f32[264,128]{1,0:T(8,128)S(1)}, f32[264,128]{1,0:T(8,128)S(1)}) custom-call(f32[256,128]{1,0:T(8,128)S(1)} %collective-permute-done.23.refs_0_, f32[256,128]{1,0:T(8,128)S(1)} %collective-permute-done.24.refs_1_, bf16[16,256,256]{2,1,0:T(8,128)(2,1)S(1)} %get-tuple-element.44.refs_2_, ...), custom_call_target="tpu_custom_call" | custom-call | flops 1610612736 | bytes 4194304 | tf_op jit(solution)/shard_map/pallas_call | solution.py:461
  64.6 0.1 collective-permute-start.26
  64.7 0.6 collective-permute-start.27
  65.3 1.5 %shard_map.96 = (f32[264,128]{1,0:T(8,128)S(1)}, f32[264,128]{1,0:T(8,128)S(1)}, f32[264,128]{1,0:T(8,128)S(1)}, f32[264,128]{1,0:T(8,128)S(1)}) custom-call(f32[256,128]{1,0:T(8,128)S(1)} %collective-permute-done.15.refs_0_, f32[256,128]{1,0:T(8,128)S(1)} %collective-permute-done.16.refs_1_, bf16[16,256,256]{2,1,0:T(8,128)(2,1)S(1)} %get-tuple-element.44.refs_2_, ...), custom_call_target="tpu_custom_call" | custom-call | flops 1610612736 | bytes 4194304 | tf_op jit(solution)/shard_map/pallas_call | solution.py:461
  66.8 0.0 collective-permute-done.12
  66.8 1.3 %collective-permute-start.28 = (f32[264,128]{1,0:T(8,128)S(1)}, f32[264,128]{1,0:T(8,128)S(1)}, u32[]{:S(2)}, u32[]{:S(2)}) collective-permute-start(f32[264,128]{1,0:T(8,128)S(1)} %get-tuple-element.73), channel_id=1, source_target_pairs={{0,3},{1,2},{2,1},{3,0},{4,7},{5,6},{6,5},{7,4},{8,11},{9,10},{10,... | collective-permute-start | bytes 405512 | tf_op jit(solution)/shard_map/ppermute | solution.py:328
  68.1 0.4 collective-permute-start.18
  68.5 0.5 collective-permute-start.19
  69.0 1.0 %collective-permute-start.20 = (f32[264,128]{1,0:T(8,128)S(1)}, f32[264,128]{1,0:T(8,128)S(1)}, u32[]{:S(2)}, u32[]{:S(2)}) collective-permute-start(f32[264,128]{1,0:T(8,128)S(1)} %get-tuple-element.63), channel_id=1, source_target_pairs={{0,3},{1,2},{2,1},{3,0},{4,7},{5,6},{6,5},{7,4},{8,11},{9,10},{10,... | collective-permute-start | bytes 405512 | tf_op jit(solution)/shard_map/ppermute | solution.py:328
  70.0 1.5 %shard_map.91 = (f32[264,128]{1,0:T(8,128)S(1)}, f32[264,128]{1,0:T(8,128)S(1)}, f32[264,128]{1,0:T(8,128)S(1)}, f32[264,128]{1,0:T(8,128)S(1)}) custom-call(f32[256,128]{1,0:T(8,128)S(1)} %collective-permute-done.2.refs_0_, f32[256,128]{1,0:T(8,128)S(1)} %collective-permute-done.3.refs_1_, bf16[16,256,256]{2,1,0:T(8,128)(2,1)S(1)} %get-tuple-element.44.refs_2_, ...), custom_call_target="tpu_custom_call" | custom-call | flops 1610612736 | bytes 4194304 | tf_op jit(solution)/shard_map/pallas_call | solution.py:461
  71.5 0.0 collective-permute-done.27.refs_2_
  71.5 0.7 collective-permute-start.5
  72.2 0.8 collective-permute-done.28.refs_3_
  73.0 1.2 %collective-permute-start.6 = (f32[264,128]{1,0:T(8,128)S(1)}, f32[264,128]{1,0:T(8,128)S(1)}, u32[]{:S(2)}, u32[]{:S(2)}) collective-permute-start(f32[264,128]{1,0:T(8,128)S(1)} %get-tuple-element.52), channel_id=1, source_target_pairs={{0,2},{1,3},{2,0},{3,1},{4,6},{5,7},{6,4},{7,5},{8,10},{9,11},{10,... | collective-permute-start | bytes 405512 | tf_op jit(solution)/shard_map/ppermute | solution.py:328
  74.3 1.0 %collective-permute-start.7 = (f32[264,128]{1,0:T(8,128)S(1)}, f32[264,128]{1,0:T(8,128)S(1)}, u32[]{:S(2)}, u32[]{:S(2)}) collective-permute-start(f32[264,128]{1,0:T(8,128)S(1)} %get-tuple-element.53), channel_id=1, source_target_pairs={{0,3},{1,2},{2,1},{3,0},{4,7},{5,6},{6,5},{7,4},{8,11},{9,10},{10,... | collective-permute-start | bytes 405512 | tf_op jit(solution)/shard_map/ppermute | solution.py:328
  75.3 1.2 %shard_map.101 = (f32[12,4,64,128]{3,2,1,0:T(8,128)}, f32[12,2,2,128]{3,2,1,0:T(2,128)}) custom-call(f32[264,128]{1,0:T(8,128)S(1)} %get-tuple-element.70.refs_0_, f32[264,128]{1,0:T(8,128)S(1)} %collective-permute-done.26.refs_1_, f32[264,128]{1,0:T(8,128)S(1)} %collective-permute-done.27.refs_2_, f32[264,128]{1,0:T(8,128)S(1)} %collective-permute-done.28.refs_3_, ...), custom_call_target="tpu_custom_call" | custom-call | flops 100663296 | bytes 1048576 | tf_op jit(solution)/shard_map/pallas_call | solution.py:472
  76.5 0.5 collective-permute-done.19.refs_2_
  77.0 1.8 %collective-permute-done.20.refs_3_ = f32[264,128]{1,0:T(8,128)S(1)} collective-permute-done((f32[264,128]{1,0:T(8,128)S(1)}, f32[264,128]{1,0:T(8,128)S(1)}, u32[]{:S(2)}, u32[]{:S(2)}) %collective-permute-start.20) | collective-permute-done | bytes 135200 | tf_op jit(solution)/shard_map/ppermute | solution.py:328
  78.8 1.2 %shard_map.102 = (f32[12,4,64,128]{3,2,1,0:T(8,128)}, f32[12,2,2,128]{3,2,1,0:T(2,128)}) custom-call(f32[264,128]{1,0:T(8,128)S(1)} %get-tuple-element.60.refs_0_, f32[264,128]{1,0:T(8,128)S(1)} %collective-permute-done.18.refs_1_, f32[264,128]{1,0:T(8,128)S(1)} %collective-permute-done.19.refs_2_, ...), custom_call_target="tpu_custom_call", output_to_operand_aliasing={{0}: (7, {}), {1}: (8, {})} | custom-call | flops 100663296 | bytes 1048576 | tf_op jit(solution)/shard_map/pallas_call | solution.py:472
  80.0 2.8 %collective-permute-done.6.refs_2_ = f32[264,128]{1,0:T(8,128)S(1)} collective-permute-done((f32[264,128]{1,0:T(8,128)S(1)}, f32[264,128]{1,0:T(8,128)S(1)}, u32[]{:S(2)}, u32[]{:S(2)}) %collective-permute-start.6) | collective-permute-done | bytes 135200 | tf_op jit(solution)/shard_map/ppermute | solution.py:328
  82.8 1.8 %collective-permute-done.7.refs_3_ = f32[264,128]{1,0:T(8,128)S(1)} collective-permute-done((f32[264,128]{1,0:T(8,128)S(1)}, f32[264,128]{1,0:T(8,128)S(1)}, u32[]{:S(2)}, u32[]{:S(2)}) %collective-permute-start.7) | collective-permute-done | bytes 135200 | tf_op jit(solution)/shard_map/ppermute | solution.py:328
  84.6 1.2 %shard_map.103 = (f32[12,4,64,128]{3,2,1,0:T(8,128)}, f32[12,2,2,128]{3,2,1,0:T(2,128)}) custom-call(f32[264,128]{1,0:T(8,128)S(1)} %get-tuple-element.50.refs_0_, f32[264,128]{1,0:T(8,128)S(1)} %collective-permute-done.5.refs_1_, f32[264,128]{1,0:T(8,128)S(1)} %collective-permute-done.6.refs_2_, ...), custom_call_target="tpu_custom_call", output_to_operand_aliasing={{0}: (7, {}), {1}: (8, {})} | custom-call | flops 100663296 | bytes 1048576 | tf_op jit(solution)/shard_map/pallas_call | solution.py:472
  (33 shorter events, 0.1 us)
Async XLA Ops:
  0.6 1.4 %copy-start = (f32[12,4,64,128]{3,2,1,0:T(8,128)S(1)}, f32[12,4,64,128]{3,2,1,0:T(8,128)}, u32[]{:S(2)}) copy-start(f32[12,4,64,128]{3,2,1,0:T(8,128)} %state_ref.13) | copy-start | bytes 4718596
  2.2 28.2 %collective-permute-start.21 = (f32[4,2,64,128]{3,2,1,0:T(8,128)S(1)}, f32[4,2,64,128]{3,2,1,0:T(8,128)S(1)}, u32[]{:S(2)}, u32[]{:S(2)}) collective-permute-start(f32[4,2,64,128]{3,2,1,0:T(8,128)S(1)} %get-tuple-element.64), channel_id=1, source_target_pairs={{0,4},{4,0},{8,12},{12,8},{16,20},{20,16},{24,28},{28,24},{1,5},{5... | collective-permute-start | bytes 786440 | tf_op jit(solution)/shard_map/ppermute | solution.py:415
  5.3 28.7 %collective-permute-start.22 = (f32[4,2,64,128]{3,2,1,0:T(8,128)S(1)}, f32[4,2,64,128]{3,2,1,0:T(8,128)S(1)}, u32[]{:S(2)}, u32[]{:S(2)}) collective-permute-start(f32[4,2,64,128]{3,2,1,0:T(8,128)S(1)} %get-tuple-element.65), channel_id=1, source_target_pairs={{0,28},{4,8},{8,4},{12,16},{16,12},{20,24},{24,20},{28,0},{1,29},{... | collective-permute-start | bytes 786440 | tf_op jit(solution)/shard_map/ppermute | solution.py:416
  9.1 7.8 %copy-start.1 = (f32[12,4,64,128]{3,2,1,0:T(8,128)S(1)}, f32[12,4,64,128]{3,2,1,0:T(8,128)}, u32[]{:S(2)}) copy-start(f32[12,4,64,128]{3,2,1,0:T(8,128)} %state_ref.13) | copy-start | bytes 4718596
  9.1 36.0 %collective-permute-start.13 = (f32[4,2,64,128]{3,2,1,0:T(8,128)S(1)}, f32[4,2,64,128]{3,2,1,0:T(8,128)S(1)}, u32[]{:S(2)}, u32[]{:S(2)}) collective-permute-start(f32[4,2,64,128]{3,2,1,0:T(8,128)S(1)} %get-tuple-element.54), channel_id=1, source_target_pairs={{0,4},{4,0},{8,12},{12,8},{16,20},{20,16},{24,28},{28,24},{1,5},{5... | collective-permute-start | bytes 786440 | tf_op jit(solution)/shard_map/ppermute | solution.py:415
  9.1 24.9 %copy-start.3 = (bf16[2,256,512]{2,1,0:T(8,128)(2,1)S(1)}, bf16[2,256,512]{2,1,0:T(8,128)(2,1)}, u32[]{:S(2)}) copy-start(bf16[2,256,512]{2,1,0:T(8,128)(2,1)} %constant.11.clone.low_ref) | copy-start | bytes 1572868
  9.2 24.9 %copy-start.4 = (bf16[2,256,512]{2,1,0:T(8,128)(2,1)S(1)}, bf16[2,256,512]{2,1,0:T(8,128)(2,1)}, u32[]{:S(2)}) copy-start(bf16[2,256,512]{2,1,0:T(8,128)(2,1)} %constant.10.clone.high_ref) | copy-start | bytes 1572868
  9.2 37.5 %collective-permute-start.14 = (f32[4,2,64,128]{3,2,1,0:T(8,128)S(1)}, f32[4,2,64,128]{3,2,1,0:T(8,128)S(1)}, u32[]{:S(2)}, u32[]{:S(2)}) collective-permute-start(f32[4,2,64,128]{3,2,1,0:T(8,128)S(1)} %get-tuple-element.55), channel_id=1, source_target_pairs={{0,28},{4,8},{8,4},{12,16},{16,12},{20,24},{24,20},{28,0},{1,29},{... | collective-permute-start | bytes 786440 | tf_op jit(solution)/shard_map/ppermute | solution.py:416
  11.3 1.2 %collective-permute-start.8 = (f32[24,128]{1,0:T(8,128)S(1)}, f32[24,128]{1,0:T(8,128)S(1)}, u32[]{:S(2)}, u32[]{:S(2)}) collective-permute-start(f32[24,128]{1,0:T(8,128)S(1)} %shard_map.92), channel_id=1, source_target_pairs={{0,1},{1,0},{2,3},{3,2},{4,5},{5,4},{6,7},{7,6},{8,9},{9,8},{10,11... | collective-permute-start | bytes 36872 | tf_op jit(solution)/shard_map/ppermute | solution.py:346
  12.5 3.7 %collective-permute-start.9 = (f32[24,128]{1,0:T(8,128)S(1)}, f32[24,128]{1,0:T(8,128)S(1)}, u32[]{:S(2)}, u32[]{:S(2)}) collective-permute-start(f32[24,128]{1,0:T(8,128)S(1)} %add.15), channel_id=1, source_target_pairs={{0,2},{1,3},{2,0},{3,1},{4,6},{5,7},{6,4},{7,5},{8,10},{9,11},{10,... | collective-permute-start | bytes 36872 | tf_op jit(solution)/shard_map/ppermute | solution.py:346
  16.2 12.5 %collective-permute-start.10 = (f32[24,128]{1,0:T(8,128)S(1)}, f32[24,128]{1,0:T(8,128)S(1)}, u32[]{:S(2)}, u32[]{:S(2)}) collective-permute-start(f32[24,128]{1,0:T(8,128)S(1)} %add.16), channel_id=1, source_target_pairs={{0,4},{4,0},{8,12},{12,8},{16,20},{20,16},{24,28},{28,24},{1,5},{5... | collective-permute-start | bytes 36872 | tf_op jit(solution)/shard_map/ppermute | solution.py:346
  28.7 20.2 %collective-permute-start = (f32[4,2,64,128]{3,2,1,0:T(8,128)S(1)}, f32[4,2,64,128]{3,2,1,0:T(8,128)S(1)}, u32[]{:S(2)}, u32[]{:S(2)}) collective-permute-start(f32[4,2,64,128]{3,2,1,0:T(8,128)S(1)} %get-tuple-element.40), channel_id=1, source_target_pairs={{0,4},{4,0},{8,12},{12,8},{16,20},{20,16},{24,28},{28,24},{1,5},{5... | collective-permute-start | bytes 786440 | tf_op jit(solution)/shard_map/ppermute | solution.py:415
  30.4 18.5 %collective-permute-start.1 = (f32[4,2,64,128]{3,2,1,0:T(8,128)S(1)}, f32[4,2,64,128]{3,2,1,0:T(8,128)S(1)}, u32[]{:S(2)}, u32[]{:S(2)}) collective-permute-start(f32[4,2,64,128]{3,2,1,0:T(8,128)S(1)} %get-tuple-element.41), channel_id=1, source_target_pairs={{0,28},{4,8},{8,4},{12,16},{16,12},{20,24},{24,20},{28,0},{1,29},{... | collective-permute-start | bytes 786440 | tf_op jit(solution)/shard_map/ppermute | solution.py:416
  34.0 4.7 %collective-permute-start.11 = (f32[24,128]{1,0:T(8,128)S(1)}, f32[24,128]{1,0:T(8,128)S(1)}, u32[]{:S(2)}, u32[]{:S(2)}) collective-permute-start(f32[24,128]{1,0:T(8,128)S(1)} %add.17), channel_id=1, source_target_pairs={{0,8},{4,12},{8,0},{12,4},{16,24},{20,28},{24,16},{28,20},{1,9},{5... | collective-permute-start | bytes 36872 | tf_op jit(solution)/shard_map/ppermute | solution.py:346
  38.7 11.5 %collective-permute-start.25 = (f32[256,128]{1,0:T(8,128)S(1)}, f32[256,128]{1,0:T(8,128)S(1)}, u32[]{:S(2)}, u32[]{:S(2)}) collective-permute-start(f32[256,128]{1,0:T(8,128)S(1)} %get-tuple-element.69), channel_id=1, source_target_pairs={{0,1},{1,0},{2,3},{3,2},{4,5},{5,4},{6,7},{7,6},{8,9},{9,8},{10,11... | collective-permute-start | bytes 393224 | tf_op jit(solution)/shard_map/ppermute | solution.py:328
  38.7 3.4 %copy-start.2 = (f32[32,256,256]{2,1,0:T(8,128)S(1)}, f32[32,256,256]{2,1,0:T(8,128)}, u32[]{:S(2)}) copy-start(f32[32,256,256]{2,1,0:T(8,128)} %inverse_ref.3) | copy-start | bytes 25165828
  45.1 21.7 %collective-permute-start.12 = (f32[24,128]{1,0:T(8,128)S(1)}, f32[24,128]{1,0:T(8,128)S(1)}, u32[]{:S(2)}, u32[]{:S(2)}) collective-permute-start(f32[24,128]{1,0:T(8,128)S(1)} %add.18), channel_id=1, source_target_pairs={{0,16},{4,20},{8,24},{12,28},{16,0},{20,4},{24,8},{28,12},{1,17},{... | collective-permute-start | bytes 36872 | tf_op jit(solution)/shard_map/ppermute | solution.py:346
  47.3 17.3 %collective-permute-start.15 = (f32[256,128]{1,0:T(8,128)S(1)}, f32[256,128]{1,0:T(8,128)S(1)}, u32[]{:S(2)}, u32[]{:S(2)}) collective-permute-start(f32[256,128]{1,0:T(8,128)S(1)} %get-tuple-element.56), channel_id=1, source_target_pairs={{0,2},{1,3},{2,0},{3,1},{4,6},{5,7},{6,4},{7,5},{8,10},{9,11},{10,... | collective-permute-start | bytes 393224 | tf_op jit(solution)/shard_map/ppermute | solution.py:328
  48.9 15.8 %collective-permute-start.16 = (f32[256,128]{1,0:T(8,128)S(1)}, f32[256,128]{1,0:T(8,128)S(1)}, u32[]{:S(2)}, u32[]{:S(2)}) collective-permute-start(f32[256,128]{1,0:T(8,128)S(1)} %get-tuple-element.57), channel_id=1, source_target_pairs={{0,3},{1,2},{2,1},{3,0},{4,7},{5,6},{6,5},{7,4},{8,11},{9,10},{10,... | collective-permute-start | bytes 393224 | tf_op jit(solution)/shard_map/ppermute | solution.py:328
  49.0 2.7 %collective-permute-start.17 = (f32[256,128]{1,0:T(8,128)S(1)}, f32[256,128]{1,0:T(8,128)S(1)}, u32[]{:S(2)}, u32[]{:S(2)}) collective-permute-start(f32[256,128]{1,0:T(8,128)S(1)} %get-tuple-element.59), channel_id=1, source_target_pairs={{0,1},{1,0},{2,3},{3,2},{4,5},{5,4},{6,7},{7,6},{8,9},{9,8},{10,11... | collective-permute-start | bytes 393224 | tf_op jit(solution)/shard_map/ppermute | solution.py:328
  50.2 4.3 %collective-permute-start.4 = (f32[256,128]{1,0:T(8,128)S(1)}, f32[256,128]{1,0:T(8,128)S(1)}, u32[]{:S(2)}, u32[]{:S(2)}) collective-permute-start(f32[256,128]{1,0:T(8,128)S(1)} %get-tuple-element.49), channel_id=1, source_target_pairs={{0,1},{1,0},{2,3},{3,2},{4,5},{5,4},{6,7},{7,6},{8,9},{9,8},{10,11... | collective-permute-start | bytes 393224 | tf_op jit(solution)/shard_map/ppermute | solution.py:328
  51.6 7.7 %collective-permute-start.23 = (f32[256,128]{1,0:T(8,128)S(1)}, f32[256,128]{1,0:T(8,128)S(1)}, u32[]{:S(2)}, u32[]{:S(2)}) collective-permute-start(f32[256,128]{1,0:T(8,128)S(1)} %get-tuple-element.66), channel_id=1, source_target_pairs={{0,2},{1,3},{2,0},{3,1},{4,6},{5,7},{6,4},{7,5},{8,10},{9,11},{10,... | collective-permute-start | bytes 393224 | tf_op jit(solution)/shard_map/ppermute | solution.py:328
  54.5 6.7 %collective-permute-start.24 = (f32[256,128]{1,0:T(8,128)S(1)}, f32[256,128]{1,0:T(8,128)S(1)}, u32[]{:S(2)}, u32[]{:S(2)}) collective-permute-start(f32[256,128]{1,0:T(8,128)S(1)} %get-tuple-element.67), channel_id=1, source_target_pairs={{0,3},{1,2},{2,1},{3,0},{4,7},{5,6},{6,5},{7,4},{8,11},{9,10},{10,... | collective-permute-start | bytes 393224 | tf_op jit(solution)/shard_map/ppermute | solution.py:328
  54.8 8.3 %copy-start.7 = (f32[8,256]{1,0:T(8,128)S(1)}, f32[8,256]{1,0:T(8,128)}, u32[]{:S(2)}) copy-start(f32[8,256]{1,0:T(8,128)} %constant.14.clone.refs_7_) | copy-start | bytes 24580
  59.4 8.8 %collective-permute-start.2 = (f32[256,128]{1,0:T(8,128)S(1)}, f32[256,128]{1,0:T(8,128)S(1)}, u32[]{:S(2)}, u32[]{:S(2)}) collective-permute-start(f32[256,128]{1,0:T(8,128)S(1)} %get-tuple-element.42), channel_id=1, source_target_pairs={{0,2},{1,3},{2,0},{3,1},{4,6},{5,7},{6,4},{7,5},{8,10},{9,11},{10,... | collective-permute-start | bytes 393224 | tf_op jit(solution)/shard_map/ppermute | solution.py:328
  61.2 7.3 %collective-permute-start.3 = (f32[256,128]{1,0:T(8,128)S(1)}, f32[256,128]{1,0:T(8,128)S(1)}, u32[]{:S(2)}, u32[]{:S(2)}) collective-permute-start(f32[256,128]{1,0:T(8,128)S(1)} %get-tuple-element.43), channel_id=1, source_target_pairs={{0,3},{1,2},{2,1},{3,0},{4,7},{5,6},{6,5},{7,4},{8,11},{9,10},{10,... | collective-permute-start | bytes 393224 | tf_op jit(solution)/shard_map/ppermute | solution.py:328
  64.6 4.4 %collective-permute-start.26 = (f32[264,128]{1,0:T(8,128)S(1)}, f32[264,128]{1,0:T(8,128)S(1)}, u32[]{:S(2)}, u32[]{:S(2)}) collective-permute-start(f32[264,128]{1,0:T(8,128)S(1)} %get-tuple-element.71), channel_id=1, source_target_pairs={{0,1},{1,0},{2,3},{3,2},{4,5},{5,4},{6,7},{7,6},{8,9},{9,8},{10,11... | collective-permute-start | bytes 405512 | tf_op jit(solution)/shard_map/ppermute | solution.py:328
  64.7 6.8 %collective-permute-start.27 = (f32[264,128]{1,0:T(8,128)S(1)}, f32[264,128]{1,0:T(8,128)S(1)}, u32[]{:S(2)}, u32[]{:S(2)}) collective-permute-start(f32[264,128]{1,0:T(8,128)S(1)} %get-tuple-element.72), channel_id=1, source_target_pairs={{0,2},{1,3},{2,0},{3,1},{4,6},{5,7},{6,4},{7,5},{8,10},{9,11},{10,... | collective-permute-start | bytes 405512 | tf_op jit(solution)/shard_map/ppermute | solution.py:328
  66.8 6.2 %collective-permute-start.28 = (f32[264,128]{1,0:T(8,128)S(1)}, f32[264,128]{1,0:T(8,128)S(1)}, u32[]{:S(2)}, u32[]{:S(2)}) collective-permute-start(f32[264,128]{1,0:T(8,128)S(1)} %get-tuple-element.73), channel_id=1, source_target_pairs={{0,3},{1,2},{2,1},{3,0},{4,7},{5,6},{6,5},{7,4},{8,11},{9,10},{10,... | collective-permute-start | bytes 405512 | tf_op jit(solution)/shard_map/ppermute | solution.py:328
  68.1 6.1 %collective-permute-start.18 = (f32[264,128]{1,0:T(8,128)S(1)}, f32[264,128]{1,0:T(8,128)S(1)}, u32[]{:S(2)}, u32[]{:S(2)}) collective-permute-start(f32[264,128]{1,0:T(8,128)S(1)} %get-tuple-element.61), channel_id=1, source_target_pairs={{0,1},{1,0},{2,3},{3,2},{4,5},{5,4},{6,7},{7,6},{8,9},{9,8},{10,11... | collective-permute-start | bytes 405512 | tf_op jit(solution)/shard_map/ppermute | solution.py:328
  68.5 8.5 %collective-permute-start.19 = (f32[264,128]{1,0:T(8,128)S(1)}, f32[264,128]{1,0:T(8,128)S(1)}, u32[]{:S(2)}, u32[]{:S(2)}) collective-permute-start(f32[264,128]{1,0:T(8,128)S(1)} %get-tuple-element.62), channel_id=1, source_target_pairs={{0,2},{1,3},{2,0},{3,1},{4,6},{5,7},{6,4},{7,5},{8,10},{9,11},{10,... | collective-permute-start | bytes 405512 | tf_op jit(solution)/shard_map/ppermute | solution.py:328
  69.0 6.3 %copy-start.5 = (bf16[128,128]{1,0:T(8,128)(2,1)S(1)}, bf16[128,128]{1,0:T(8,128)(2,1)}, u32[]{:S(2)}) copy-start(bf16[128,128]{1,0:T(8,128)(2,1)} %constant.13.clone.refs_5_) | copy-start | bytes 98308
  69.0 6.3 %copy-start.6 = (bf16[128,128]{1,0:T(8,128)(2,1)S(1)}, bf16[128,128]{1,0:T(8,128)(2,1)}, u32[]{:S(2)}) copy-start(bf16[128,128]{1,0:T(8,128)(2,1)} %constant.12.clone.refs_4_) | copy-start | bytes 98308
  69.0 9.8 %collective-permute-start.20 = (f32[264,128]{1,0:T(8,128)S(1)}, f32[264,128]{1,0:T(8,128)S(1)}, u32[]{:S(2)}, u32[]{:S(2)}) collective-permute-start(f32[264,128]{1,0:T(8,128)S(1)} %get-tuple-element.63), channel_id=1, source_target_pairs={{0,3},{1,2},{2,1},{3,0},{4,7},{5,6},{6,5},{7,4},{8,11},{9,10},{10,... | collective-permute-start | bytes 405512 | tf_op jit(solution)/shard_map/ppermute | solution.py:328
  71.5 8.5 %collective-permute-start.5 = (f32[264,128]{1,0:T(8,128)S(1)}, f32[264,128]{1,0:T(8,128)S(1)}, u32[]{:S(2)}, u32[]{:S(2)}) collective-permute-start(f32[264,128]{1,0:T(8,128)S(1)} %get-tuple-element.51), channel_id=1, source_target_pairs={{0,1},{1,0},{2,3},{3,2},{4,5},{5,4},{6,7},{7,6},{8,9},{9,8},{10,11... | collective-permute-start | bytes 405512 | tf_op jit(solution)/shard_map/ppermute | solution.py:328
  73.0 9.8 %collective-permute-start.6 = (f32[264,128]{1,0:T(8,128)S(1)}, f32[264,128]{1,0:T(8,128)S(1)}, u32[]{:S(2)}, u32[]{:S(2)}) collective-permute-start(f32[264,128]{1,0:T(8,128)S(1)} %get-tuple-element.52), channel_id=1, source_target_pairs={{0,2},{1,3},{2,0},{3,1},{4,6},{5,7},{6,4},{7,5},{8,10},{9,11},{10,... | collective-permute-start | bytes 405512 | tf_op jit(solution)/shard_map/ppermute | solution.py:328
  74.3 10.4 %collective-permute-start.7 = (f32[264,128]{1,0:T(8,128)S(1)}, f32[264,128]{1,0:T(8,128)S(1)}, u32[]{:S(2)}, u32[]{:S(2)}) collective-permute-start(f32[264,128]{1,0:T(8,128)S(1)} %get-tuple-element.53), channel_id=1, source_target_pairs={{0,3},{1,2},{2,1},{3,0},{4,7},{5,6},{6,5},{7,4},{8,11},{9,10},{10,... | collective-permute-start | bytes 405512 | tf_op jit(solution)/shard_map/ppermute | solution.py:328

commit v6 on v5

--- a/solution.py
+++ b/solution.py
@@ -26,6 +26,7 @@
 ANY = pl.BlockSpec(memory_space=pl.ANY)
 NT = (((1,), (1,)), ((), ()))
 NN = (((1,), (0,)), ((), ()))
+TN = (((0,), (0,)), ((), ()))
 
 
 def window_tables(window, rim_width, points, mode_count):
@@ -276,9 +277,8 @@
     for r in range(rows):
         q, f = divmod(r, fields)
         s = jnp.concatenate([ref[pl.ds(r, slots, stride=rows), :] for ref in recv_refs], axis=0)
-        s = (s * scale[r : r + 1]).T
-        s_high, s_low = split(s)
-        o = dot(s_high, b_high, NN) + (dot(s_high, b_low, NN) + dot(s_low, b_high, NN))
+        s_high, s_low = split(s * scale[r : r + 1])
+        o = dot(s_high, b_high, TN) + (dot(s_high, b_low, TN) + dot(s_low, b_high, TN))
         for e in range(2):
             values_ref[2 * q + e, f] = o[e * coef : (e + 1) * coef]
         if f == fields - 1:

time: 86 us -> 86 us (level)
  no operation moved by 1% of the time
where the time goes in v6:
time: 86 us; the launch traced here: 85.8 us
  starting transfers between devices  32 us (37%)
  waiting for transfers between devices  30.3 us (35%)
  Pallas kernels  17.7 us (21%)
  local copies, waits for them, and re-layouts  4.82 us (6%)
  between operations  0.92 us (1%)
    ppermute x5, waiting for transfers between devices, full_sum(): other = lax.ppermute(x, axis, [(i, i ^ hop) for i in range(n)])  19 us
    ppermute x18, starting transfers between devices, exchanged(): got[d] = lax.ppermute(pieces[d], axis, [(i, i ^ d) for i in range(n)])  14.4 us
    ppermute x18, waiting for transfers between devices, exchanged(): got[d] = lax.ppermute(pieces[d], axis, [(i, i ^ d) for i in range(n)])  11.3 us
    ppermute x3, starting transfers between devices, per_device(): far = lax.ppermute(far, 'gx', far_pairs)  9.02 us
    ppermute x3, starting transfers between devices, per_device(): near = lax.ppermute(near, 'gx', near_pairs)  4.84 us
    unnamed x16, local copies, waits for them, and re-layouts  4.82 us
    pallas_call x3, Pallas kernels, per_device(): call(functools.partial(solve_kernel, parts, rows), 6, flops, 2 * mine * c...  4.49 us
    pallas_call x3, Pallas kernels, per_device(): call(functools.partial(begin_kernel, rows), 6, flops, 2 * mine * coef_cou...  4.04 us
  transfers between devices with their start and end apart: 29, of which 11 were waited for; matrix products, arithmetic and copies ran while one was open for 0% of the time, Pallas kernels for 19%

profile of v6, /device:TPU:0, one launch (start us, length us, event | category | flops | bytes accessed | tf_op | source)
XLA Modules:
  0.0 85.8 jit_solution(15592542593522321588)
XLA Ops:
  0.6 0.0 copy-start
  0.6 1.4 %copy-done = f32[12,4,64,128]{3,2,1,0:T(8,128)S(1)} copy-done((f32[12,4,64,128]{3,2,1,0:T(8,128)S(1)}, f32[12,4,64,128]{3,2,1,0:T(8,128)}, u32[]{:S(2)}) %copy-start) | copy-done | bytes 1572888
  2.0 0.2 shard_map.97
  2.2 3.0 %collective-permute-start.21 = (f32[4,2,64,128]{3,2,1,0:T(8,128)S(1)}, f32[4,2,64,128]{3,2,1,0:T(8,128)S(1)}, u32[]{:S(2)}, u32[]{:S(2)}) collective-permute-start(f32[4,2,64,128]{3,2,1,0:T(8,128)S(1)} %get-tuple-element.64), channel_id=1, source_target_pairs={{0,4},{4,0},{8,12},{12,8},{16,20},{20,16},{24,28},{28,24},{1,5},{5... | collective-permute-start | bytes 786440 | tf_op jit(solution)/shard_map/ppermute | solution.py:415
  5.3 3.6 %collective-permute-start.22 = (f32[4,2,64,128]{3,2,1,0:T(8,128)S(1)}, f32[4,2,64,128]{3,2,1,0:T(8,128)S(1)}, u32[]{:S(2)}, u32[]{:S(2)}) collective-permute-start(f32[4,2,64,128]{3,2,1,0:T(8,128)S(1)} %get-tuple-element.65), channel_id=1, source_target_pairs={{0,28},{4,8},{8,4},{12,16},{16,12},{20,24},{24,20},{28,0},{1,29},{... | collective-permute-start | bytes 786440 | tf_op jit(solution)/shard_map/ppermute | solution.py:416
  8.9 0.2 shard_map.93
  9.1 0.0 copy-start.1
  9.1 0.1 collective-permute-start.13
  9.1 0.0 copy-start.3
  9.2 0.0 copy-start.4
  9.2 1.9 %collective-permute-start.14 = (f32[4,2,64,128]{3,2,1,0:T(8,128)S(1)}, f32[4,2,64,128]{3,2,1,0:T(8,128)S(1)}, u32[]{:S(2)}, u32[]{:S(2)}) collective-permute-start(f32[4,2,64,128]{3,2,1,0:T(8,128)S(1)} %get-tuple-element.55), channel_id=1, source_target_pairs={{0,28},{4,8},{8,4},{12,16},{16,12},{20,24},{24,20},{28,0},{1,29},{... | collective-permute-start | bytes 786440 | tf_op jit(solution)/shard_map/ppermute | solution.py:416
  11.1 0.2 shard_map.92
  11.3 0.1 collective-permute-start.8
  11.4 1.2 %collective-permute-done.8 = f32[24,128]{1,0:T(8,128)S(1)} collective-permute-done((f32[24,128]{1,0:T(8,128)S(1)}, f32[24,128]{1,0:T(8,128)S(1)}, u32[]{:S(2)}, u32[]{:S(2)}) %collective-permute-start.8) | collective-permute-done | bytes 12320 | tf_op jit(solution)/shard_map/ppermute | solution.py:346
  12.5 1.5 %collective-permute-start.9 = (f32[24,128]{1,0:T(8,128)S(1)}, f32[24,128]{1,0:T(8,128)S(1)}, u32[]{:S(2)}, u32[]{:S(2)}) collective-permute-start(f32[24,128]{1,0:T(8,128)S(1)} %add.15), channel_id=1, source_target_pairs={{0,2},{1,3},{2,0},{3,1},{4,6},{5,7},{6,4},{7,5},{8,10},{9,11},{10,... | collective-permute-start | bytes 36872 | tf_op jit(solution)/shard_map/ppermute | solution.py:346
  14.1 2.2 %collective-permute-done.9 = f32[24,128]{1,0:T(8,128)S(1)} collective-permute-done((f32[24,128]{1,0:T(8,128)S(1)}, f32[24,128]{1,0:T(8,128)S(1)}, u32[]{:S(2)}, u32[]{:S(2)}) %collective-permute-start.9) | collective-permute-done | bytes 12320 | tf_op jit(solution)/shard_map/ppermute | solution.py:346
  16.2 0.6 collective-permute-start.10
  16.8 0.2 shard_map.86
  17.0 11.7 %collective-permute-done.10 = f32[24,128]{1,0:T(8,128)S(1)} collective-permute-done((f32[24,128]{1,0:T(8,128)S(1)}, f32[24,128]{1,0:T(8,128)S(1)}, u32[]{:S(2)}, u32[]{:S(2)}) %collective-permute-start.10) | collective-permute-done | bytes 12320 | tf_op jit(solution)/shard_map/ppermute | solution.py:346
  28.7 1.7 %collective-permute-start = (f32[4,2,64,128]{3,2,1,0:T(8,128)S(1)}, f32[4,2,64,128]{3,2,1,0:T(8,128)S(1)}, u32[]{:S(2)}, u32[]{:S(2)}) collective-permute-start(f32[4,2,64,128]{3,2,1,0:T(8,128)S(1)} %get-tuple-element.40), channel_id=1, source_target_pairs={{0,4},{4,0},{8,12},{12,8},{16,20},{20,16},{24,28},{28,24},{1,5},{5... | collective-permute-start | bytes 786440 | tf_op jit(solution)/shard_map/ppermute | solution.py:415
  30.4 3.6 %collective-permute-start.1 = (f32[4,2,64,128]{3,2,1,0:T(8,128)S(1)}, f32[4,2,64,128]{3,2,1,0:T(8,128)S(1)}, u32[]{:S(2)}, u32[]{:S(2)}) collective-permute-start(f32[4,2,64,128]{3,2,1,0:T(8,128)S(1)} %get-tuple-element.41), channel_id=1, source_target_pairs={{0,28},{4,8},{8,4},{12,16},{16,12},{20,24},{24,20},{28,0},{1,29},{... | collective-permute-start | bytes 786440 | tf_op jit(solution)/shard_map/ppermute | solution.py:416
  34.1 0.6 shard_map.98
  34.7 4.0 %collective-permute-done.11 = f32[24,128]{1,0:T(8,128)S(1)} collective-permute-done((f32[24,128]{1,0:T(8,128)S(1)}, f32[24,128]{1,0:T(8,128)S(1)}, u32[]{:S(2)}, u32[]{:S(2)}) %collective-permute-start.11) | collective-permute-done | bytes 12320 | tf_op jit(solution)/shard_map/ppermute | solution.py:346
  38.7 3.4 %copy-done.2 = f32[32,256,256]{2,1,0:T(8,128)S(1)} copy-done((f32[32,256,256]{2,1,0:T(8,128)S(1)}, f32[32,256,256]{2,1,0:T(8,128)}, u32[]{:S(2)}) %copy-start.2) | copy-done | bytes 8388632
  42.1 1.5 %shard_map.89 = (bf16[16,256,256]{2,1,0:T(8,128)(2,1)S(1)}, bf16[16,256,256]{2,1,0:T(8,128)(2,1)S(1)}) custom-call(f32[32,256,256]{2,1,0:T(8,128)S(1)} %copy-done.2), custom_call_target="tpu_custom_call" | custom-call | flops 10000000 | bytes 8388608 | tf_op jit(solution)/shard_map/pallas_call | solution.py:425
  43.6 1.5 %shard_map.88 = (bf16[16,256,256]{2,1,0:T(8,128)(2,1)S(1)}, bf16[16,256,256]{2,1,0:T(8,128)(2,1)S(1)}) custom-call(f32[32,256,256]{2,1,0:T(8,128)S(1)} %copy-done.2), custom_call_target="tpu_custom_call" | custom-call | flops 10000000 | bytes 8388608 | tf_op jit(solution)/shard_map/pallas_call | solution.py:425
  45.1 1.6 %collective-permute-start.12 = (f32[24,128]{1,0:T(8,128)S(1)}, f32[24,128]{1,0:T(8,128)S(1)}, u32[]{:S(2)}, u32[]{:S(2)}) collective-permute-start(f32[24,128]{1,0:T(8,128)S(1)} %add.18), channel_id=1, source_target_pairs={{0,16},{4,20},{8,24},{12,28},{16,0},{20,4},{24,8},{28,12},{1,17},{... | collective-permute-start | bytes 36872 | tf_op jit(solution)/shard_map/ppermute | solution.py:346
  46.7 0.6 shard_map.94
  47.3 1.6 %collective-permute-start.15 = (f32[256,128]{1,0:T(8,128)S(1)}, f32[256,128]{1,0:T(8,128)S(1)}, u32[]{:S(2)}, u32[]{:S(2)}) collective-permute-start(f32[256,128]{1,0:T(8,128)S(1)} %get-tuple-element.56), channel_id=1, source_target_pairs={{0,2},{1,3},{2,0},{3,1},{4,6},{5,7},{6,4},{7,5},{8,10},{9,11},{10,... | collective-permute-start | bytes 393224 | tf_op jit(solution)/shard_map/ppermute | solution.py:328
  48.9 0.1 collective-permute-start.16
  49.0 0.6 collective-permute-start.17
  49.5 0.6 shard_map.87
  50.2 0.1 collective-permute-start.4
  50.3 1.3 %shard_map.99.refs_6_ = f32[512,256]{1,0:T(8,128)S(1)} custom-call(f32[256,128]{1,0:T(8,128)S(1)} %get-tuple-element.68.refs_0_, f32[256,128]{1,0:T(8,128)S(1)} %collective-permute-done.25.refs_1_, bf16[16,256,256]{2,1,0:T(8,128)(2,1)S(1)} %get-tuple-element.44.refs_2_, bf16[16,256,256]{2,1,0:T(8,128)(2,1)S(1)} %get-tuple-element.45.refs_3_, ...), custom_call_target="tpu_custom_call" | custom-call | flops 1610612736 | bytes 4194304 | tf_op jit(solution)/shard_map/pallas_call | solution.py:452
  51.6 1.5 %collective-permute-start.23 = (f32[256,128]{1,0:T(8,128)S(1)}, f32[256,128]{1,0:T(8,128)S(1)}, u32[]{:S(2)}, u32[]{:S(2)}) collective-permute-start(f32[256,128]{1,0:T(8,128)S(1)} %get-tuple-element.66), channel_id=1, source_target_pairs={{0,2},{1,3},{2,0},{3,1},{4,6},{5,7},{6,4},{7,5},{8,10},{9,11},{10,... | collective-permute-start | bytes 393224 | tf_op jit(solution)/shard_map/ppermute | solution.py:328
  53.2 1.3 %shard_map.95.refs_6_ = f32[512,256]{1,0:T(8,128)S(1)} custom-call(f32[256,128]{1,0:T(8,128)S(1)} %get-tuple-element.58.refs_0_, f32[256,128]{1,0:T(8,128)S(1)} %collective-permute-done.17.refs_1_, bf16[16,256,256]{2,1,0:T(8,128)(2,1)S(1)} %get-tuple-element.44.refs_2_, bf16[16,256,256]{2,1,0:T(8,128)(2,1)S(1)} %get-tuple-element.45.refs_3_, ...), custom_call_target="tpu_custom_call" | custom-call | flops 1610612736 | bytes 4194304 | tf_op jit(solution)/shard_map/pallas_call | solution.py:452
  54.5 0.3 collective-permute-start.24
  54.9 1.4 %shard_map.90.refs_6_ = f32[512,256]{1,0:T(8,128)S(1)} custom-call(f32[256,128]{1,0:T(8,128)S(1)} %get-tuple-element.48.refs_0_, f32[256,128]{1,0:T(8,128)S(1)} %collective-permute-done.4.refs_1_, bf16[16,256,256]{2,1,0:T(8,128)(2,1)S(1)} %get-tuple-element.44.refs_2_, bf16[16,256,256]{2,1,0:T(8,128)(2,1)S(1)} %get-tuple-element.45.refs_3_, ...), custom_call_target="tpu_custom_call" | custom-call | flops 1610612736 | bytes 4194304 | tf_op jit(solution)/shard_map/pallas_call | solution.py:452
  56.2 3.2 %collective-permute-done.23.refs_0_ = f32[256,128]{1,0:T(8,128)S(1)} collective-permute-done((f32[256,128]{1,0:T(8,128)S(1)}, f32[256,128]{1,0:T(8,128)S(1)}, u32[]{:S(2)}, u32[]{:S(2)}) %collective-permute-start.23) | collective-permute-done | bytes 131104 | tf_op jit(solution)/shard_map/ppermute | solution.py:328
  59.4 1.5 %collective-permute-start.2 = (f32[256,128]{1,0:T(8,128)S(1)}, f32[256,128]{1,0:T(8,128)S(1)}, u32[]{:S(2)}, u32[]{:S(2)}) collective-permute-start(f32[256,128]{1,0:T(8,128)S(1)} %get-tuple-element.42), channel_id=1, source_target_pairs={{0,2},{1,3},{2,0},{3,1},{4,6},{5,7},{6,4},{7,5},{8,10},{9,11},{10,... | collective-permute-start | bytes 393224 | tf_op jit(solution)/shard_map/ppermute | solution.py:328
  60.9 0.3 collective-permute-done.24.refs_1_
  61.2 1.9 %collective-permute-start.3 = (f32[256,128]{1,0:T(8,128)S(1)}, f32[256,128]{1,0:T(8,128)S(1)}, u32[]{:S(2)}, u32[]{:S(2)}) collective-permute-start(f32[256,128]{1,0:T(8,128)S(1)} %get-tuple-element.43), channel_id=1, source_target_pairs={{0,3},{1,2},{2,1},{3,0},{4,7},{5,6},{6,5},{7,4},{8,11},{9,10},{10,... | collective-permute-start | bytes 393224 | tf_op jit(solution)/shard_map/ppermute | solution.py:328
  63.1 1.5 %shard_map.100 = (f32[264,128]{1,0:T(8,128)S(1)}, f32[264,128]{1,0:T(8,128)S(1)}, f32[264,128]{1,0:T(8,128)S(1)}, f32[264,128]{1,0:T(8,128)S(1)}) custom-call(f32[256,128]{1,0:T(8,128)S(1)} %collective-permute-done.23.refs_0_, f32[256,128]{1,0:T(8,128)S(1)} %collective-permute-done.24.refs_1_, bf16[16,256,256]{2,1,0:T(8,128)(2,1)S(1)} %get-tuple-element.44.refs_2_, ...), custom_call_target="tpu_custom_call" | custom-call | flops 1610612736 | bytes 4194304 | tf_op jit(solution)/shard_map/pallas_call | solution.py:461
  64.6 0.1 collective-permute-start.26
  64.7 0.6 collective-permute-start.27
  65.3 1.5 %shard_map.96 = (f32[264,128]{1,0:T(8,128)S(1)}, f32[264,128]{1,0:T(8,128)S(1)}, f32[264,128]{1,0:T(8,128)S(1)}, f32[264,128]{1,0:T(8,128)S(1)}) custom-call(f32[256,128]{1,0:T(8,128)S(1)} %collective-permute-done.15.refs_0_, f32[256,128]{1,0:T(8,128)S(1)} %collective-permute-done.16.refs_1_, bf16[16,256,256]{2,1,0:T(8,128)(2,1)S(1)} %get-tuple-element.44.refs_2_, ...), custom_call_target="tpu_custom_call" | custom-call | flops 1610612736 | bytes 4194304 | tf_op jit(solution)/shard_map/pallas_call | solution.py:461
  66.8 0.0 collective-permute-done.12
  66.8 1.3 %collective-permute-start.28 = (f32[264,128]{1,0:T(8,128)S(1)}, f32[264,128]{1,0:T(8,128)S(1)}, u32[]{:S(2)}, u32[]{:S(2)}) collective-permute-start(f32[264,128]{1,0:T(8,128)S(1)} %get-tuple-element.73), channel_id=1, source_target_pairs={{0,3},{1,2},{2,1},{3,0},{4,7},{5,6},{6,5},{7,4},{8,11},{9,10},{10,... | collective-permute-start | bytes 405512 | tf_op jit(solution)/shard_map/ppermute | solution.py:328
  68.1 0.4 collective-permute-start.18
  68.5 0.5 collective-permute-start.19
  69.0 1.0 %collective-permute-start.20 = (f32[264,128]{1,0:T(8,128)S(1)}, f32[264,128]{1,0:T(8,128)S(1)}, u32[]{:S(2)}, u32[]{:S(2)}) collective-permute-start(f32[264,128]{1,0:T(8,128)S(1)} %get-tuple-element.63), channel_id=1, source_target_pairs={{0,3},{1,2},{2,1},{3,0},{4,7},{5,6},{6,5},{7,4},{8,11},{9,10},{10,... | collective-permute-start | bytes 405512 | tf_op jit(solution)/shard_map/ppermute | solution.py:328
  70.0 1.5 %shard_map.91 = (f32[264,128]{1,0:T(8,128)S(1)}, f32[264,128]{1,0:T(8,128)S(1)}, f32[264,128]{1,0:T(8,128)S(1)}, f32[264,128]{1,0:T(8,128)S(1)}) custom-call(f32[256,128]{1,0:T(8,128)S(1)} %collective-permute-done.2.refs_0_, f32[256,128]{1,0:T(8,128)S(1)} %collective-permute-done.3.refs_1_, bf16[16,256,256]{2,1,0:T(8,128)(2,1)S(1)} %get-tuple-element.44.refs_2_, ...), custom_call_target="tpu_custom_call" | custom-call | flops 1610612736 | bytes 4194304 | tf_op jit(solution)/shard_map/pallas_call | solution.py:461
  71.5 0.0 collective-permute-done.27.refs_2_
  71.5 0.7 collective-permute-start.5
  72.2 0.8 collective-permute-done.28.refs_3_
  73.0 1.2 %collective-permute-start.6 = (f32[264,128]{1,0:T(8,128)S(1)}, f32[264,128]{1,0:T(8,128)S(1)}, u32[]{:S(2)}, u32[]{:S(2)}) collective-permute-start(f32[264,128]{1,0:T(8,128)S(1)} %get-tuple-element.52), channel_id=1, source_target_pairs={{0,2},{1,3},{2,0},{3,1},{4,6},{5,7},{6,4},{7,5},{8,10},{9,11},{10,... | collective-permute-start | bytes 405512 | tf_op jit(solution)/shard_map/ppermute | solution.py:328
  74.3 1.0 %collective-permute-start.7 = (f32[264,128]{1,0:T(8,128)S(1)}, f32[264,128]{1,0:T(8,128)S(1)}, u32[]{:S(2)}, u32[]{:S(2)}) collective-permute-start(f32[264,128]{1,0:T(8,128)S(1)} %get-tuple-element.53), channel_id=1, source_target_pairs={{0,3},{1,2},{2,1},{3,0},{4,7},{5,6},{6,5},{7,4},{8,11},{9,10},{10,... | collective-permute-start | bytes 405512 | tf_op jit(solution)/shard_map/ppermute | solution.py:328
  75.3 1.2 %shard_map.101 = (f32[12,4,64,128]{3,2,1,0:T(8,128)}, f32[12,2,2,128]{3,2,1,0:T(2,128)}) custom-call(f32[264,128]{1,0:T(8,128)S(1)} %get-tuple-element.70.refs_0_, f32[264,128]{1,0:T(8,128)S(1)} %collective-permute-done.26.refs_1_, f32[264,128]{1,0:T(8,128)S(1)} %collective-permute-done.27.refs_2_, f32[264,128]{1,0:T(8,128)S(1)} %collective-permute-done.28.refs_3_, ...), custom_call_target="tpu_custom_call" | custom-call | flops 100663296 | bytes 1048576 | tf_op jit(solution)/shard_map/pallas_call | solution.py:472
  76.5 0.5 collective-permute-done.19.refs_2_
  77.0 1.8 %collective-permute-done.20.refs_3_ = f32[264,128]{1,0:T(8,128)S(1)} collective-permute-done((f32[264,128]{1,0:T(8,128)S(1)}, f32[264,128]{1,0:T(8,128)S(1)}, u32[]{:S(2)}, u32[]{:S(2)}) %collective-permute-start.20) | collective-permute-done | bytes 135200 | tf_op jit(solution)/shard_map/ppermute | solution.py:328
  78.8 1.1 %shard_map.102 = (f32[12,4,64,128]{3,2,1,0:T(8,128)}, f32[12,2,2,128]{3,2,1,0:T(2,128)}) custom-call(f32[264,128]{1,0:T(8,128)S(1)} %get-tuple-element.60.refs_0_, f32[264,128]{1,0:T(8,128)S(1)} %collective-permute-done.18.refs_1_, f32[264,128]{1,0:T(8,128)S(1)} %collective-permute-done.19.refs_2_, ...), custom_call_target="tpu_custom_call", output_to_operand_aliasing={{0}: (7, {}), {1}: (8, {})} | custom-call | flops 100663296 | bytes 1048576 | tf_op jit(solution)/shard_map/pallas_call | solution.py:472
  80.0 2.8 %collective-permute-done.6.refs_2_ = f32[264,128]{1,0:T(8,128)S(1)} collective-permute-done((f32[264,128]{1,0:T(8,128)S(1)}, f32[264,128]{1,0:T(8,128)S(1)}, u32[]{:S(2)}, u32[]{:S(2)}) %collective-permute-start.6) | collective-permute-done | bytes 135200 | tf_op jit(solution)/shard_map/ppermute | solution.py:328
  82.8 1.8 %collective-permute-done.7.refs_3_ = f32[264,128]{1,0:T(8,128)S(1)} collective-permute-done((f32[264,128]{1,0:T(8,128)S(1)}, f32[264,128]{1,0:T(8,128)S(1)}, u32[]{:S(2)}, u32[]{:S(2)}) %collective-permute-start.7) | collective-permute-done | bytes 135200 | tf_op jit(solution)/shard_map/ppermute | solution.py:328
  84.6 1.1 %shard_map.103 = (f32[12,4,64,128]{3,2,1,0:T(8,128)}, f32[12,2,2,128]{3,2,1,0:T(2,128)}) custom-call(f32[264,128]{1,0:T(8,128)S(1)} %get-tuple-element.50.refs_0_, f32[264,128]{1,0:T(8,128)S(1)} %collective-permute-done.5.refs_1_, f32[264,128]{1,0:T(8,128)S(1)} %collective-permute-done.6.refs_2_, ...), custom_call_target="tpu_custom_call", output_to_operand_aliasing={{0}: (7, {}), {1}: (8, {})} | custom-call | flops 100663296 | bytes 1048576 | tf_op jit(solution)/shard_map/pallas_call | solution.py:472
  (33 shorter events, 0.1 us)
Async XLA Ops:
  0.6 1.4 %copy-start = (f32[12,4,64,128]{3,2,1,0:T(8,128)S(1)}, f32[12,4,64,128]{3,2,1,0:T(8,128)}, u32[]{:S(2)}) copy-start(f32[12,4,64,128]{3,2,1,0:T(8,128)} %state_ref.13) | copy-start | bytes 4718596
  2.2 28.2 %collective-permute-start.21 = (f32[4,2,64,128]{3,2,1,0:T(8,128)S(1)}, f32[4,2,64,128]{3,2,1,0:T(8,128)S(1)}, u32[]{:S(2)}, u32[]{:S(2)}) collective-permute-start(f32[4,2,64,128]{3,2,1,0:T(8,128)S(1)} %get-tuple-element.64), channel_id=1, source_target_pairs={{0,4},{4,0},{8,12},{12,8},{16,20},{20,16},{24,28},{28,24},{1,5},{5... | collective-permute-start | bytes 786440 | tf_op jit(solution)/shard_map/ppermute | solution.py:415
  5.3 28.7 %collective-permute-start.22 = (f32[4,2,64,128]{3,2,1,0:T(8,128)S(1)}, f32[4,2,64,128]{3,2,1,0:T(8,128)S(1)}, u32[]{:S(2)}, u32[]{:S(2)}) collective-permute-start(f32[4,2,64,128]{3,2,1,0:T(8,128)S(1)} %get-tuple-element.65), channel_id=1, source_target_pairs={{0,28},{4,8},{8,4},{12,16},{16,12},{20,24},{24,20},{28,0},{1,29},{... | collective-permute-start | bytes 786440 | tf_op jit(solution)/shard_map/ppermute | solution.py:416
  9.1 7.8 %copy-start.1 = (f32[12,4,64,128]{3,2,1,0:T(8,128)S(1)}, f32[12,4,64,128]{3,2,1,0:T(8,128)}, u32[]{:S(2)}) copy-start(f32[12,4,64,128]{3,2,1,0:T(8,128)} %state_ref.13) | copy-start | bytes 4718596
  9.1 36.0 %collective-permute-start.13 = (f32[4,2,64,128]{3,2,1,0:T(8,128)S(1)}, f32[4,2,64,128]{3,2,1,0:T(8,128)S(1)}, u32[]{:S(2)}, u32[]{:S(2)}) collective-permute-start(f32[4,2,64,128]{3,2,1,0:T(8,128)S(1)} %get-tuple-element.54), channel_id=1, source_target_pairs={{0,4},{4,0},{8,12},{12,8},{16,20},{20,16},{24,28},{28,24},{1,5},{5... | collective-permute-start | bytes 786440 | tf_op jit(solution)/shard_map/ppermute | solution.py:415
  9.1 24.9 %copy-start.3 = (bf16[2,256,512]{2,1,0:T(8,128)(2,1)S(1)}, bf16[2,256,512]{2,1,0:T(8,128)(2,1)}, u32[]{:S(2)}) copy-start(bf16[2,256,512]{2,1,0:T(8,128)(2,1)} %constant.11.clone.low_ref) | copy-start | bytes 1572868
  9.2 24.9 %copy-start.4 = (bf16[2,256,512]{2,1,0:T(8,128)(2,1)S(1)}, bf16[2,256,512]{2,1,0:T(8,128)(2,1)}, u32[]{:S(2)}) copy-start(bf16[2,256,512]{2,1,0:T(8,128)(2,1)} %constant.10.clone.high_ref) | copy-start | bytes 1572868
  9.2 37.5 %collective-permute-start.14 = (f32[4,2,64,128]{3,2,1,0:T(8,128)S(1)}, f32[4,2,64,128]{3,2,1,0:T(8,128)S(1)}, u32[]{:S(2)}, u32[]{:S(2)}) collective-permute-start(f32[4,2,64,128]{3,2,1,0:T(8,128)S(1)} %get-tuple-element.55), channel_id=1, source_target_pairs={{0,28},{4,8},{8,4},{12,16},{16,12},{20,24},{24,20},{28,0},{1,29},{... | collective-permute-start | bytes 786440 | tf_op jit(solution)/shard_map/ppermute | solution.py:416
  11.3 1.2 %collective-permute-start.8 = (f32[24,128]{1,0:T(8,128)S(1)}, f32[24,128]{1,0:T(8,128)S(1)}, u32[]{:S(2)}, u32[]{:S(2)}) collective-permute-start(f32[24,128]{1,0:T(8,128)S(1)} %shard_map.92), channel_id=1, source_target_pairs={{0,1},{1,0},{2,3},{3,2},{4,5},{5,4},{6,7},{7,6},{8,9},{9,8},{10,11... | collective-permute-start | bytes 36872 | tf_op jit(solution)/shard_map/ppermute | solution.py:346
  12.5 3.7 %collective-permute-start.9 = (f32[24,128]{1,0:T(8,128)S(1)}, f32[24,128]{1,0:T(8,128)S(1)}, u32[]{:S(2)}, u32[]{:S(2)}) collective-permute-start(f32[24,128]{1,0:T(8,128)S(1)} %add.15), channel_id=1, source_target_pairs={{0,2},{1,3},{2,0},{3,1},{4,6},{5,7},{6,4},{7,5},{8,10},{9,11},{10,... | collective-permute-start | bytes 36872 | tf_op jit(solution)/shard_map/ppermute | solution.py:346
  16.2 12.5 %collective-permute-start.10 = (f32[24,128]{1,0:T(8,128)S(1)}, f32[24,128]{1,0:T(8,128)S(1)}, u32[]{:S(2)}, u32[]{:S(2)}) collective-permute-start(f32[24,128]{1,0:T(8,128)S(1)} %add.16), channel_id=1, source_target_pairs={{0,4},{4,0},{8,12},{12,8},{16,20},{20,16},{24,28},{28,24},{1,5},{5... | collective-permute-start | bytes 36872 | tf_op jit(solution)/shard_map/ppermute | solution.py:346
  28.7 20.2 %collective-permute-start = (f32[4,2,64,128]{3,2,1,0:T(8,128)S(1)}, f32[4,2,64,128]{3,2,1,0:T(8,128)S(1)}, u32[]{:S(2)}, u32[]{:S(2)}) collective-permute-start(f32[4,2,64,128]{3,2,1,0:T(8,128)S(1)} %get-tuple-element.40), channel_id=1, source_target_pairs={{0,4},{4,0},{8,12},{12,8},{16,20},{20,16},{24,28},{28,24},{1,5},{5... | collective-permute-start | bytes 786440 | tf_op jit(solution)/shard_map/ppermute | solution.py:415
  30.4 18.5 %collective-permute-start.1 = (f32[4,2,64,128]{3,2,1,0:T(8,128)S(1)}, f32[4,2,64,128]{3,2,1,0:T(8,128)S(1)}, u32[]{:S(2)}, u32[]{:S(2)}) collective-permute-start(f32[4,2,64,128]{3,2,1,0:T(8,128)S(1)} %get-tuple-element.41), channel_id=1, source_target_pairs={{0,28},{4,8},{8,4},{12,16},{16,12},{20,24},{24,20},{28,0},{1,29},{... | collective-permute-start | bytes 786440 | tf_op jit(solution)/shard_map/ppermute | solution.py:416
  34.0 4.7 %collective-permute-start.11 = (f32[24,128]{1,0:T(8,128)S(1)}, f32[24,128]{1,0:T(8,128)S(1)}, u32[]{:S(2)}, u32[]{:S(2)}) collective-permute-start(f32[24,128]{1,0:T(8,128)S(1)} %add.17), channel_id=1, source_target_pairs={{0,8},{4,12},{8,0},{12,4},{16,24},{20,28},{24,16},{28,20},{1,9},{5... | collective-permute-start | bytes 36872 | tf_op jit(solution)/shard_map/ppermute | solution.py:346
  38.7 11.5 %collective-permute-start.25 = (f32[256,128]{1,0:T(8,128)S(1)}, f32[256,128]{1,0:T(8,128)S(1)}, u32[]{:S(2)}, u32[]{:S(2)}) collective-permute-start(f32[256,128]{1,0:T(8,128)S(1)} %get-tuple-element.69), channel_id=1, source_target_pairs={{0,1},{1,0},{2,3},{3,2},{4,5},{5,4},{6,7},{7,6},{8,9},{9,8},{10,11... | collective-permute-start | bytes 393224 | tf_op jit(solution)/shard_map/ppermute | solution.py:328
  38.7 3.4 %copy-start.2 = (f32[32,256,256]{2,1,0:T(8,128)S(1)}, f32[32,256,256]{2,1,0:T(8,128)}, u32[]{:S(2)}) copy-start(f32[32,256,256]{2,1,0:T(8,128)} %inverse_ref.3) | copy-start | bytes 25165828
  45.1 21.7 %collective-permute-start.12 = (f32[24,128]{1,0:T(8,128)S(1)}, f32[24,128]{1,0:T(8,128)S(1)}, u32[]{:S(2)}, u32[]{:S(2)}) collective-permute-start(f32[24,128]{1,0:T(8,128)S(1)} %add.18), channel_id=1, source_target_pairs={{0,16},{4,20},{8,24},{12,28},{16,0},{20,4},{24,8},{28,12},{1,17},{... | collective-permute-start | bytes 36872 | tf_op jit(solution)/shard_map/ppermute | solution.py:346
  47.3 17.3 %collective-permute-start.15 = (f32[256,128]{1,0:T(8,128)S(1)}, f32[256,128]{1,0:T(8,128)S(1)}, u32[]{:S(2)}, u32[]{:S(2)}) collective-permute-start(f32[256,128]{1,0:T(8,128)S(1)} %get-tuple-element.56), channel_id=1, source_target_pairs={{0,2},{1,3},{2,0},{3,1},{4,6},{5,7},{6,4},{7,5},{8,10},{9,11},{10,... | collective-permute-start | bytes 393224 | tf_op jit(solution)/shard_map/ppermute | solution.py:328
  48.9 15.8 %collective-permute-start.16 = (f32[256,128]{1,0:T(8,128)S(1)}, f32[256,128]{1,0:T(8,128)S(1)}, u32[]{:S(2)}, u32[]{:S(2)}) collective-permute-start(f32[256,128]{1,0:T(8,128)S(1)} %get-tuple-element.57), channel_id=1, source_target_pairs={{0,3},{1,2},{2,1},{3,0},{4,7},{5,6},{6,5},{7,4},{8,11},{9,10},{10,... | collective-permute-start | bytes 393224 | tf_op jit(solution)/shard_map/ppermute | solution.py:328
  49.0 2.7 %collective-permute-start.17 = (f32[256,128]{1,0:T(8,128)S(1)}, f32[256,128]{1,0:T(8,128)S(1)}, u32[]{:S(2)}, u32[]{:S(2)}) collective-permute-start(f32[256,128]{1,0:T(8,128)S(1)} %get-tuple-element.59), channel_id=1, source_target_pairs={{0,1},{1,0},{2,3},{3,2},{4,5},{5,4},{6,7},{7,6},{8,9},{9,8},{10,11... | collective-permute-start | bytes 393224 | tf_op jit(solution)/shard_map/ppermute | solution.py:328
  50.2 4.3 %collective-permute-start.4 = (f32[256,128]{1,0:T(8,128)S(1)}, f32[256,128]{1,0:T(8,128)S(1)}, u32[]{:S(2)}, u32[]{:S(2)}) collective-permute-start(f32[256,128]{1,0:T(8,128)S(1)} %get-tuple-element.49), channel_id=1, source_target_pairs={{0,1},{1,0},{2,3},{3,2},{4,5},{5,4},{6,7},{7,6},{8,9},{9,8},{10,11... | collective-permute-start | bytes 393224 | tf_op jit(solution)/shard_map/ppermute | solution.py:328
  51.6 7.7 %collective-permute-start.23 = (f32[256,128]{1,0:T(8,128)S(1)}, f32[256,128]{1,0:T(8,128)S(1)}, u32[]{:S(2)}, u32[]{:S(2)}) collective-permute-start(f32[256,128]{1,0:T(8,128)S(1)} %get-tuple-element.66), channel_id=1, source_target_pairs={{0,2},{1,3},{2,0},{3,1},{4,6},{5,7},{6,4},{7,5},{8,10},{9,11},{10,... | collective-permute-start | bytes 393224 | tf_op jit(solution)/shard_map/ppermute | solution.py:328
  54.5 6.7 %collective-permute-start.24 = (f32[256,128]{1,0:T(8,128)S(1)}, f32[256,128]{1,0:T(8,128)S(1)}, u32[]{:S(2)}, u32[]{:S(2)}) collective-permute-start(f32[256,128]{1,0:T(8,128)S(1)} %get-tuple-element.67), channel_id=1, source_target_pairs={{0,3},{1,2},{2,1},{3,0},{4,7},{5,6},{6,5},{7,4},{8,11},{9,10},{10,... | collective-permute-start | bytes 393224 | tf_op jit(solution)/shard_map/ppermute | solution.py:328
  54.8 8.3 %copy-start.7 = (f32[8,256]{1,0:T(8,128)S(1)}, f32[8,256]{1,0:T(8,128)}, u32[]{:S(2)}) copy-start(f32[8,256]{1,0:T(8,128)} %constant.14.clone.refs_7_) | copy-start | bytes 24580
  59.4 8.8 %collective-permute-start.2 = (f32[256,128]{1,0:T(8,128)S(1)}, f32[256,128]{1,0:T(8,128)S(1)}, u32[]{:S(2)}, u32[]{:S(2)}) collective-permute-start(f32[256,128]{1,0:T(8,128)S(1)} %get-tuple-element.42), channel_id=1, source_target_pairs={{0,2},{1,3},{2,0},{3,1},{4,6},{5,7},{6,4},{7,5},{8,10},{9,11},{10,... | collective-permute-start | bytes 393224 | tf_op jit(solution)/shard_map/ppermute | solution.py:328
  61.2 7.3 %collective-permute-start.3 = (f32[256,128]{1,0:T(8,128)S(1)}, f32[256,128]{1,0:T(8,128)S(1)}, u32[]{:S(2)}, u32[]{:S(2)}) collective-permute-start(f32[256,128]{1,0:T(8,128)S(1)} %get-tuple-element.43), channel_id=1, source_target_pairs={{0,3},{1,2},{2,1},{3,0},{4,7},{5,6},{6,5},{7,4},{8,11},{9,10},{10,... | collective-permute-start | bytes 393224 | tf_op jit(solution)/shard_map/ppermute | solution.py:328
  64.6 4.4 %collective-permute-start.26 = (f32[264,128]{1,0:T(8,128)S(1)}, f32[264,128]{1,0:T(8,128)S(1)}, u32[]{:S(2)}, u32[]{:S(2)}) collective-permute-start(f32[264,128]{1,0:T(8,128)S(1)} %get-tuple-element.71), channel_id=1, source_target_pairs={{0,1},{1,0},{2,3},{3,2},{4,5},{5,4},{6,7},{7,6},{8,9},{9,8},{10,11... | collective-permute-start | bytes 405512 | tf_op jit(solution)/shard_map/ppermute | solution.py:328
  64.7 6.8 %collective-permute-start.27 = (f32[264,128]{1,0:T(8,128)S(1)}, f32[264,128]{1,0:T(8,128)S(1)}, u32[]{:S(2)}, u32[]{:S(2)}) collective-permute-start(f32[264,128]{1,0:T(8,128)S(1)} %get-tuple-element.72), channel_id=1, source_target_pairs={{0,2},{1,3},{2,0},{3,1},{4,6},{5,7},{6,4},{7,5},{8,10},{9,11},{10,... | collective-permute-start | bytes 405512 | tf_op jit(solution)/shard_map/ppermute | solution.py:328
  66.8 6.2 %collective-permute-start.28 = (f32[264,128]{1,0:T(8,128)S(1)}, f32[264,128]{1,0:T(8,128)S(1)}, u32[]{:S(2)}, u32[]{:S(2)}) collective-permute-start(f32[264,128]{1,0:T(8,128)S(1)} %get-tuple-element.73), channel_id=1, source_target_pairs={{0,3},{1,2},{2,1},{3,0},{4,7},{5,6},{6,5},{7,4},{8,11},{9,10},{10,... | collective-permute-start | bytes 405512 | tf_op jit(solution)/shard_map/ppermute | solution.py:328
  68.1 6.1 %collective-permute-start.18 = (f32[264,128]{1,0:T(8,128)S(1)}, f32[264,128]{1,0:T(8,128)S(1)}, u32[]{:S(2)}, u32[]{:S(2)}) collective-permute-start(f32[264,128]{1,0:T(8,128)S(1)} %get-tuple-element.61), channel_id=1, source_target_pairs={{0,1},{1,0},{2,3},{3,2},{4,5},{5,4},{6,7},{7,6},{8,9},{9,8},{10,11... | collective-permute-start | bytes 405512 | tf_op jit(solution)/shard_map/ppermute | solution.py:328
  68.5 8.5 %collective-permute-start.19 = (f32[264,128]{1,0:T(8,128)S(1)}, f32[264,128]{1,0:T(8,128)S(1)}, u32[]{:S(2)}, u32[]{:S(2)}) collective-permute-start(f32[264,128]{1,0:T(8,128)S(1)} %get-tuple-element.62), channel_id=1, source_target_pairs={{0,2},{1,3},{2,0},{3,1},{4,6},{5,7},{6,4},{7,5},{8,10},{9,11},{10,... | collective-permute-start | bytes 405512 | tf_op jit(solution)/shard_map/ppermute | solution.py:328
  69.0 6.3 %copy-start.5 = (bf16[128,128]{1,0:T(8,128)(2,1)S(1)}, bf16[128,128]{1,0:T(8,128)(2,1)}, u32[]{:S(2)}) copy-start(bf16[128,128]{1,0:T(8,128)(2,1)} %constant.13.clone.refs_5_) | copy-start | bytes 98308
  69.0 6.3 %copy-start.6 = (bf16[128,128]{1,0:T(8,128)(2,1)S(1)}, bf16[128,128]{1,0:T(8,128)(2,1)}, u32[]{:S(2)}) copy-start(bf16[128,128]{1,0:T(8,128)(2,1)} %constant.12.clone.refs_4_) | copy-start | bytes 98308
  69.0 9.8 %collective-permute-start.20 = (f32[264,128]{1,0:T(8,128)S(1)}, f32[264,128]{1,0:T(8,128)S(1)}, u32[]{:S(2)}, u32[]{:S(2)}) collective-permute-start(f32[264,128]{1,0:T(8,128)S(1)} %get-tuple-element.63), channel_id=1, source_target_pairs={{0,3},{1,2},{2,1},{3,0},{4,7},{5,6},{6,5},{7,4},{8,11},{9,10},{10,... | collective-permute-start | bytes 405512 | tf_op jit(solution)/shard_map/ppermute | solution.py:328
  71.5 8.5 %collective-permute-start.5 = (f32[264,128]{1,0:T(8,128)S(1)}, f32[264,128]{1,0:T(8,128)S(1)}, u32[]{:S(2)}, u32[]{:S(2)}) collective-permute-start(f32[264,128]{1,0:T(8,128)S(1)} %get-tuple-element.51), channel_id=1, source_target_pairs={{0,1},{1,0},{2,3},{3,2},{4,5},{5,4},{6,7},{7,6},{8,9},{9,8},{10,11... | collective-permute-start | bytes 405512 | tf_op jit(solution)/shard_map/ppermute | solution.py:328
  73.0 9.8 %collective-permute-start.6 = (f32[264,128]{1,0:T(8,128)S(1)}, f32[264,128]{1,0:T(8,128)S(1)}, u32[]{:S(2)}, u32[]{:S(2)}) collective-permute-start(f32[264,128]{1,0:T(8,128)S(1)} %get-tuple-element.52), channel_id=1, source_target_pairs={{0,2},{1,3},{2,0},{3,1},{4,6},{5,7},{6,4},{7,5},{8,10},{9,11},{10,... | collective-permute-start | bytes 405512 | tf_op jit(solution)/shard_map/ppermute | solution.py:328
  74.3 10.4 %collective-permute-start.7 = (f32[264,128]{1,0:T(8,128)S(1)}, f32[264,128]{1,0:T(8,128)S(1)}, u32[]{:S(2)}, u32[]{:S(2)}) collective-permute-start(f32[264,128]{1,0:T(8,128)S(1)} %get-tuple-element.53), channel_id=1, source_target_pairs={{0,3},{1,2},{2,1},{3,0},{4,7},{5,6},{6,5},{7,4},{8,11},{9,10},{10,... | collective-permute-start | bytes 405512 | tf_op jit(solution)/shard_map/ppermute | solution.py:328

commit v7 on v6

--- a/solution.py
+++ b/solution.py
@@ -152,7 +152,34 @@
             high_ref[at], low_ref[at] = split(x)
 
 
-def project_kernel(base, state_ref, near_ref, far_ref, high_ref, low_ref, *out_refs):
+def table_rows(ref, p, where, count, slots, columns):
+    return jnp.concatenate(
+        [ref[p, pl.ds(f * count + at, slots), columns] for f in range(2) for at in where], axis=0
+    )
+
+
+def own_kernel(base, parts, state_ref, high_ref, low_ref, out_ref):
+    coef = state_ref.shape[2]
+    members = out_ref.shape[2] // coef
+    count = high_ref.shape[1] // 2
+    slots = count // parts
+    where = [pl.multiple_of(peer * slots, slots) for peer in peers(parts)]
+    columns = slice(0, 2 * LANES)
+    for p in range(2):
+        x = jnp.concatenate(
+            [
+                state_ref[base : base + members, p].reshape(members * coef, LANES),
+                state_ref[base : base + members, p + 2].reshape(members * coef, LANES),
+            ],
+            axis=1,
+        )
+        x_high, x_low = split(x)
+        w_high = table_rows(high_ref, p, where, count, slots, columns)
+        w_low = table_rows(low_ref, p, where, count, slots, columns)
+        out_ref[p] = dot(w_high, x_high, NT) + (dot(w_high, x_low, NT) + dot(w_low, x_high, NT))
+
+
+def project_kernel(own_ref, near_ref, far_ref, high_ref, low_ref, *out_refs):
     parts = len(out_refs)
     members, _, coef, _ = near_ref.shape
     rows = 2 * members
@@ -168,22 +195,16 @@
         far = far_ref[:, p].reshape(members * coef, LANES)
         x = jnp.concatenate(
             [
-                state_ref[base : base + members, p].reshape(members * coef, LANES),
-                state_ref[base : base + members, p + 2].reshape(members * coef, LANES),
                 jnp.where(even, far, near),
                 jnp.where(even, near, far),
             ],
             axis=1,
         )
         x_high, x_low = split(x)
-        w_high, w_low = [
-            jnp.concatenate(
-                [ref[p, pl.ds(f * count + at, slots), :] for f in range(2) for at in where], axis=0
-            )
-            for ref in (high_ref, low_ref)
-        ]
+        w_high = table_rows(high_ref, p, where, count, slots, slice(2 * LANES, 4 * LANES))
+        w_low = table_rows(low_ref, p, where, count, slots, slice(2 * LANES, 4 * LANES))
         t = dot(w_high, x_high, NT) + (dot(w_high, x_low, NT) + dot(w_low, x_high, NT))
-        t = jnp.where(interior, t, 0.0)
+        t = jnp.where(interior, t + own_ref[p], 0.0)
         for d in range(parts):
             for f in range(2):
                 first = f * count + d * slots
@@ -438,15 +459,24 @@
     outputs = []
     for g, (first, count) in enumerate(plan):
         rows = count * fields // 2
+        own = call(
+            functools.partial(own_kernel, first, parts),
+            8,
+            3 * 2 * 2 * (2 * MODES) * (2 * LANES) * count * coef,
+            2 * count * member_bytes,
+            in_specs=[VMEM] * 3,
+            out_specs=VMEM,
+            out_shape=array(2, 2 * MODES, count * coef),
+        )(state, step_high, step_low)
         sent = call(
-            functools.partial(project_kernel, first),
+            project_kernel,
             8,
             3 * 2 * 2 * (2 * MODES) * (4 * LANES) * count * coef,
             3 * count * member_bytes,
             in_specs=[VMEM] * 5,
             out_specs=[VMEM] * parts,
             out_shape=[array(mine * rows, LANES)] * parts,
-        )(state, *halos[g], step_high, step_low)
+        )(own, *halos[g], step_high, step_low)
         got = exchanged(sent, "gy")
         flops = 3 * mine * coef_count**2 * 256
         begun = call(

time: 86 us -> 83.9 us (0.976)
  local copies, waits for them, and re-layouts: 4.82 us -> 1.43 us
    unnamed x16, local copies, waits for them, and re-layouts: 4.82 us -> 1.43 us
    pallas_call x3 -> x6, Pallas kernels: 1.93 us -> 2.59 us  [the longest x3 1.4 us: per_device(): call(project_kernel, 8, 3 * 2 * 2 * (2 * MODES) * (4 * LANES) * count * c...]
  transfers between devices with their start and end apart: 29 -> 29, of which waited for: 11 -> 11; matrix products, arithmetic and copies ran while one was open for 0% -> 0% of each run, Pallas kernels for 19% -> 20%
where the time goes in v7:
time: 83.9 us; the launch traced here: 83 us
  starting transfers between devices  31.3 us (37%)
  waiting for transfers between devices  31 us (37%)
  Pallas kernels  18.3 us (22%)
  local copies, waits for them, and re-layouts  1.43 us (2%)
  between operations  0.92 us (1%)
    ppermute x5, waiting for transfers between devices, full_sum(): other = lax.ppermute(x, axis, [(i, i ^ hop) for i in range(n)])  19.5 us
    ppermute x18, starting transfers between devices, exchanged(): got[d] = lax.ppermute(pieces[d], axis, [(i, i ^ d) for i in range(n)])  14.4 us
    ppermute x18, waiting for transfers between devices, exchanged(): got[d] = lax.ppermute(pieces[d], axis, [(i, i ^ d) for i in range(n)])  11.5 us
    ppermute x3, starting transfers between devices, per_device(): far = lax.ppermute(far, 'gx', far_pairs)  8.63 us
    ppermute x3, starting transfers between devices, per_device(): near = lax.ppermute(near, 'gx', near_pairs)  4.86 us
    pallas_call x3, Pallas kernels, per_device(): call(functools.partial(solve_kernel, parts, rows), 6, flops, 2 * mine * c...  4.49 us
    pallas_call x3, Pallas kernels, per_device(): call(functools.partial(begin_kernel, rows), 6, flops, 2 * mine * coef_cou...  4.04 us
    pallas_call x3, Pallas kernels, per_device(): call(functools.partial(back_kernel, float(fields * coef_count * grid_x),...  3.45 us
  transfers between devices with their start and end apart: 29, of which 11 were waited for; matrix products, arithmetic and copies ran while one was open for 0% of the time, Pallas kernels for 20%

profile of v7, /device:TPU:0, one launch (start us, length us, event | category | flops | bytes accessed | tf_op | source)
XLA Modules:
  0.0 83.0 jit_solution(6792431003627599106)
XLA Ops:
  0.6 0.0 copy-start
  0.6 1.4 %copy-done = f32[12,4,64,128]{3,2,1,0:T(8,128)S(1)} copy-done((f32[12,4,64,128]{3,2,1,0:T(8,128)S(1)}, f32[12,4,64,128]{3,2,1,0:T(8,128)}, u32[]{:S(2)}) %copy-start) | copy-done | bytes 1572888
  2.0 0.2 shard_map.100
  2.2 3.0 %collective-permute-start.21 = (f32[4,2,64,128]{3,2,1,0:T(8,128)S(1)}, f32[4,2,64,128]{3,2,1,0:T(8,128)S(1)}, u32[]{:S(2)}, u32[]{:S(2)}) collective-permute-start(f32[4,2,64,128]{3,2,1,0:T(8,128)S(1)} %get-tuple-element.64), channel_id=1, source_target_pairs={{0,4},{4,0},{8,12},{12,8},{16,20},{20,16},{24,28},{28,24},{1,5},{5... | collective-permute-start | bytes 786440 | tf_op jit(solution)/shard_map/ppermute | solution.py:436
  5.3 0.2 shard_map.95
  5.5 0.0 copy-start.1
  5.5 0.1 collective-permute-start.13
  5.6 5.0 %collective-permute-start.22 = (f32[4,2,64,128]{3,2,1,0:T(8,128)S(1)}, f32[4,2,64,128]{3,2,1,0:T(8,128)S(1)}, u32[]{:S(2)}, u32[]{:S(2)}) collective-permute-start(f32[4,2,64,128]{3,2,1,0:T(8,128)S(1)} %get-tuple-element.65), channel_id=1, source_target_pairs={{0,28},{4,8},{8,4},{12,16},{16,12},{20,24},{24,20},{28,0},{1,29},{... | collective-permute-start | bytes 786440 | tf_op jit(solution)/shard_map/ppermute | solution.py:437
  10.6 0.0 collective-permute-start.14
  10.7 0.2 shard_map.93
  10.9 0.1 collective-permute-start.8
  11.0 1.2 %collective-permute-done.8 = f32[24,128]{1,0:T(8,128)S(1)} collective-permute-done((f32[24,128]{1,0:T(8,128)S(1)}, f32[24,128]{1,0:T(8,128)S(1)}, u32[]{:S(2)}, u32[]{:S(2)}) %collective-permute-start.8) | collective-permute-done | bytes 12320 | tf_op jit(solution)/shard_map/ppermute | solution.py:367
  12.1 1.7 %collective-permute-start.9 = (f32[24,128]{1,0:T(8,128)S(1)}, f32[24,128]{1,0:T(8,128)S(1)}, u32[]{:S(2)}, u32[]{:S(2)}) collective-permute-start(f32[24,128]{1,0:T(8,128)S(1)} %add.15), channel_id=1, source_target_pairs={{0,2},{1,3},{2,0},{3,1},{4,6},{5,7},{6,4},{7,5},{8,10},{9,11},{10,... | collective-permute-start | bytes 36872 | tf_op jit(solution)/shard_map/ppermute | solution.py:367
  13.8 2.0 %collective-permute-done.9 = f32[24,128]{1,0:T(8,128)S(1)} collective-permute-done((f32[24,128]{1,0:T(8,128)S(1)}, f32[24,128]{1,0:T(8,128)S(1)}, u32[]{:S(2)}, u32[]{:S(2)}) %collective-permute-start.9) | collective-permute-done | bytes 12320 | tf_op jit(solution)/shard_map/ppermute | solution.py:367
  15.9 0.2 shard_map.87
  16.1 12.6 %collective-permute-done.10 = f32[24,128]{1,0:T(8,128)S(1)} collective-permute-done((f32[24,128]{1,0:T(8,128)S(1)}, f32[24,128]{1,0:T(8,128)S(1)}, u32[]{:S(2)}, u32[]{:S(2)}) %collective-permute-start.10) | collective-permute-done | bytes 12320 | tf_op jit(solution)/shard_map/ppermute | solution.py:367
  28.7 1.7 %collective-permute-start = (f32[4,2,64,128]{3,2,1,0:T(8,128)S(1)}, f32[4,2,64,128]{3,2,1,0:T(8,128)S(1)}, u32[]{:S(2)}, u32[]{:S(2)}) collective-permute-start(f32[4,2,64,128]{3,2,1,0:T(8,128)S(1)} %get-tuple-element.40), channel_id=1, source_target_pairs={{0,4},{4,0},{8,12},{12,8},{16,20},{20,16},{24,28},{28,24},{1,5},{5... | collective-permute-start | bytes 786440 | tf_op jit(solution)/shard_map/ppermute | solution.py:436
  30.4 3.6 %collective-permute-start.1 = (f32[4,2,64,128]{3,2,1,0:T(8,128)S(1)}, f32[4,2,64,128]{3,2,1,0:T(8,128)S(1)}, u32[]{:S(2)}, u32[]{:S(2)}) collective-permute-start(f32[4,2,64,128]{3,2,1,0:T(8,128)S(1)} %get-tuple-element.41), channel_id=1, source_target_pairs={{0,28},{4,8},{8,4},{12,16},{16,12},{20,24},{24,20},{28,0},{1,29},{... | collective-permute-start | bytes 786440 | tf_op jit(solution)/shard_map/ppermute | solution.py:437
  34.0 0.4 shard_map.99.own_ref
  34.4 0.1 collective-permute-start.11
  34.5 0.5 shard_map.101
  35.0 3.7 %collective-permute-done.11 = f32[24,128]{1,0:T(8,128)S(1)} collective-permute-done((f32[24,128]{1,0:T(8,128)S(1)}, f32[24,128]{1,0:T(8,128)S(1)}, u32[]{:S(2)}, u32[]{:S(2)}) %collective-permute-start.11) | collective-permute-done | bytes 12320 | tf_op jit(solution)/shard_map/ppermute | solution.py:367
  38.7 1.5 %shard_map.90 = (bf16[16,256,256]{2,1,0:T(8,128)(2,1)S(1)}, bf16[16,256,256]{2,1,0:T(8,128)(2,1)S(1)}) custom-call(f32[32,256,256]{2,1,0:T(8,128)S(1)} %copy-done.2), custom_call_target="tpu_custom_call" | custom-call | flops 10000000 | bytes 8388608 | tf_op jit(solution)/shard_map/pallas_call | solution.py:446
  40.2 1.5 %shard_map.89 = (bf16[16,256,256]{2,1,0:T(8,128)(2,1)S(1)}, bf16[16,256,256]{2,1,0:T(8,128)(2,1)S(1)}) custom-call(f32[32,256,256]{2,1,0:T(8,128)S(1)} %copy-done.2), custom_call_target="tpu_custom_call" | custom-call | flops 10000000 | bytes 8388608 | tf_op jit(solution)/shard_map/pallas_call | solution.py:446
  41.7 0.4 shard_map.94.own_ref
  42.1 0.4 shard_map.86.own_ref
  42.5 1.6 %collective-permute-start.12 = (f32[24,128]{1,0:T(8,128)S(1)}, f32[24,128]{1,0:T(8,128)S(1)}, u32[]{:S(2)}, u32[]{:S(2)}) collective-permute-start(f32[24,128]{1,0:T(8,128)S(1)} %add.18), channel_id=1, source_target_pairs={{0,16},{4,20},{8,24},{12,28},{16,0},{20,4},{24,8},{28,12},{1,17},{... | collective-permute-start | bytes 36872 | tf_op jit(solution)/shard_map/ppermute | solution.py:367
  44.1 0.5 shard_map.96
  44.6 1.6 %collective-permute-start.15 = (f32[256,128]{1,0:T(8,128)S(1)}, f32[256,128]{1,0:T(8,128)S(1)}, u32[]{:S(2)}, u32[]{:S(2)}) collective-permute-start(f32[256,128]{1,0:T(8,128)S(1)} %get-tuple-element.56), channel_id=1, source_target_pairs={{0,2},{1,3},{2,0},{3,1},{4,6},{5,7},{6,4},{7,5},{8,10},{9,11},{10,... | collective-permute-start | bytes 393224 | tf_op jit(solution)/shard_map/ppermute | solution.py:349
  46.1 0.1 collective-permute-start.16
  46.2 0.6 collective-permute-start.17
  46.8 0.5 shard_map.88
  47.3 0.1 collective-permute-start.4
  47.3 1.3 %shard_map.102.refs_6_ = f32[512,256]{1,0:T(8,128)S(1)} custom-call(f32[256,128]{1,0:T(8,128)S(1)} %get-tuple-element.68.refs_0_, f32[256,128]{1,0:T(8,128)S(1)} %collective-permute-done.25.refs_1_, bf16[16,256,256]{2,1,0:T(8,128)(2,1)S(1)} %get-tuple-element.44.refs_2_, bf16[16,256,256]{2,1,0:T(8,128)(2,1)S(1)} %get-tuple-element.45.refs_3_, ...), custom_call_target="tpu_custom_call" | custom-call | flops 1610612736 | bytes 4194304 | tf_op jit(solution)/shard_map/pallas_call | solution.py:482
  48.7 1.5 %collective-permute-start.23 = (f32[256,128]{1,0:T(8,128)S(1)}, f32[256,128]{1,0:T(8,128)S(1)}, u32[]{:S(2)}, u32[]{:S(2)}) collective-permute-start(f32[256,128]{1,0:T(8,128)S(1)} %get-tuple-element.66), channel_id=1, source_target_pairs={{0,2},{1,3},{2,0},{3,1},{4,6},{5,7},{6,4},{7,5},{8,10},{9,11},{10,... | collective-permute-start | bytes 393224 | tf_op jit(solution)/shard_map/ppermute | solution.py:349
  50.2 1.4 %shard_map.97.refs_6_ = f32[512,256]{1,0:T(8,128)S(1)} custom-call(f32[256,128]{1,0:T(8,128)S(1)} %get-tuple-element.58.refs_0_, f32[256,128]{1,0:T(8,128)S(1)} %collective-permute-done.17.refs_1_, bf16[16,256,256]{2,1,0:T(8,128)(2,1)S(1)} %get-tuple-element.44.refs_2_, bf16[16,256,256]{2,1,0:T(8,128)(2,1)S(1)} %get-tuple-element.45.refs_3_, ...), custom_call_target="tpu_custom_call" | custom-call | flops 1610612736 | bytes 4194304 | tf_op jit(solution)/shard_map/pallas_call | solution.py:482
  51.6 0.3 collective-permute-start.24
  51.9 1.3 %shard_map.91.refs_6_ = f32[512,256]{1,0:T(8,128)S(1)} custom-call(f32[256,128]{1,0:T(8,128)S(1)} %get-tuple-element.48.refs_0_, f32[256,128]{1,0:T(8,128)S(1)} %collective-permute-done.4.refs_1_, bf16[16,256,256]{2,1,0:T(8,128)(2,1)S(1)} %get-tuple-element.44.refs_2_, bf16[16,256,256]{2,1,0:T(8,128)(2,1)S(1)} %get-tuple-element.45.refs_3_, ...), custom_call_target="tpu_custom_call" | custom-call | flops 1610612736 | bytes 4194304 | tf_op jit(solution)/shard_map/pallas_call | solution.py:482
  53.3 3.3 %collective-permute-done.23.refs_0_ = f32[256,128]{1,0:T(8,128)S(1)} collective-permute-done((f32[256,128]{1,0:T(8,128)S(1)}, f32[256,128]{1,0:T(8,128)S(1)}, u32[]{:S(2)}, u32[]{:S(2)}) %collective-permute-start.23) | collective-permute-done | bytes 131104 | tf_op jit(solution)/shard_map/ppermute | solution.py:349
  56.6 1.5 %collective-permute-start.2 = (f32[256,128]{1,0:T(8,128)S(1)}, f32[256,128]{1,0:T(8,128)S(1)}, u32[]{:S(2)}, u32[]{:S(2)}) collective-permute-start(f32[256,128]{1,0:T(8,128)S(1)} %get-tuple-element.42), channel_id=1, source_target_pairs={{0,2},{1,3},{2,0},{3,1},{4,6},{5,7},{6,4},{7,5},{8,10},{9,11},{10,... | collective-permute-start | bytes 393224 | tf_op jit(solution)/shard_map/ppermute | solution.py:349
  58.1 0.3 collective-permute-done.24.refs_1_
  58.5 1.9 %collective-permute-start.3 = (f32[256,128]{1,0:T(8,128)S(1)}, f32[256,128]{1,0:T(8,128)S(1)}, u32[]{:S(2)}, u32[]{:S(2)}) collective-permute-start(f32[256,128]{1,0:T(8,128)S(1)} %get-tuple-element.43), channel_id=1, source_target_pairs={{0,3},{1,2},{2,1},{3,0},{4,7},{5,6},{6,5},{7,4},{8,11},{9,10},{10,... | collective-permute-start | bytes 393224 | tf_op jit(solution)/shard_map/ppermute | solution.py:349
  60.4 1.5 %shard_map.103 = (f32[264,128]{1,0:T(8,128)S(1)}, f32[264,128]{1,0:T(8,128)S(1)}, f32[264,128]{1,0:T(8,128)S(1)}, f32[264,128]{1,0:T(8,128)S(1)}) custom-call(f32[256,128]{1,0:T(8,128)S(1)} %collective-permute-done.23.refs_0_, f32[256,128]{1,0:T(8,128)S(1)} %collective-permute-done.24.refs_1_, bf16[16,256,256]{2,1,0:T(8,128)(2,1)S(1)} %get-tuple-element.44.refs_2_, ...), custom_call_target="tpu_custom_call" | custom-call | flops 1610612736 | bytes 4194304 | tf_op jit(solution)/shard_map/pallas_call | solution.py:491
  61.9 0.0 collective-permute-done.15.refs_0_
  61.9 0.1 collective-permute-start.26
  62.0 0.6 collective-permute-start.27
  62.5 1.5 %shard_map.98 = (f32[264,128]{1,0:T(8,128)S(1)}, f32[264,128]{1,0:T(8,128)S(1)}, f32[264,128]{1,0:T(8,128)S(1)}, f32[264,128]{1,0:T(8,128)S(1)}) custom-call(f32[256,128]{1,0:T(8,128)S(1)} %collective-permute-done.15.refs_0_, f32[256,128]{1,0:T(8,128)S(1)} %collective-permute-done.16.refs_1_, bf16[16,256,256]{2,1,0:T(8,128)(2,1)S(1)} %get-tuple-element.44.refs_2_, ...), custom_call_target="tpu_custom_call" | custom-call | flops 1610612736 | bytes 4194304 | tf_op jit(solution)/shard_map/pallas_call | solution.py:491
  64.0 0.0 collective-permute-done.12
  64.1 1.3 %collective-permute-start.28 = (f32[264,128]{1,0:T(8,128)S(1)}, f32[264,128]{1,0:T(8,128)S(1)}, u32[]{:S(2)}, u32[]{:S(2)}) collective-permute-start(f32[264,128]{1,0:T(8,128)S(1)} %get-tuple-element.73), channel_id=1, source_target_pairs={{0,3},{1,2},{2,1},{3,0},{4,7},{5,6},{6,5},{7,4},{8,11},{9,10},{10,... | collective-permute-start | bytes 405512 | tf_op jit(solution)/shard_map/ppermute | solution.py:349
  65.4 0.4 collective-permute-start.18
  65.8 0.5 collective-permute-start.19
  66.3 1.0 %collective-permute-start.20 = (f32[264,128]{1,0:T(8,128)S(1)}, f32[264,128]{1,0:T(8,128)S(1)}, u32[]{:S(2)}, u32[]{:S(2)}) collective-permute-start(f32[264,128]{1,0:T(8,128)S(1)} %get-tuple-element.63), channel_id=1, source_target_pairs={{0,3},{1,2},{2,1},{3,0},{4,7},{5,6},{6,5},{7,4},{8,11},{9,10},{10,... | collective-permute-start | bytes 405512 | tf_op jit(solution)/shard_map/ppermute | solution.py:349
  67.3 1.5 %shard_map.92 = (f32[264,128]{1,0:T(8,128)S(1)}, f32[264,128]{1,0:T(8,128)S(1)}, f32[264,128]{1,0:T(8,128)S(1)}, f32[264,128]{1,0:T(8,128)S(1)}) custom-call(f32[256,128]{1,0:T(8,128)S(1)} %collective-permute-done.2.refs_0_, f32[256,128]{1,0:T(8,128)S(1)} %collective-permute-done.3.refs_1_, bf16[16,256,256]{2,1,0:T(8,128)(2,1)S(1)} %get-tuple-element.44.refs_2_, ...), custom_call_target="tpu_custom_call" | custom-call | flops 1610612736 | bytes 4194304 | tf_op jit(solution)/shard_map/pallas_call | solution.py:491
  68.8 0.7 collective-permute-start.5
  69.5 0.8 collective-permute-done.28.refs_3_
  70.3 1.2 %collective-permute-start.6 = (f32[264,128]{1,0:T(8,128)S(1)}, f32[264,128]{1,0:T(8,128)S(1)}, u32[]{:S(2)}, u32[]{:S(2)}) collective-permute-start(f32[264,128]{1,0:T(8,128)S(1)} %get-tuple-element.52), channel_id=1, source_target_pairs={{0,2},{1,3},{2,0},{3,1},{4,6},{5,7},{6,4},{7,5},{8,10},{9,11},{10,... | collective-permute-start | bytes 405512 | tf_op jit(solution)/shard_map/ppermute | solution.py:349
  71.5 1.0 %collective-permute-start.7 = (f32[264,128]{1,0:T(8,128)S(1)}, f32[264,128]{1,0:T(8,128)S(1)}, u32[]{:S(2)}, u32[]{:S(2)}) collective-permute-start(f32[264,128]{1,0:T(8,128)S(1)} %get-tuple-element.53), channel_id=1, source_target_pairs={{0,3},{1,2},{2,1},{3,0},{4,7},{5,6},{6,5},{7,4},{8,11},{9,10},{10,... | collective-permute-start | bytes 405512 | tf_op jit(solution)/shard_map/ppermute | solution.py:349
  72.6 1.2 %shard_map.104 = (f32[12,4,64,128]{3,2,1,0:T(8,128)}, f32[12,2,2,128]{3,2,1,0:T(2,128)}) custom-call(f32[264,128]{1,0:T(8,128)S(1)} %get-tuple-element.70.refs_0_, f32[264,128]{1,0:T(8,128)S(1)} %collective-permute-done.26.refs_1_, f32[264,128]{1,0:T(8,128)S(1)} %collective-permute-done.27.refs_2_, f32[264,128]{1,0:T(8,128)S(1)} %collective-permute-done.28.refs_3_, ...), custom_call_target="tpu_custom_call" | custom-call | flops 100663296 | bytes 1048576 | tf_op jit(solution)/shard_map/pallas_call | solution.py:502
  73.7 0.5 collective-permute-done.19.refs_2_
  74.3 1.8 %collective-permute-done.20.refs_3_ = f32[264,128]{1,0:T(8,128)S(1)} collective-permute-done((f32[264,128]{1,0:T(8,128)S(1)}, f32[264,128]{1,0:T(8,128)S(1)}, u32[]{:S(2)}, u32[]{:S(2)}) %collective-permute-start.20) | collective-permute-done | bytes 135200 | tf_op jit(solution)/shard_map/ppermute | solution.py:349
  76.1 1.1 %shard_map.105 = (f32[12,4,64,128]{3,2,1,0:T(8,128)}, f32[12,2,2,128]{3,2,1,0:T(2,128)}) custom-call(f32[264,128]{1,0:T(8,128)S(1)} %get-tuple-element.60.refs_0_, f32[264,128]{1,0:T(8,128)S(1)} %collective-permute-done.18.refs_1_, f32[264,128]{1,0:T(8,128)S(1)} %collective-permute-done.19.refs_2_, ...), custom_call_target="tpu_custom_call", output_to_operand_aliasing={{0}: (7, {}), {1}: (8, {})} | custom-call | flops 100663296 | bytes 1048576 | tf_op jit(solution)/shard_map/pallas_call | solution.py:502
  77.3 2.8 %collective-permute-done.6.refs_2_ = f32[264,128]{1,0:T(8,128)S(1)} collective-permute-done((f32[264,128]{1,0:T(8,128)S(1)}, f32[264,128]{1,0:T(8,128)S(1)}, u32[]{:S(2)}, u32[]{:S(2)}) %collective-permute-start.6) | collective-permute-done | bytes 135200 | tf_op jit(solution)/shard_map/ppermute | solution.py:349
  80.1 1.8 %collective-permute-done.7.refs_3_ = f32[264,128]{1,0:T(8,128)S(1)} collective-permute-done((f32[264,128]{1,0:T(8,128)S(1)}, f32[264,128]{1,0:T(8,128)S(1)}, u32[]{:S(2)}, u32[]{:S(2)}) %collective-permute-start.7) | collective-permute-done | bytes 135200 | tf_op jit(solution)/shard_map/ppermute | solution.py:349
  81.9 1.1 %shard_map.106 = (f32[12,4,64,128]{3,2,1,0:T(8,128)}, f32[12,2,2,128]{3,2,1,0:T(2,128)}) custom-call(f32[264,128]{1,0:T(8,128)S(1)} %get-tuple-element.50.refs_0_, f32[264,128]{1,0:T(8,128)S(1)} %collective-permute-done.5.refs_1_, f32[264,128]{1,0:T(8,128)S(1)} %collective-permute-done.6.refs_2_, ...), custom_call_target="tpu_custom_call", output_to_operand_aliasing={{0}: (7, {}), {1}: (8, {})} | custom-call | flops 100663296 | bytes 1048576 | tf_op jit(solution)/shard_map/pallas_call | solution.py:502
  (36 shorter events, 0.1 us)
Async XLA Ops:
  0.6 1.4 %copy-start = (f32[12,4,64,128]{3,2,1,0:T(8,128)S(1)}, f32[12,4,64,128]{3,2,1,0:T(8,128)}, u32[]{:S(2)}) copy-start(f32[12,4,64,128]{3,2,1,0:T(8,128)} %state_ref.13) | copy-start | bytes 4718596
  2.2 28.2 %collective-permute-start.21 = (f32[4,2,64,128]{3,2,1,0:T(8,128)S(1)}, f32[4,2,64,128]{3,2,1,0:T(8,128)S(1)}, u32[]{:S(2)}, u32[]{:S(2)}) collective-permute-start(f32[4,2,64,128]{3,2,1,0:T(8,128)S(1)} %get-tuple-element.64), channel_id=1, source_target_pairs={{0,4},{4,0},{8,12},{12,8},{16,20},{20,16},{24,28},{28,24},{1,5},{5... | collective-permute-start | bytes 786440 | tf_op jit(solution)/shard_map/ppermute | solution.py:436
  5.3 28.7 %copy-start.4 = (bf16[2,256,512]{2,1,0:T(8,128)(2,1)S(1)}, bf16[2,256,512]{2,1,0:T(8,128)(2,1)}, u32[]{:S(2)}) copy-start(bf16[2,256,512]{2,1,0:T(8,128)(2,1)} %constant.10.clone.high_ref) | copy-start | bytes 1572868
  5.5 10.4 %copy-start.1 = (f32[12,4,64,128]{3,2,1,0:T(8,128)S(1)}, f32[12,4,64,128]{3,2,1,0:T(8,128)}, u32[]{:S(2)}) copy-start(f32[12,4,64,128]{3,2,1,0:T(8,128)} %state_ref.13) | copy-start | bytes 4718596
  5.5 37.0 %collective-permute-start.13 = (f32[4,2,64,128]{3,2,1,0:T(8,128)S(1)}, f32[4,2,64,128]{3,2,1,0:T(8,128)S(1)}, u32[]{:S(2)}, u32[]{:S(2)}) collective-permute-start(f32[4,2,64,128]{3,2,1,0:T(8,128)S(1)} %get-tuple-element.54), channel_id=1, source_target_pairs={{0,4},{4,0},{8,12},{12,8},{16,20},{20,16},{24,28},{28,24},{1,5},{5... | collective-permute-start | bytes 786440 | tf_op jit(solution)/shard_map/ppermute | solution.py:436
  5.6 28.9 %collective-permute-start.22 = (f32[4,2,64,128]{3,2,1,0:T(8,128)S(1)}, f32[4,2,64,128]{3,2,1,0:T(8,128)S(1)}, u32[]{:S(2)}, u32[]{:S(2)}) collective-permute-start(f32[4,2,64,128]{3,2,1,0:T(8,128)S(1)} %get-tuple-element.65), channel_id=1, source_target_pairs={{0,28},{4,8},{8,4},{12,16},{16,12},{20,24},{24,20},{28,0},{1,29},{... | collective-permute-start | bytes 786440 | tf_op jit(solution)/shard_map/ppermute | solution.py:437
  10.6 23.4 %copy-start.3 = (bf16[2,256,512]{2,1,0:T(8,128)(2,1)S(1)}, bf16[2,256,512]{2,1,0:T(8,128)(2,1)}, u32[]{:S(2)}) copy-start(bf16[2,256,512]{2,1,0:T(8,128)(2,1)} %constant.11.clone.low_ref) | copy-start | bytes 1572868
  10.6 33.5 %collective-permute-start.14 = (f32[4,2,64,128]{3,2,1,0:T(8,128)S(1)}, f32[4,2,64,128]{3,2,1,0:T(8,128)S(1)}, u32[]{:S(2)}, u32[]{:S(2)}) collective-permute-start(f32[4,2,64,128]{3,2,1,0:T(8,128)S(1)} %get-tuple-element.55), channel_id=1, source_target_pairs={{0,28},{4,8},{8,4},{12,16},{16,12},{20,24},{24,20},{28,0},{1,29},{... | collective-permute-start | bytes 786440 | tf_op jit(solution)/shard_map/ppermute | solution.py:437
  10.7 28.1 %copy-start.2 = (f32[32,256,256]{2,1,0:T(8,128)S(1)}, f32[32,256,256]{2,1,0:T(8,128)}, u32[]{:S(2)}) copy-start(f32[32,256,256]{2,1,0:T(8,128)} %inverse_ref.3) | copy-start | bytes 25165828
  10.9 1.2 %collective-permute-start.8 = (f32[24,128]{1,0:T(8,128)S(1)}, f32[24,128]{1,0:T(8,128)S(1)}, u32[]{:S(2)}, u32[]{:S(2)}) collective-permute-start(f32[24,128]{1,0:T(8,128)S(1)} %shard_map.93), channel_id=1, source_target_pairs={{0,1},{1,0},{2,3},{3,2},{4,5},{5,4},{6,7},{7,6},{8,9},{9,8},{10,11... | collective-permute-start | bytes 36872 | tf_op jit(solution)/shard_map/ppermute | solution.py:367
  12.1 3.7 %collective-permute-start.9 = (f32[24,128]{1,0:T(8,128)S(1)}, f32[24,128]{1,0:T(8,128)S(1)}, u32[]{:S(2)}, u32[]{:S(2)}) collective-permute-start(f32[24,128]{1,0:T(8,128)S(1)} %add.15), channel_id=1, source_target_pairs={{0,2},{1,3},{2,0},{3,1},{4,6},{5,7},{6,4},{7,5},{8,10},{9,11},{10,... | collective-permute-start | bytes 36872 | tf_op jit(solution)/shard_map/ppermute | solution.py:367
  15.8 12.9 %collective-permute-start.10 = (f32[24,128]{1,0:T(8,128)S(1)}, f32[24,128]{1,0:T(8,128)S(1)}, u32[]{:S(2)}, u32[]{:S(2)}) collective-permute-start(f32[24,128]{1,0:T(8,128)S(1)} %add.16), channel_id=1, source_target_pairs={{0,4},{4,0},{8,12},{12,8},{16,20},{20,16},{24,28},{28,24},{1,5},{5... | collective-permute-start | bytes 36872 | tf_op jit(solution)/shard_map/ppermute | solution.py:367
  28.7 17.4 %collective-permute-start = (f32[4,2,64,128]{3,2,1,0:T(8,128)S(1)}, f32[4,2,64,128]{3,2,1,0:T(8,128)S(1)}, u32[]{:S(2)}, u32[]{:S(2)}) collective-permute-start(f32[4,2,64,128]{3,2,1,0:T(8,128)S(1)} %get-tuple-element.40), channel_id=1, source_target_pairs={{0,4},{4,0},{8,12},{12,8},{16,20},{20,16},{24,28},{28,24},{1,5},{5... | collective-permute-start | bytes 786440 | tf_op jit(solution)/shard_map/ppermute | solution.py:436
  30.4 15.8 %collective-permute-start.1 = (f32[4,2,64,128]{3,2,1,0:T(8,128)S(1)}, f32[4,2,64,128]{3,2,1,0:T(8,128)S(1)}, u32[]{:S(2)}, u32[]{:S(2)}) collective-permute-start(f32[4,2,64,128]{3,2,1,0:T(8,128)S(1)} %get-tuple-element.41), channel_id=1, source_target_pairs={{0,28},{4,8},{8,4},{12,16},{16,12},{20,24},{24,20},{28,0},{1,29},{... | collective-permute-start | bytes 786440 | tf_op jit(solution)/shard_map/ppermute | solution.py:437
  34.4 4.3 %collective-permute-start.11 = (f32[24,128]{1,0:T(8,128)S(1)}, f32[24,128]{1,0:T(8,128)S(1)}, u32[]{:S(2)}, u32[]{:S(2)}) collective-permute-start(f32[24,128]{1,0:T(8,128)S(1)} %add.17), channel_id=1, source_target_pairs={{0,8},{4,12},{8,0},{12,4},{16,24},{20,28},{24,16},{28,20},{1,9},{5... | collective-permute-start | bytes 36872 | tf_op jit(solution)/shard_map/ppermute | solution.py:367
  38.7 8.5 %collective-permute-start.25 = (f32[256,128]{1,0:T(8,128)S(1)}, f32[256,128]{1,0:T(8,128)S(1)}, u32[]{:S(2)}, u32[]{:S(2)}) collective-permute-start(f32[256,128]{1,0:T(8,128)S(1)} %get-tuple-element.69), channel_id=1, source_target_pairs={{0,1},{1,0},{2,3},{3,2},{4,5},{5,4},{6,7},{7,6},{8,9},{9,8},{10,11... | collective-permute-start | bytes 393224 | tf_op jit(solution)/shard_map/ppermute | solution.py:349
  42.5 21.5 %collective-permute-start.12 = (f32[24,128]{1,0:T(8,128)S(1)}, f32[24,128]{1,0:T(8,128)S(1)}, u32[]{:S(2)}, u32[]{:S(2)}) collective-permute-start(f32[24,128]{1,0:T(8,128)S(1)} %add.18), channel_id=1, source_target_pairs={{0,16},{4,20},{8,24},{12,28},{16,0},{20,4},{24,8},{28,12},{1,17},{... | collective-permute-start | bytes 36872 | tf_op jit(solution)/shard_map/ppermute | solution.py:367
  44.6 17.3 %collective-permute-start.15 = (f32[256,128]{1,0:T(8,128)S(1)}, f32[256,128]{1,0:T(8,128)S(1)}, u32[]{:S(2)}, u32[]{:S(2)}) collective-permute-start(f32[256,128]{1,0:T(8,128)S(1)} %get-tuple-element.56), channel_id=1, source_target_pairs={{0,2},{1,3},{2,0},{3,1},{4,6},{5,7},{6,4},{7,5},{8,10},{9,11},{10,... | collective-permute-start | bytes 393224 | tf_op jit(solution)/shard_map/ppermute | solution.py:349
  46.1 15.8 %collective-permute-start.16 = (f32[256,128]{1,0:T(8,128)S(1)}, f32[256,128]{1,0:T(8,128)S(1)}, u32[]{:S(2)}, u32[]{:S(2)}) collective-permute-start(f32[256,128]{1,0:T(8,128)S(1)} %get-tuple-element.57), channel_id=1, source_target_pairs={{0,3},{1,2},{2,1},{3,0},{4,7},{5,6},{6,5},{7,4},{8,11},{9,10},{10,... | collective-permute-start | bytes 393224 | tf_op jit(solution)/shard_map/ppermute | solution.py:349
  46.2 2.5 %collective-permute-start.17 = (f32[256,128]{1,0:T(8,128)S(1)}, f32[256,128]{1,0:T(8,128)S(1)}, u32[]{:S(2)}, u32[]{:S(2)}) collective-permute-start(f32[256,128]{1,0:T(8,128)S(1)} %get-tuple-element.59), channel_id=1, source_target_pairs={{0,1},{1,0},{2,3},{3,2},{4,5},{5,4},{6,7},{7,6},{8,9},{9,8},{10,11... | collective-permute-start | bytes 393224 | tf_op jit(solution)/shard_map/ppermute | solution.py:349
  47.3 4.3 %collective-permute-start.4 = (f32[256,128]{1,0:T(8,128)S(1)}, f32[256,128]{1,0:T(8,128)S(1)}, u32[]{:S(2)}, u32[]{:S(2)}) collective-permute-start(f32[256,128]{1,0:T(8,128)S(1)} %get-tuple-element.49), channel_id=1, source_target_pairs={{0,1},{1,0},{2,3},{3,2},{4,5},{5,4},{6,7},{7,6},{8,9},{9,8},{10,11... | collective-permute-start | bytes 393224 | tf_op jit(solution)/shard_map/ppermute | solution.py:349
  48.7 7.9 %collective-permute-start.23 = (f32[256,128]{1,0:T(8,128)S(1)}, f32[256,128]{1,0:T(8,128)S(1)}, u32[]{:S(2)}, u32[]{:S(2)}) collective-permute-start(f32[256,128]{1,0:T(8,128)S(1)} %get-tuple-element.66), channel_id=1, source_target_pairs={{0,2},{1,3},{2,0},{3,1},{4,6},{5,7},{6,4},{7,5},{8,10},{9,11},{10,... | collective-permute-start | bytes 393224 | tf_op jit(solution)/shard_map/ppermute | solution.py:349
  51.6 6.9 %collective-permute-start.24 = (f32[256,128]{1,0:T(8,128)S(1)}, f32[256,128]{1,0:T(8,128)S(1)}, u32[]{:S(2)}, u32[]{:S(2)}) collective-permute-start(f32[256,128]{1,0:T(8,128)S(1)} %get-tuple-element.67), channel_id=1, source_target_pairs={{0,3},{1,2},{2,1},{3,0},{4,7},{5,6},{6,5},{7,4},{8,11},{9,10},{10,... | collective-permute-start | bytes 393224 | tf_op jit(solution)/shard_map/ppermute | solution.py:349
  51.9 8.4 %copy-start.7 = (f32[8,256]{1,0:T(8,128)S(1)}, f32[8,256]{1,0:T(8,128)}, u32[]{:S(2)}) copy-start(f32[8,256]{1,0:T(8,128)} %constant.14.clone.refs_7_) | copy-start | bytes 24580
  56.6 8.8 %collective-permute-start.2 = (f32[256,128]{1,0:T(8,128)S(1)}, f32[256,128]{1,0:T(8,128)S(1)}, u32[]{:S(2)}, u32[]{:S(2)}) collective-permute-start(f32[256,128]{1,0:T(8,128)S(1)} %get-tuple-element.42), channel_id=1, source_target_pairs={{0,2},{1,3},{2,0},{3,1},{4,6},{5,7},{6,4},{7,5},{8,10},{9,11},{10,... | collective-permute-start | bytes 393224 | tf_op jit(solution)/shard_map/ppermute | solution.py:349
  58.5 7.3 %collective-permute-start.3 = (f32[256,128]{1,0:T(8,128)S(1)}, f32[256,128]{1,0:T(8,128)S(1)}, u32[]{:S(2)}, u32[]{:S(2)}) collective-permute-start(f32[256,128]{1,0:T(8,128)S(1)} %get-tuple-element.43), channel_id=1, source_target_pairs={{0,3},{1,2},{2,1},{3,0},{4,7},{5,6},{6,5},{7,4},{8,11},{9,10},{10,... | collective-permute-start | bytes 393224 | tf_op jit(solution)/shard_map/ppermute | solution.py:349
  61.9 4.4 %collective-permute-start.26 = (f32[264,128]{1,0:T(8,128)S(1)}, f32[264,128]{1,0:T(8,128)S(1)}, u32[]{:S(2)}, u32[]{:S(2)}) collective-permute-start(f32[264,128]{1,0:T(8,128)S(1)} %get-tuple-element.71), channel_id=1, source_target_pairs={{0,1},{1,0},{2,3},{3,2},{4,5},{5,4},{6,7},{7,6},{8,9},{9,8},{10,11... | collective-permute-start | bytes 405512 | tf_op jit(solution)/shard_map/ppermute | solution.py:349
  62.0 6.8 %collective-permute-start.27 = (f32[264,128]{1,0:T(8,128)S(1)}, f32[264,128]{1,0:T(8,128)S(1)}, u32[]{:S(2)}, u32[]{:S(2)}) collective-permute-start(f32[264,128]{1,0:T(8,128)S(1)} %get-tuple-element.72), channel_id=1, source_target_pairs={{0,2},{1,3},{2,0},{3,1},{4,6},{5,7},{6,4},{7,5},{8,10},{9,11},{10,... | collective-permute-start | bytes 405512 | tf_op jit(solution)/shard_map/ppermute | solution.py:349
  64.1 6.2 %collective-permute-start.28 = (f32[264,128]{1,0:T(8,128)S(1)}, f32[264,128]{1,0:T(8,128)S(1)}, u32[]{:S(2)}, u32[]{:S(2)}) collective-permute-start(f32[264,128]{1,0:T(8,128)S(1)} %get-tuple-element.73), channel_id=1, source_target_pairs={{0,3},{1,2},{2,1},{3,0},{4,7},{5,6},{6,5},{7,4},{8,11},{9,10},{10,... | collective-permute-start | bytes 405512 | tf_op jit(solution)/shard_map/ppermute | solution.py:349
  65.4 6.1 %collective-permute-start.18 = (f32[264,128]{1,0:T(8,128)S(1)}, f32[264,128]{1,0:T(8,128)S(1)}, u32[]{:S(2)}, u32[]{:S(2)}) collective-permute-start(f32[264,128]{1,0:T(8,128)S(1)} %get-tuple-element.61), channel_id=1, source_target_pairs={{0,1},{1,0},{2,3},{3,2},{4,5},{5,4},{6,7},{7,6},{8,9},{9,8},{10,11... | collective-permute-start | bytes 405512 | tf_op jit(solution)/shard_map/ppermute | solution.py:349
  65.8 8.5 %collective-permute-start.19 = (f32[264,128]{1,0:T(8,128)S(1)}, f32[264,128]{1,0:T(8,128)S(1)}, u32[]{:S(2)}, u32[]{:S(2)}) collective-permute-start(f32[264,128]{1,0:T(8,128)S(1)} %get-tuple-element.62), channel_id=1, source_target_pairs={{0,2},{1,3},{2,0},{3,1},{4,6},{5,7},{6,4},{7,5},{8,10},{9,11},{10,... | collective-permute-start | bytes 405512 | tf_op jit(solution)/shard_map/ppermute | solution.py:349
  66.3 6.3 %copy-start.5 = (bf16[128,128]{1,0:T(8,128)(2,1)S(1)}, bf16[128,128]{1,0:T(8,128)(2,1)}, u32[]{:S(2)}) copy-start(bf16[128,128]{1,0:T(8,128)(2,1)} %constant.13.clone.refs_5_) | copy-start | bytes 98308
  66.3 6.3 %copy-start.6 = (bf16[128,128]{1,0:T(8,128)(2,1)S(1)}, bf16[128,128]{1,0:T(8,128)(2,1)}, u32[]{:S(2)}) copy-start(bf16[128,128]{1,0:T(8,128)(2,1)} %constant.12.clone.refs_4_) | copy-start | bytes 98308
  66.3 9.8 %collective-permute-start.20 = (f32[264,128]{1,0:T(8,128)S(1)}, f32[264,128]{1,0:T(8,128)S(1)}, u32[]{:S(2)}, u32[]{:S(2)}) collective-permute-start(f32[264,128]{1,0:T(8,128)S(1)} %get-tuple-element.63), channel_id=1, source_target_pairs={{0,3},{1,2},{2,1},{3,0},{4,7},{5,6},{6,5},{7,4},{8,11},{9,10},{10,... | collective-permute-start | bytes 405512 | tf_op jit(solution)/shard_map/ppermute | solution.py:349
  68.8 8.5 %collective-permute-start.5 = (f32[264,128]{1,0:T(8,128)S(1)}, f32[264,128]{1,0:T(8,128)S(1)}, u32[]{:S(2)}, u32[]{:S(2)}) collective-permute-start(f32[264,128]{1,0:T(8,128)S(1)} %get-tuple-element.51), channel_id=1, source_target_pairs={{0,1},{1,0},{2,3},{3,2},{4,5},{5,4},{6,7},{7,6},{8,9},{9,8},{10,11... | collective-permute-start | bytes 405512 | tf_op jit(solution)/shard_map/ppermute | solution.py:349
  70.3 9.8 %collective-permute-start.6 = (f32[264,128]{1,0:T(8,128)S(1)}, f32[264,128]{1,0:T(8,128)S(1)}, u32[]{:S(2)}, u32[]{:S(2)}) collective-permute-start(f32[264,128]{1,0:T(8,128)S(1)} %get-tuple-element.52), channel_id=1, source_target_pairs={{0,2},{1,3},{2,0},{3,1},{4,6},{5,7},{6,4},{7,5},{8,10},{9,11},{10,... | collective-permute-start | bytes 405512 | tf_op jit(solution)/shard_map/ppermute | solution.py:349
  71.5 10.4 %collective-permute-start.7 = (f32[264,128]{1,0:T(8,128)S(1)}, f32[264,128]{1,0:T(8,128)S(1)}, u32[]{:S(2)}, u32[]{:S(2)}) collective-permute-start(f32[264,128]{1,0:T(8,128)S(1)} %get-tuple-element.53), channel_id=1, source_target_pairs={{0,3},{1,2},{2,1},{3,0},{4,7},{5,6},{6,5},{7,4},{8,11},{9,10},{10,... | collective-permute-start | bytes 405512 | tf_op jit(solution)/shard_map/ppermute | solution.py:349
